TPU v7x, 8 devices: a whole 2x2x1 slice. The times are simulated.
8 devices in a mesh: data: 4 (over z, y, x), stage: 2 (over core).
Axes of the slice: x: 2, y: 2, z: 1, core: 2. Of those that a mesh axis runs over, the one named last changes fastest.
Arguments:
- master_up: float32 [2, 576, 1536], P('stage', 'data')
- master_down: float32 [2, 1536, 576], P('stage', 'data')
- moment1_up: float32 [2, 576, 1536], P('stage', 'data')
- moment2_up: float32 [2, 576, 1536], P('stage', 'data')
- moment1_down: float32 [2, 1536, 576], P('stage', 'data')
- moment2_down: float32 [2, 1536, 576], P('stage', 'data')
- compute_up: bfloat16 [2, 576, 1536], P('stage')
- compute_down: bfloat16 [2, 1536, 576], P('stage')
- accum_up: float32 [4, 2, 576, 1536], P('data', 'stage')
- accum_down: float32 [4, 2, 1536, 576], P('data', 'stage')
- stage_acts: bfloat16 [2, 8192, 576], P('stage', 'data')
- loss_grad: bfloat16 [8192, 576], P('data')
- next_micro: bfloat16 [16, 8192, 576], P(None, 'data')
- learn_rate: float32 [], replicated
- max_norm: float32 [], replicated
Outputs:
- output 1: float32 [2, 576, 1536], P('stage', 'data')
- output 2: float32 [2, 1536, 576], P('stage', 'data')
- output 3: float32 [2, 576, 1536], P('stage', 'data')
- output 4: float32 [2, 576, 1536], P('stage', 'data')
- output 5: float32 [2, 1536, 576], P('stage', 'data')
- output 6: float32 [2, 1536, 576], P('stage', 'data')
- output 7: bfloat16 [16, 8192, 576], P(None, 'data')
All inputs are finite; a program needn't handle non-finite values.
Results may differ from a plain program's by a relative error of at most 0.00552048.
Values are sent between devices in bfloat16 or wider.
A program may use at most 1 GiB of HBM per device.

v0:
```python
import jax
import jax.numpy as jnp
from jax import lax
from jax.sharding import PartitionSpec as P

BETA_ONE = 0.9
BETA_TWO = 0.95
ADAM_EPS = 1e-8
WEIGHT_DECAY = 0.1
NORM_EPS = 1e-6
STEP_NUM = 10
BIAS_ONE = 1.0 - BETA_ONE ** STEP_NUM
BIAS_TWO = 1.0 - BETA_TWO ** STEP_NUM
DOT_ROWS = (((0,), (0,)), ((), ()))
DOT_COLS = (((1,), (1,)), ((), ()))


def gelu_tanh(pre_act):
    return jax.nn.gelu(pre_act, approximate=True)


def stage_forward(stage_in, w_up, w_down):
    pre_act = jnp.dot(stage_in, w_up, preferred_element_type=jnp.float32)
    hidden = gelu_tanh(pre_act).astype(jnp.bfloat16)
    branch = jnp.dot(hidden, w_down, preferred_element_type=jnp.float32)
    return (stage_in.astype(jnp.float32) + branch).astype(jnp.bfloat16)


def stage_backward(stage_in, grad_in, w_up, w_down):
    pre_act = jnp.dot(stage_in, w_up, preferred_element_type=jnp.float32)
    hidden, gelu_pull = jax.vjp(gelu_tanh, pre_act)
    hidden = hidden.astype(jnp.bfloat16)
    dw_down = lax.dot_general(hidden, grad_in, DOT_ROWS, preferred_element_type=jnp.float32)
    d_hidden = lax.dot_general(grad_in, w_down, DOT_COLS, preferred_element_type=jnp.float32)
    d_pre = gelu_pull(d_hidden)[0].astype(jnp.bfloat16)
    dw_up = lax.dot_general(stage_in, d_pre, DOT_ROWS, preferred_element_type=jnp.float32)
    d_in = grad_in.astype(jnp.float32) + lax.dot_general(d_pre, w_up, DOT_COLS, preferred_element_type=jnp.float32)
    return dw_up, dw_down, d_in.astype(jnp.bfloat16)


def adamw_update(master, moment_one, moment_two, grad_step, learn_rate):
    mom_one = BETA_ONE * moment_one + (1.0 - BETA_ONE) * grad_step
    mom_two = BETA_TWO * moment_two + (1.0 - BETA_TWO) * grad_step * grad_step
    step_dir = (mom_one / BIAS_ONE) / (jnp.sqrt(mom_two / BIAS_TWO) + ADAM_EPS)
    new_master = master - learn_rate * (step_dir + WEIGHT_DECAY * master)
    return new_master, mom_one, mom_two


def solution(mesh):
    n_stage = mesh.shape['stage']
    n_data = mesh.shape['data']
    last_stage = n_stage - 1
    back_perm = [(source, source - 1) for source in range(1, n_stage)]
    fwd_perm = [(source, source + 1) for source in range(last_stage)]

    def backward_stages(my_stage, stage_in, grad_last, w_up, w_down, acc_up, acc_down):
        def run_stage(operands):
            grad_in, sum_up, sum_down = operands
            dw_up, dw_down, d_in = stage_backward(stage_in, grad_in, w_up, w_down)
            return sum_up + dw_up, sum_down + dw_down, d_in

        def pass_through(operands):
            return operands[1], operands[2], operands[0]

        grad_buf = grad_last
        for step in range(n_stage):
            acc_up, acc_down, d_in = lax.cond(my_stage == last_stage - step, run_stage, pass_through,
                                              (grad_buf, acc_up, acc_down))
            if step < last_stage:
                grad_buf = lax.ppermute(d_in, 'stage', back_perm)
        return acc_up, acc_down

    def forward_stages(my_stage, micro_in, w_up, w_down):
        def run_block(block):
            return stage_forward(block, w_up, w_down)

        def keep_block(block):
            return block

        n_micro = micro_in.shape[0]
        n_steps = n_micro + last_stage
        received = jnp.zeros_like(micro_in[0])
        results = []
        for step in range(n_steps):
            stage_in = jnp.where(my_stage == 0, micro_in[min(step, n_micro - 1)], received)
            active = (my_stage <= step) & (my_stage > step - n_micro)
            stage_out = lax.cond(active, run_block, keep_block, stage_in)
            if step >= last_stage:
                results.append(stage_out)
            if step < n_steps - 1:
                received = lax.ppermute(stage_out, 'stage', fwd_perm)
        stacked = jnp.stack(results)
        own_part = jnp.where(my_stage == last_stage, stacked, jnp.zeros_like(stacked))
        return lax.psum(own_part, 'stage')

    def step_body(master_up, master_down, moment1_up, moment2_up, moment1_down, moment2_down,
                  compute_up, compute_down, accum_up, accum_down, stage_acts, loss_grad, next_micro,
                  learn_rate, max_norm):
        my_stage = lax.axis_index('stage')
        sum_up, sum_down = backward_stages(my_stage, stage_acts[0], loss_grad, compute_up[0], compute_down[0],
                                           accum_up[0, 0], accum_down[0, 0])
        shard_up = lax.psum_scatter(sum_up, 'data', scatter_dimension=0, tiled=True) / n_data
        shard_down = lax.psum_scatter(sum_down, 'data', scatter_dimension=0, tiled=True) / n_data
        local_sq = jnp.sum(shard_up * shard_up) + jnp.sum(shard_down * shard_down)
        total_sq = lax.psum(local_sq, ('stage', 'data'))
        clip = jnp.minimum(1.0, max_norm / (jnp.sqrt(total_sq) + NORM_EPS))
        new_up, mom1_up, mom2_up = adamw_update(master_up[0], moment1_up[0], moment2_up[0], clip * shard_up, learn_rate)
        new_down, mom1_down, mom2_down = adamw_update(master_down[0], moment1_down[0], moment2_down[0], clip * shard_down, learn_rate)
        full_up = lax.all_gather(new_up.astype(jnp.bfloat16), 'data', axis=0, tiled=True)
        full_down = lax.all_gather(new_down.astype(jnp.bfloat16), 'data', axis=0, tiled=True)
        last_acts = forward_stages(my_stage, next_micro, full_up, full_down)
        return (new_up[None], new_down[None], mom1_up[None], mom2_up[None],
                mom1_down[None], mom2_down[None], last_acts)

    shard_spec = P('stage', 'data', None)
    whole_spec = P('stage', None, None)
    accum_spec = P('data', 'stage', None, None)
    micro_spec = P(None, 'data', None)
    in_specs = (shard_spec,) * 6 + (whole_spec, whole_spec, accum_spec, accum_spec,
                                    P('stage', 'data', None), P('data', None), micro_spec, P(), P())
    out_specs = (shard_spec,) * 6 + (micro_spec,)
    return jax.shard_map(step_body, mesh=mesh, in_specs=in_specs, out_specs=out_specs, check_vma=False)
```

profile of v0, /device:TPU:0, one launch (start us, length us, event | category | flops | bytes accessed | tf_op | source)
XLA Modules:
  0.0 926.2 jit_solution(1484398743007936727)
XLA Ops:
  7.2 4.0 copy.209
  14.3 4.0 copy.42
  18.3 4.3 copy.43
  23.9 48.4 %collective-permute-done = bf16[2048,576]{0,1:T(8,128)(2,1)} collective-permute-done((bf16[2048,576]{0,1:T(8,128)(2,1)}, bf16[2048,576]{0,1:T(8,128)(2,1)}, u32[]{:S(2)}, u32[]{:S(2)}) %collective-permute-start) | collective-permute-done | bytes 2359328 | tf_op jit(solution)/shard_map/ppermute | solution.py:70
  72.3 45.1 %conditional.20 = ((f32[576,1536]{1,0:T(8,128)}, f32[1536,576]{0,1:T(8,128)S(1)})) conditional(s32[]{:T(128)} %convert_element_type.234, (f32[576,1536]{1,0:T(8,128)}, f32[1536,576]{0,1:T(8,128)S(1)}) %tuple.188, (bf16[2048,576]{0,1:T(8,128)(2,1)}, bf16[1536,576]{1,0:T(8,128)(2,1)}, bf16[2048,576]{1,0:T(8,128)(2,1)}, bf16[576,1536]{1,0:T(8,128)(2,1)}, ...), branch_computations={%region_2.0_spmd, %region_3.0_spmd} | conditional | flops 14588510208 | bytes 64880664 | solution.py:67
  72.5 9.8 %fusion.257 = f32[2048,1536]{1,0:T(8,128)} fusion(bf16[2048,576]{1,0:T(8,128)(2,1)} %get-tuple-element.215, bf16[576,1536]{1,0:T(8,128)(2,1)} %get-tuple-element.216), kind=kOutput, calls=%fused_computation.344 | convolution fusion | flops 3623878656 | bytes 16711680 | tf_op jit(solution)/shard_map/cond/branch_1_fun/dot_general | solution.py:30
  82.3 26.1 %bitcast_add_fusion.1 = f32[576,1536]{1,0:T(8,128)} fusion(f32[576,1536]{1,0:T(8,128)} %get-tuple-element.212, bf16[2048,576]{1,0:T(8,128)(2,1)} %get-tuple-element.215, f32[2048,1536]{1,0:T(8,128)} %fusion.257, bf16[2048,576]{0,1:T(8,128)(2,1)} %get-tuple-element.397, bf16[1536,576]{1,0:T(8,128)(2,1)} %get-tuple-element.214), kind=kOutput, calls=%fused_computation.36 | convolution fusion | flops 7311556608 | bytes 26148864 | tf_op jit(solution)/shard_map/cond/branch_1_fun/dot_general | solution.py:36
  108.4 8.6 fusion.28
  120.1 40.7 %reduce-scatter.3.cloned.1.call-done = f32[144,1536]{1,0:T(8,128)} async-done(((f32[576,1536]{1,0:T(8,128)}), f32[144,1536]{1,0:T(8,128)}) %reduce-scatter.3.cloned.1.call-update) | async-done | bytes 884752 | tf_op jit(solution)/shard_map/reduce_scatter | solution.py:102
  162.8 43.0 %reduce-scatter.5.cloned.1.call-done = f32[384,576]{0,1:T(8,128)} async-done(((f32[1536,576]{0,1:T(8,128)}), f32[384,576]{0,1:T(8,128)}) %reduce-scatter.5.cloned.1.call-update) | async-done | bytes 884752 | tf_op jit(solution)/shard_map/reduce_scatter | solution.py:103
  209.8 22.2 %psum.14 = f32[]{:T(128)} all-reduce(f32[]{:T(128)S(6)} %add.226), channel_id=1, replica_groups=mesh['data'=4,'stage'=2] {'stage','data'}, use_global_device_ids=true, to_apply=%region_8.0 | all-reduce | flops 1 | bytes 8 | tf_op jit(solution)/shard_map/psum | solution.py:105
  232.8 4.3 fusion.255
  241.5 24.3 %all-gather.3.cloned.1.call-done = bf16[576,1536]{1,0:T(8,128)(2,1)} async-done(((bf16[144,1536]{1,0:T(8,128)(2,1)}), bf16[576,1536]{1,0:T(8,128)(2,1)}) %all-gather.3.cloned.1.call-update) | async-done | bytes 1769488 | tf_op jit(solution)/shard_map/all_gather | solution.py:109
  265.8 28.1 %all-gather.5.cloned.1.call-done = bf16[1536,576]{0,1:T(8,128)(2,1)} async-done(((bf16[384,576]{0,1:T(8,128)(2,1)}), bf16[1536,576]{0,1:T(8,128)(2,1)}) %all-gather.5.cloned.1.call-update) | async-done | bytes 1769488 | tf_op jit(solution)/shard_map/all_gather | solution.py:110
  293.9 14.0 %conditional.21 = (bf16[2048,576]{0,1:T(8,128)(2,1)S(1)}) conditional(s32[]{:T(128)} %convert_element_type.237, bf16[2048,576]{0,1:T(8,128)(2,1)S(1)} %select_bitcast_fusion, (bf16[2048,576]{0,1:T(8,128)(2,1)S(1)}, bf16[576,1536]{1,0:T(8,128)(2,1)}, bf16[1536,576]{0,1:T(8,128)(2,1)}) %tuple.190), branch_computations={%region_9.10_spmd, %region_10.11_spmd} | conditional | flops 7279607808 | bytes 12976136 | solution.py:87
  295.4 12.5 %add_convert_fusion.1 = bf16[2048,576]{0,1:T(8,128)(2,1)S(1)} fusion(bf16[2048,576]{0,1:T(8,128)(2,1)} %copy.193, bf16[1536,576]{0,1:T(8,128)(2,1)} %get-tuple-element.405, bf16[576,1536]{1,0:T(8,128)(2,1)} %get-tuple-element.219), kind=kOutput, calls=%fused_computation.57 | convolution fusion | flops 7279607808 | bytes 8257536 | tf_op jit(solution)/shard_map/cond/branch_1_fun/dot_general | solution.py:25
  316.7 16.6 %conditional.22 = (bf16[2048,576]{0,1:T(8,128)(2,1)}, bf16[1,2048,576]{1,2,0:T(8,128)(2,1)S(1)}) conditional(s32[]{:T(128)} %convert_element_type.236, bf16[2048,576]{0,1:T(8,128)(2,1)} %bitcast_select_fusion.15, (bf16[2048,576]{0,1:T(8,128)(2,1)}, bf16[576,1536]{1,0:T(8,128)(2,1)}, bf16[1536,576]{0,1:T(8,128)(2,1)}) %tuple.191), branch_computations={%region_11.12_spmd, %region_12.13_spmd} | conditional | flops 7279607808 | bytes 17694736 | solution.py:87
  318.3 13.3 %add_convert_fusion.2 = bf16[2048,576]{0,1:T(8,128)(2,1)} fusion(bf16[2048,576]{0,1:T(8,128)(2,1)S(1)} %copy.194, bf16[1536,576]{0,1:T(8,128)(2,1)} %get-tuple-element.408, bf16[576,1536]{1,0:T(8,128)(2,1)} %get-tuple-element.222), kind=kOutput, calls=%fused_computation.71 | convolution fusion | flops 7279607808 | bytes 8257536 | tf_op jit(solution)/shard_map/cond/branch_1_fun/dot_general | solution.py:25
  333.3 4.5 collective-permute-start.2
  343.7 18.3 %conditional.23 = (bf16[2048,576]{0,1:T(8,128)(2,1)}, bf16[1,2048,576]{1,2,0:T(8,128)(2,1)}) conditional(s32[]{:T(128)} %convert_element_type.240, bf16[2048,576]{0,1:T(8,128)(2,1)} %bitcast_select_fusion.14, (bf16[2048,576]{0,1:T(8,128)(2,1)}, bf16[576,1536]{1,0:T(8,128)(2,1)}, bf16[1536,576]{0,1:T(8,128)(2,1)}) %tuple.192), branch_computations={%region_13.14_spmd, %region_14.15_spmd} | conditional | flops 7279607808 | bytes 17694736 | solution.py:87
  345.4 13.3 %add_convert_fusion.3 = bf16[2048,576]{0,1:T(8,128)(2,1)} fusion(bf16[2048,576]{0,1:T(8,128)(2,1)S(1)} %copy.195, bf16[1536,576]{0,1:T(8,128)(2,1)} %get-tuple-element.411, bf16[576,1536]{1,0:T(8,128)(2,1)} %get-tuple-element.225), kind=kOutput, calls=%fused_computation.85 | convolution fusion | flops 7279607808 | bytes 8257536 | tf_op jit(solution)/shard_map/cond/branch_1_fun/dot_general | solution.py:25
  365.5 3.6 collective-permute-done.3
  372.4 16.6 %conditional.24 = (bf16[2048,576]{0,1:T(8,128)(2,1)}, bf16[1,2048,576]{1,2,0:T(8,128)(2,1)S(1)}) conditional(s32[]{:T(128)} %convert_element_type.241, bf16[2048,576]{0,1:T(8,128)(2,1)} %bitcast_select_fusion.13, (bf16[2048,576]{0,1:T(8,128)(2,1)}, bf16[576,1536]{1,0:T(8,128)(2,1)}, bf16[1536,576]{0,1:T(8,128)(2,1)}) %tuple.193), branch_computations={%region_15.16_spmd, %region_16.17_spmd} | conditional | flops 7279607808 | bytes 17694736 | solution.py:87
  374.1 13.3 %add_convert_fusion.4 = bf16[2048,576]{0,1:T(8,128)(2,1)} fusion(bf16[2048,576]{0,1:T(8,128)(2,1)S(1)} %copy.196, bf16[1536,576]{0,1:T(8,128)(2,1)} %get-tuple-element.414, bf16[576,1536]{1,0:T(8,128)(2,1)} %get-tuple-element.228), kind=kOutput, calls=%fused_computation.99 | convolution fusion | flops 7279607808 | bytes 8257536 | tf_op jit(solution)/shard_map/cond/branch_1_fun/dot_general | solution.py:25
  389.1 3.8 collective-permute-start.4
  398.8 18.4 %conditional.25 = (bf16[2048,576]{0,1:T(8,128)(2,1)}, bf16[1,2048,576]{1,2,0:T(8,128)(2,1)}) conditional(s32[]{:T(128)} %convert_element_type.242, bf16[2048,576]{0,1:T(8,128)(2,1)} %bitcast_select_fusion.12, (bf16[2048,576]{0,1:T(8,128)(2,1)}, bf16[576,1536]{1,0:T(8,128)(2,1)}, bf16[1536,576]{0,1:T(8,128)(2,1)}) %tuple.194), branch_computations={%region_17.18_spmd, %region_18.19_spmd} | conditional | flops 7279607808 | bytes 17694736 | solution.py:87
  400.5 13.3 %add_convert_fusion.5 = bf16[2048,576]{0,1:T(8,128)(2,1)} fusion(bf16[2048,576]{0,1:T(8,128)(2,1)S(1)} %copy.197, bf16[1536,576]{0,1:T(8,128)(2,1)} %get-tuple-element.417, bf16[576,1536]{1,0:T(8,128)(2,1)} %get-tuple-element.231), kind=kOutput, calls=%fused_computation.113 | convolution fusion | flops 7279607808 | bytes 8257536 | tf_op jit(solution)/shard_map/cond/branch_1_fun/dot_general | solution.py:25
  420.5 3.8 collective-permute-done.5
  427.6 16.6 %conditional.26 = (bf16[2048,576]{0,1:T(8,128)(2,1)}, bf16[1,2048,576]{1,2,0:T(8,128)(2,1)S(1)}) conditional(s32[]{:T(128)} %convert_element_type.243, bf16[2048,576]{0,1:T(8,128)(2,1)} %bitcast_select_fusion.11, (bf16[2048,576]{0,1:T(8,128)(2,1)}, bf16[576,1536]{1,0:T(8,128)(2,1)}, bf16[1536,576]{0,1:T(8,128)(2,1)}) %tuple.195), branch_computations={%region_19.20_spmd, %region_20.21_spmd} | conditional | flops 7279607808 | bytes 17694736 | solution.py:87
  429.3 13.3 %add_convert_fusion.6 = bf16[2048,576]{0,1:T(8,128)(2,1)} fusion(bf16[2048,576]{0,1:T(8,128)(2,1)S(1)} %copy.198, bf16[1536,576]{0,1:T(8,128)(2,1)} %get-tuple-element.420, bf16[576,1536]{1,0:T(8,128)(2,1)} %get-tuple-element.234), kind=kOutput, calls=%fused_computation.127 | convolution fusion | flops 7279607808 | bytes 8257536 | tf_op jit(solution)/shard_map/cond/branch_1_fun/dot_general | solution.py:25
  444.2 4.1 collective-permute-start.6
  454.0 18.3 %conditional.27 = (bf16[2048,576]{0,1:T(8,128)(2,1)}, bf16[1,2048,576]{1,2,0:T(8,128)(2,1)}) conditional(s32[]{:T(128)} %convert_element_type.244, bf16[2048,576]{0,1:T(8,128)(2,1)} %bitcast_select_fusion.10, (bf16[2048,576]{0,1:T(8,128)(2,1)}, bf16[576,1536]{1,0:T(8,128)(2,1)}, bf16[1536,576]{0,1:T(8,128)(2,1)}) %tuple.196), branch_computations={%region_21.22_spmd, %region_22.23_spmd} | conditional | flops 7279607808 | bytes 17694736 | solution.py:87
  455.6 13.3 %add_convert_fusion.7 = bf16[2048,576]{0,1:T(8,128)(2,1)} fusion(bf16[2048,576]{0,1:T(8,128)(2,1)S(1)} %copy.199, bf16[1536,576]{0,1:T(8,128)(2,1)} %get-tuple-element.423, bf16[576,1536]{1,0:T(8,128)(2,1)} %get-tuple-element.237), kind=kOutput, calls=%fused_computation.141 | convolution fusion | flops 7279607808 | bytes 8257536 | tf_op jit(solution)/shard_map/cond/branch_1_fun/dot_general | solution.py:25
  475.6 3.8 collective-permute-done.7
  482.7 16.6 %conditional.28 = (bf16[2048,576]{0,1:T(8,128)(2,1)}, bf16[1,2048,576]{1,2,0:T(8,128)(2,1)S(1)}) conditional(s32[]{:T(128)} %convert_element_type.245, bf16[2048,576]{0,1:T(8,128)(2,1)} %bitcast_select_fusion.9, (bf16[2048,576]{0,1:T(8,128)(2,1)}, bf16[576,1536]{1,0:T(8,128)(2,1)}, bf16[1536,576]{0,1:T(8,128)(2,1)}) %tuple.197), branch_computations={%region_23.24_spmd, %region_24.25_spmd} | conditional | flops 7279607808 | bytes 17694736 | solution.py:87
  484.4 13.3 %add_convert_fusion.8 = bf16[2048,576]{0,1:T(8,128)(2,1)} fusion(bf16[2048,576]{0,1:T(8,128)(2,1)S(1)} %copy.200, bf16[1536,576]{0,1:T(8,128)(2,1)} %get-tuple-element.426, bf16[576,1536]{1,0:T(8,128)(2,1)} %get-tuple-element.240), kind=kOutput, calls=%fused_computation.155 | convolution fusion | flops 7279607808 | bytes 8257536 | tf_op jit(solution)/shard_map/cond/branch_1_fun/dot_general | solution.py:25
  499.4 3.9 collective-permute-start.8
  509.1 18.3 %conditional.29 = (bf16[2048,576]{0,1:T(8,128)(2,1)}, bf16[1,2048,576]{1,2,0:T(8,128)(2,1)}) conditional(s32[]{:T(128)} %convert_element_type.246, bf16[2048,576]{0,1:T(8,128)(2,1)} %bitcast_select_fusion.8, (bf16[2048,576]{0,1:T(8,128)(2,1)}, bf16[576,1536]{1,0:T(8,128)(2,1)}, bf16[1536,576]{0,1:T(8,128)(2,1)}) %tuple.198), branch_computations={%region_25.26_spmd, %region_26.27_spmd} | conditional | flops 7279607808 | bytes 17694736 | solution.py:87
  510.7 13.3 %add_convert_fusion.9 = bf16[2048,576]{0,1:T(8,128)(2,1)} fusion(bf16[2048,576]{0,1:T(8,128)(2,1)S(1)} %copy.201, bf16[1536,576]{0,1:T(8,128)(2,1)} %get-tuple-element.429, bf16[576,1536]{1,0:T(8,128)(2,1)} %get-tuple-element.243), kind=kOutput, calls=%fused_computation.169 | convolution fusion | flops 7279607808 | bytes 8257536 | tf_op jit(solution)/shard_map/cond/branch_1_fun/dot_general | solution.py:25
  530.9 3.6 collective-permute-done.9
  537.8 16.6 %conditional.30 = (bf16[2048,576]{0,1:T(8,128)(2,1)}, bf16[1,2048,576]{1,2,0:T(8,128)(2,1)S(1)}) conditional(s32[]{:T(128)} %convert_element_type.247, bf16[2048,576]{0,1:T(8,128)(2,1)} %bitcast_select_fusion.7, (bf16[2048,576]{0,1:T(8,128)(2,1)}, bf16[576,1536]{1,0:T(8,128)(2,1)}, bf16[1536,576]{0,1:T(8,128)(2,1)}) %tuple.199), branch_computations={%region_27.28_spmd, %region_28.29_spmd} | conditional | flops 7279607808 | bytes 17694736 | solution.py:87
  539.5 13.3 %add_convert_fusion.10 = bf16[2048,576]{0,1:T(8,128)(2,1)} fusion(bf16[2048,576]{0,1:T(8,128)(2,1)S(1)} %copy.202, bf16[1536,576]{0,1:T(8,128)(2,1)} %get-tuple-element.432, bf16[576,1536]{1,0:T(8,128)(2,1)} %get-tuple-element.246), kind=kOutput, calls=%fused_computation.183 | convolution fusion | flops 7279607808 | bytes 8257536 | tf_op jit(solution)/shard_map/cond/branch_1_fun/dot_general | solution.py:25
  554.4 3.8 collective-permute-start.10
  564.2 18.3 %conditional.31 = (bf16[2048,576]{0,1:T(8,128)(2,1)}, bf16[1,2048,576]{1,2,0:T(8,128)(2,1)}) conditional(s32[]{:T(128)} %convert_element_type.248, bf16[2048,576]{0,1:T(8,128)(2,1)} %bitcast_select_fusion.6, (bf16[2048,576]{0,1:T(8,128)(2,1)}, bf16[576,1536]{1,0:T(8,128)(2,1)}, bf16[1536,576]{0,1:T(8,128)(2,1)}) %tuple.200), branch_computations={%region_29.30_spmd, %region_30.31_spmd} | conditional | flops 7279607808 | bytes 17694736 | solution.py:87
  565.8 13.3 %add_convert_fusion.11 = bf16[2048,576]{0,1:T(8,128)(2,1)} fusion(bf16[2048,576]{0,1:T(8,128)(2,1)S(1)} %copy.203, bf16[1536,576]{0,1:T(8,128)(2,1)} %get-tuple-element.435, bf16[576,1536]{1,0:T(8,128)(2,1)} %get-tuple-element.249), kind=kOutput, calls=%fused_computation.197 | convolution fusion | flops 7279607808 | bytes 8257536 | tf_op jit(solution)/shard_map/cond/branch_1_fun/dot_general | solution.py:25
  585.8 3.8 collective-permute-done.11
  592.9 16.6 %conditional.32 = (bf16[2048,576]{0,1:T(8,128)(2,1)}, bf16[1,2048,576]{1,2,0:T(8,128)(2,1)S(1)}) conditional(s32[]{:T(128)} %convert_element_type.249, bf16[2048,576]{0,1:T(8,128)(2,1)} %bitcast_select_fusion.5, (bf16[2048,576]{0,1:T(8,128)(2,1)}, bf16[576,1536]{1,0:T(8,128)(2,1)}, bf16[1536,576]{0,1:T(8,128)(2,1)}) %tuple.201), branch_computations={%region_31.32_spmd, %region_32.33_spmd} | conditional | flops 7279607808 | bytes 17694736 | solution.py:87
  594.5 13.3 %add_convert_fusion.12 = bf16[2048,576]{0,1:T(8,128)(2,1)} fusion(bf16[2048,576]{0,1:T(8,128)(2,1)S(1)} %copy.204, bf16[1536,576]{0,1:T(8,128)(2,1)} %get-tuple-element.438, bf16[576,1536]{1,0:T(8,128)(2,1)} %get-tuple-element.252), kind=kOutput, calls=%fused_computation.211 | convolution fusion | flops 7279607808 | bytes 8257536 | tf_op jit(solution)/shard_map/cond/branch_1_fun/dot_general | solution.py:25
  609.5 4.0 collective-permute-start.12
  619.3 18.3 %conditional.33 = (bf16[2048,576]{0,1:T(8,128)(2,1)}, bf16[1,2048,576]{1,2,0:T(8,128)(2,1)}) conditional(s32[]{:T(128)} %convert_element_type.250, bf16[2048,576]{0,1:T(8,128)(2,1)} %bitcast_select_fusion.4, (bf16[2048,576]{0,1:T(8,128)(2,1)}, bf16[576,1536]{1,0:T(8,128)(2,1)}, bf16[1536,576]{0,1:T(8,128)(2,1)}) %tuple.202), branch_computations={%region_33.34_spmd, %region_34.35_spmd} | conditional | flops 7279607808 | bytes 17694736 | solution.py:87
  620.9 13.3 %add_convert_fusion.13 = bf16[2048,576]{0,1:T(8,128)(2,1)} fusion(bf16[2048,576]{0,1:T(8,128)(2,1)S(1)} %copy.205, bf16[1536,576]{0,1:T(8,128)(2,1)} %get-tuple-element.441, bf16[576,1536]{1,0:T(8,128)(2,1)} %get-tuple-element.255), kind=kOutput, calls=%fused_computation.225 | convolution fusion | flops 7279607808 | bytes 8257536 | tf_op jit(solution)/shard_map/cond/branch_1_fun/dot_general | solution.py:25
  640.8 3.8 collective-permute-done.13
  648.0 16.6 %conditional.34 = (bf16[2048,576]{0,1:T(8,128)(2,1)}, bf16[1,2048,576]{1,2,0:T(8,128)(2,1)S(1)}) conditional(s32[]{:T(128)} %convert_element_type.251, bf16[2048,576]{0,1:T(8,128)(2,1)} %bitcast_select_fusion.3, (bf16[2048,576]{0,1:T(8,128)(2,1)}, bf16[576,1536]{1,0:T(8,128)(2,1)}, bf16[1536,576]{0,1:T(8,128)(2,1)}) %tuple.203), branch_computations={%region_35.36_spmd, %region_36.37_spmd} | conditional | flops 7279607808 | bytes 17694736 | solution.py:87
  649.6 13.3 %add_convert_fusion.14 = bf16[2048,576]{0,1:T(8,128)(2,1)} fusion(bf16[2048,576]{0,1:T(8,128)(2,1)S(1)} %copy.206, bf16[1536,576]{0,1:T(8,128)(2,1)} %get-tuple-element.444, bf16[576,1536]{1,0:T(8,128)(2,1)} %get-tuple-element.258), kind=kOutput, calls=%fused_computation.239 | convolution fusion | flops 7279607808 | bytes 8257536 | tf_op jit(solution)/shard_map/cond/branch_1_fun/dot_general | solution.py:25
  664.6 3.9 collective-permute-start.14
  674.4 20.5 %conditional.35 = (bf16[2048,576]{0,1:T(8,128)(2,1)}, bf16[1,2048,576]{1,2,0:T(8,128)(2,1)}) conditional(s32[]{:T(128)} %convert_element_type.252, bf16[2048,576]{0,1:T(8,128)(2,1)} %bitcast_select_fusion.2, (bf16[2048,576]{0,1:T(8,128)(2,1)}, bf16[576,1536]{1,0:T(8,128)(2,1)}, bf16[1536,576]{0,1:T(8,128)(2,1)}) %tuple.204), branch_computations={%region_37.38_spmd, %region_38.39_spmd} | conditional | flops 7279607808 | bytes 17694736 | solution.py:87
  677.9 13.6 %add_convert_fusion.15 = bf16[2048,576]{0,1:T(8,128)(2,1)} fusion(bf16[2048,576]{0,1:T(8,128)(2,1)} %copy.207, bf16[1536,576]{0,1:T(8,128)(2,1)} %get-tuple-element.447, bf16[576,1536]{1,0:T(8,128)(2,1)} %get-tuple-element.261), kind=kOutput, calls=%fused_computation.253 | convolution fusion | flops 7279607808 | bytes 8257536 | tf_op jit(solution)/shard_map/cond/branch_1_fun/dot_general | solution.py:25
  694.9 4.3 collective-permute-start.15
  717.4 18.8 %conditional.36 = (bf16[2048,576]{0,1:T(8,128)(2,1)}, bf16[1,2048,576]{1,2,0:T(8,128)(2,1)S(1)}) conditional(s32[]{:T(128)} %convert_element_type.253, bf16[2048,576]{0,1:T(8,128)(2,1)} %bitcast_select_fusion.1, (bf16[2048,576]{0,1:T(8,128)(2,1)}, bf16[576,1536]{1,0:T(8,128)(2,1)}, bf16[1536,576]{0,1:T(8,128)(2,1)}) %tuple.205), branch_computations={%region_39.40_spmd, %region_40.41_spmd} | conditional | flops 7279607808 | bytes 17694736 | solution.py:87
  717.4 3.5 copy.208
  720.9 13.6 %add_convert_fusion.16 = bf16[2048,576]{0,1:T(8,128)(2,1)} fusion(bf16[2048,576]{0,1:T(8,128)(2,1)} %copy.208, bf16[1536,576]{0,1:T(8,128)(2,1)} %get-tuple-element.450, bf16[576,1536]{1,0:T(8,128)(2,1)} %get-tuple-element.264), kind=kOutput, calls=%fused_computation.267 | convolution fusion | flops 7279607808 | bytes 8257536 | tf_op jit(solution)/shard_map/cond/branch_1_fun/dot_general | solution.py:25
  764.0 12.5 %broadcast_select_fusion = bf16[16,2048,576]{1,2,0:T(8,128)(2,1)} fusion(bf16[16,2048,576]{1,2,0:T(8,128)(2,1)} %constant_dynamic-update-slice_fusion, pred[]{:T(512)S(6)} %eq.5), kind=kLoop, calls=%fused_computation.287 | loop fusion | flops 18874368 | bytes 75497472 | tf_op jit(solution)/shard_map/jit(_where)/select_n | solution.py:93
  776.5 117.4 %all-reduce.2.cloned.1.call-done = bf16[16,2048,576]{1,2,0:T(8,128)(2,1)} async-done(((bf16[16,2048,576]{1,2,0:T(8,128)(2,1)}), bf16[16,2048,576]{1,2,0:T(8,128)(2,1)}) %all-reduce.2.cloned.1.call-update) | async-done | bytes 37748752 | tf_op jit(solution)/shard_map/psum | solution.py:94
  894.0 25.3 %copy.212 = bf16[16,2048,576]{1,2,0:T(8,128)(2,1)} copy(bf16[16,2048,576]{1,2,0:T(8,128)(2,1)} %all-reduce.2.cloned.1.call-done) | data formatting | bytes 75497472
  (145 shorter events, 213.3 us)
Async XLA Ops:
  7.2 153.6 %reduce-scatter.3.cloned.1.call-start = ((), (), s32[]{:S(2)}) async-start(), calls=%async_computation.2 | async-start | bytes 4423680 | tf_op jit(solution)/shard_map/reduce_scatter | solution.py:102
  11.2 1.7 copy-start.22
  14.3 8.4 copy-start.1
  22.6 49.7 %collective-permute-start = (bf16[2048,576]{0,1:T(8,128)(2,1)}, bf16[2048,576]{0,1:T(8,128)(2,1)}, u32[]{:S(2)}, u32[]{:S(2)}) collective-permute-start(bf16[2048,576]{0,1:T(8,128)(2,1)} %get-tuple-element.313), channel_id=1, source_target_pairs={{1,0},{3,2},{5,4},{7,6}} | collective-permute-start | bytes 7077896 | tf_op jit(solution)/shard_map/ppermute | solution.py:70
  117.4 1.8 copy-start
  117.4 88.4 %reduce-scatter.5.cloned.1.call-start = ((), (), s32[]{:S(2)}) async-start(), calls=%async_computation.3 | async-start | bytes 4423680 | tf_op jit(solution)/shard_map/reduce_scatter | solution.py:103
  119.2 118.0 %copy-start.26 = (f32[1,384,576]{1,2,0:T(8,128)S(1)}, f32[1,384,576]{1,2,0:T(8,128)}, u32[]{:S(2)}) copy-start(f32[1,384,576]{1,2,0:T(8,128)} %param.58) | copy-start | bytes 2654212
  119.2 118.0 %copy-start.27 = (f32[1,384,576]{1,2,0:T(8,128)S(1)}, f32[1,384,576]{1,2,0:T(8,128)}, u32[]{:S(2)}) copy-start(f32[1,384,576]{1,2,0:T(8,128)} %param.57) | copy-start | bytes 2654212
  119.2 118.0 %copy-start.28 = (f32[1,384,576]{1,2,0:T(8,128)S(1)}, f32[1,384,576]{1,2,0:T(8,128)}, u32[]{:S(2)}) copy-start(f32[1,384,576]{1,2,0:T(8,128)} %param.54) | copy-start | bytes 2654212
  119.2 146.6 %all-gather.3.cloned.1.call-start = ((), (), s32[]{:S(2)}) async-start(), calls=%async_computation.4 | async-start | bytes 2211840 | tf_op jit(solution)/shard_map/all_gather | solution.py:109
  205.8 31.4 %copy-start.20 = (f32[384,576]{0,1:T(8,128)S(1)}, f32[384,576]{0,1:T(8,128)}, u32[]{:S(2)}) copy-start(f32[384,576]{0,1:T(8,128)} %reduce-scatter.5.cloned.1.call-done) | copy-start | bytes 2654212
  237.1 56.8 %all-gather.5.cloned.1.call-start = ((), (), s32[]{:S(2)}) async-start(), calls=%async_computation.5 | async-start | bytes 2211840 | tf_op jit(solution)/shard_map/all_gather | solution.py:110
  239.6 654.4 %all-reduce.2.cloned.1.call-start = ((), (), s32[]{:S(2)}) async-start(), calls=%async_computation.6 | async-start | bytes 75497472 | tf_op jit(solution)/shard_map/psum | solution.py:94
  307.9 5.4 collective-permute-start.1
  333.3 10.4 %copy-start.4 = (bf16[1,2048,576]{1,2,0:T(8,128)(2,1)}, bf16[1,2048,576]{1,2,0:T(8,128)(2,1)S(1)}, u32[]{:S(2)}) copy-start(bf16[1,2048,576]{1,2,0:T(8,128)(2,1)S(1)} %get-tuple-element.316) | copy-start | bytes 7077892
  333.3 7.1 collective-permute-start.2
  362.0 7.1 collective-permute-start.3
  389.1 9.7 %copy-start.6 = (bf16[1,2048,576]{1,2,0:T(8,128)(2,1)}, bf16[1,2048,576]{1,2,0:T(8,128)(2,1)S(1)}, u32[]{:S(2)}) copy-start(bf16[1,2048,576]{1,2,0:T(8,128)(2,1)S(1)} %get-tuple-element.320) | copy-start | bytes 7077892
  389.1 6.4 collective-permute-start.4
  417.2 7.1 collective-permute-start.5
  444.2 9.7 %copy-start.8 = (bf16[1,2048,576]{1,2,0:T(8,128)(2,1)}, bf16[1,2048,576]{1,2,0:T(8,128)(2,1)S(1)}, u32[]{:S(2)}) copy-start(bf16[1,2048,576]{1,2,0:T(8,128)(2,1)S(1)} %get-tuple-element.324) | copy-start | bytes 7077892
  444.2 6.4 collective-permute-start.6
  472.3 7.1 collective-permute-start.7
  499.3 9.7 %copy-start.10 = (bf16[1,2048,576]{1,2,0:T(8,128)(2,1)}, bf16[1,2048,576]{1,2,0:T(8,128)(2,1)S(1)}, u32[]{:S(2)}) copy-start(bf16[1,2048,576]{1,2,0:T(8,128)(2,1)S(1)} %get-tuple-element.328) | copy-start | bytes 7077892
  499.4 6.4 collective-permute-start.8
  527.4 7.1 collective-permute-start.9
  554.4 9.7 %copy-start.12 = (bf16[1,2048,576]{1,2,0:T(8,128)(2,1)}, bf16[1,2048,576]{1,2,0:T(8,128)(2,1)S(1)}, u32[]{:S(2)}) copy-start(bf16[1,2048,576]{1,2,0:T(8,128)(2,1)S(1)} %get-tuple-element.332) | copy-start | bytes 7077892
  554.4 6.4 collective-permute-start.10
  582.5 7.1 collective-permute-start.11
  609.5 9.8 %copy-start.14 = (bf16[1,2048,576]{1,2,0:T(8,128)(2,1)}, bf16[1,2048,576]{1,2,0:T(8,128)(2,1)S(1)}, u32[]{:S(2)}) copy-start(bf16[1,2048,576]{1,2,0:T(8,128)(2,1)S(1)} %get-tuple-element.336) | copy-start | bytes 7077892
  609.5 6.4 collective-permute-start.12
  637.6 7.1 collective-permute-start.13
  664.6 9.8 %copy-start.16 = (bf16[1,2048,576]{1,2,0:T(8,128)(2,1)}, bf16[1,2048,576]{1,2,0:T(8,128)(2,1)S(1)}, u32[]{:S(2)}) copy-start(bf16[1,2048,576]{1,2,0:T(8,128)(2,1)S(1)} %get-tuple-element.340) | copy-start | bytes 7077892
  664.6 6.4 collective-permute-start.14
  674.4 24.9 %copy-start.5 = (bf16[1,2048,576]{1,2,0:T(8,128)(2,1)S(1)}, bf16[1,2048,576]{1,2,0:T(8,128)(2,1)}, u32[]{:S(2)}) copy-start(bf16[1,2048,576]{1,2,0:T(8,128)(2,1)} %copy-done.4) | copy-start | bytes 7077892
  694.9 19.1 %collective-permute-start.15 = (bf16[2048,576]{0,1:T(8,128)(2,1)}, bf16[2048,576]{0,1:T(8,128)(2,1)}, u32[]{:S(2)}, u32[]{:S(2)}) collective-permute-start(bf16[2048,576]{0,1:T(8,128)(2,1)} %get-tuple-element.343), channel_id=1, source_target_pairs={{0,1},{2,3},{4,5},{6,7}} | collective-permute-start | bytes 7077896 | tf_op jit(solution)/shard_map/ppermute | solution.py:91
  699.3 4.9 copy-start.7
  704.2 4.9 copy-start.9
  717.4 20.5 %copy-start.11 = (bf16[1,2048,576]{1,2,0:T(8,128)(2,1)S(1)}, bf16[1,2048,576]{1,2,0:T(8,128)(2,1)}, u32[]{:S(2)}) copy-start(bf16[1,2048,576]{1,2,0:T(8,128)(2,1)} %copy-done.10) | copy-start | bytes 7077892
  736.1 1.7 copy-start.18
  736.1 23.0 %collective-permute-start.16 = (bf16[2048,576]{0,1:T(8,128)(2,1)}, bf16[2048,576]{0,1:T(8,128)(2,1)S(1)}, u32[]{:S(2)}, u32[]{:S(2)}) collective-permute-start(bf16[2048,576]{0,1:T(8,128)(2,1)} %get-tuple-element.345), channel_id=1, source_target_pairs={{0,1},{2,3},{4,5},{6,7}} | collective-permute-start | bytes 7077896 | tf_op jit(solution)/shard_map/ppermute | solution.py:91
  737.8 4.9 copy-start.13
  742.8 4.9 copy-start.15
  747.7 4.9 copy-start.17
  752.6 4.9 copy-start.19
Sparse Core Ops, SparseCore 0:
  117.5 43.1 reduce-scatter.2
  164.4 41.3 reduce-scatter.4
  237.2 28.5 all-gather.2
  267.4 26.4 all-gather.4
  776.6 117.2 all-reduce.1
where the time goes:
time: 938 us; the launch traced here: 926 us
  waiting for transfers between devices  345 us (37%)
  matrix products  257 us (27%)
  local copies, waits for them, and re-layouts  148 us (16%)
  other arithmetic  76.7 us (8%)
  starting transfers between devices  58.4 us (6%)
  blocking collectives  22.2 us (2%)
  between operations  18 us (2%)
    dot_general x16, matrix products, stage_forward(): branch = jnp.dot(hidden, w_down, preferred_element_type=jnp.float32)  213 us
    psum x1, waiting for transfers between devices, forward_stages(): return lax.psum(own_part, 'stage')  117 us
    unnamed x67, local copies, waits for them, and re-layouts  79.9 us
    cond x31, local copies, waits for them, and re-layouts  67 us
    ppermute x16, starting transfers between devices, forward_stages(): received = lax.ppermute(stage_out, 'stage', fwd_perm)  56.9 us
    select_n x17, other arithmetic, forward_stages(): jnp.where(my_stage == 0, micro_in[min(step, n_micro - 1)], received)  53.5 us
    ppermute x1, waiting for transfers between devices, backward_stages(): grad_buf = lax.ppermute(d_in, 'stage', back_perm)  48.4 us
    reduce_scatter x1, waiting for transfers between devices, step_body(): lax.psum_scatter(sum_down, 'data', scatter_dimension=0, tiled=True) / n_data  43 us
  transfers between devices with their start and end apart: 22, of which 20 were waited for; matrix products, arithmetic and copies ran while one was open for 5% of the time, Pallas kernels for 0%

commit v1 on v0

--- a/solution.py
+++ b/solution.py
@@ -1,6 +1,8 @@
 import jax
 import jax.numpy as jnp
 from jax import lax
+from jax.experimental import pallas as pl
+from jax.experimental.pallas import tpu as pltpu
 from jax.sharding import PartitionSpec as P
 
 BETA_ONE = 0.9
@@ -19,13 +21,6 @@
     return jax.nn.gelu(pre_act, approximate=True)
 
 
-def stage_forward(stage_in, w_up, w_down):
-    pre_act = jnp.dot(stage_in, w_up, preferred_element_type=jnp.float32)
-    hidden = gelu_tanh(pre_act).astype(jnp.bfloat16)
-    branch = jnp.dot(hidden, w_down, preferred_element_type=jnp.float32)
-    return (stage_in.astype(jnp.float32) + branch).astype(jnp.bfloat16)
-
-
 def stage_backward(stage_in, grad_in, w_up, w_down):
     pre_act = jnp.dot(stage_in, w_up, preferred_element_type=jnp.float32)
     hidden, gelu_pull = jax.vjp(gelu_tanh, pre_act)
@@ -46,12 +41,143 @@
     return new_master, mom_one, mom_two
 
 
+GELU_LIN = 0.7978845608028654
+GELU_CUB = GELU_LIN * 0.044715
+ROW_TILE = 512
+FF_TILE = 512
+CHUNKS = (4, 2, 1, 1)
+
+
+def gelu_half(pre_act):
+    inner = pre_act * (GELU_LIN + GELU_CUB * (pre_act * pre_act))
+    half = 0.5 * pre_act
+    return half + half * jnp.tanh(inner)
+
+
+def block_forward(cols_in, w_up_t, w_down_t, block, hidden_ref):
+    ff_width = w_up_t.shape[1]
+    for start in range(0, ff_width, FF_TILE):
+        pre_act = jnp.dot(w_up_t[block, start:start + FF_TILE, :], cols_in, preferred_element_type=jnp.float32)
+        hidden_ref[start:start + FF_TILE, :] = gelu_half(pre_act).astype(jnp.bfloat16)
+    branch = jnp.dot(w_down_t[block], hidden_ref[...], preferred_element_type=jnp.float32)
+    return (cols_in.astype(jnp.float32) + branch).astype(jnp.bfloat16)
+
+
+def forward_kernel(has_prev, n_recv, base, recv_base, n_own, n_tiles, *refs):
+    refs = list(refs)
+    x_ref, w_up_t, w_down_t = refs[:3]
+    refs = refs[3:]
+    recv_ref = None
+    if n_recv:
+        recv_ref = refs.pop(0)
+    if has_prev:
+        refs.pop(0)
+    out_ref, y_ref, hidden_ref, y_buf, y_sem, recv_sem = refs
+    mine = lax.axis_index('stage')
+    micro, tile = pl.program_id(0), pl.program_id(1)
+    step = micro * n_tiles + tile
+    slot = lax.rem(step, 2)
+    tile_cols = pl.ds(pl.multiple_of(tile * ROW_TILE, ROW_TILE), ROW_TILE)
+
+    def y_copy(which):
+        return pltpu.make_async_copy(y_buf.at[which], out_ref.at[mine * n_own + base + micro, :, tile_cols], y_sem.at[which])
+
+    def recv_copy():
+        first = (1 - mine) * n_own + recv_base
+        return pltpu.make_async_copy(recv_ref, out_ref.at[pl.ds(first, n_recv), :, tile_cols], recv_sem)
+
+    if n_recv:
+        recv_copy().start()
+
+    cols = x_ref[0]
+    for block in range(2):
+        cols = block_forward(cols, w_up_t, w_down_t, block, hidden_ref)
+
+    @pl.when(step >= 2)
+    def _():
+        y_copy(slot).wait()
+
+    y_buf[slot] = cols
+    y_ref[0] = cols
+    y_copy(slot).start()
+    if n_recv:
+        recv_copy().wait()
+
+    @pl.when(step == pl.num_programs(0) * n_tiles - 1)
+    def _():
+        y_copy(slot).wait()
+        y_copy(1 - slot).wait()
+
+
+def forward_chunk(base, n_chunk, micro_t, w_up_t, w_down_t, prev_out, recv, recv_base):
+    n_micro, width, n_rows = micro_t.shape
+    n_own = n_micro // 2
+    n_tiles = n_rows // ROW_TILE
+    ff_width = w_up_t.shape[1]
+    n_recv = 0 if recv is None else recv.shape[0]
+    mine = lax.axis_index('stage')
+    any_spec = pl.BlockSpec(memory_space=pl.ANY)
+    scalar = jnp.full((1,), mine * n_own + base, jnp.int32)
+    in_specs = [pl.BlockSpec((1, width, ROW_TILE), lambda i, j, first: (first[0] + i, 0, j)),
+                pl.BlockSpec((2, ff_width, width), lambda i, j, first: (0, 0, 0)),
+                pl.BlockSpec((2, width, ff_width), lambda i, j, first: (0, 0, 0))]
+    operands = [micro_t, w_up_t, w_down_t]
+    if n_recv:
+        in_specs.append(pl.BlockSpec((n_recv, width, ROW_TILE), lambda i, j, first: (0, 0, j)))
+        operands.append(recv)
+    aliases = {}
+    if prev_out is not None:
+        in_specs.append(any_spec)
+        operands.append(prev_out)
+        aliases = {len(operands): 0}
+
+    def body(first, *refs):
+        forward_kernel(prev_out is not None, n_recv, base, recv_base, n_own, n_tiles, *refs)
+
+    flops = 8 * n_chunk * n_rows * width * ff_width
+    return pl.pallas_call(
+        body,
+        grid_spec=pltpu.PrefetchScalarGridSpec(
+            num_scalar_prefetch=1, grid=(n_chunk, n_tiles), in_specs=in_specs,
+            out_specs=[any_spec, pl.BlockSpec((1, width, ROW_TILE), lambda i, j, first: (i, 0, j))],
+            scratch_shapes=[pltpu.VMEM((ff_width, ROW_TILE), jnp.bfloat16), pltpu.VMEM((2, width, ROW_TILE), jnp.bfloat16),
+                            pltpu.SemaphoreType.DMA((2,)), pltpu.SemaphoreType.DMA]),
+        out_shape=[jax.ShapeDtypeStruct(micro_t.shape, jnp.bfloat16),
+                   jax.ShapeDtypeStruct((n_chunk, width, n_rows), jnp.bfloat16)],
+        input_output_aliases=aliases,
+        compiler_params=pltpu.CompilerParams(dimension_semantics=("arbitrary", "arbitrary"),
+                                             vmem_limit_bytes=48 * 1024 * 1024),
+        cost_estimate=pl.CostEstimate(flops=flops, bytes_accessed=4 * n_chunk * n_rows * width, transcendentals=0),
+        name=f"fwd_{base}",
+    )(scalar, *operands)
+
+
+def forward_all(micro_in, w_up_t, w_down_t):
+    micro_t = jnp.swapaxes(micro_in, 1, 2)
+    n_own = micro_in.shape[0] // 2
+    swap = [(0, 1), (1, 0)]
+    mine = lax.axis_index('stage')
+    out, base = None, 0
+    received = []
+    for n_chunk in CHUNKS:
+        recv, recv_base = None, 0
+        if len(received) >= 2 and received[-2] is not None:
+            recv, recv_base = received[-2]
+            received[-2] = None
+        out, part = forward_chunk(base, n_chunk, micro_t, w_up_t, w_down_t, out, recv, recv_base)
+        received.append((lax.ppermute(part, 'stage', swap), base))
+        base += n_chunk
+    for item in received:
+        if item is not None:
+            out = lax.dynamic_update_slice(out, item[0], ((1 - mine) * n_own + item[1], 0, 0))
+    return jnp.swapaxes(out, 1, 2)
+
+
 def solution(mesh):
     n_stage = mesh.shape['stage']
     n_data = mesh.shape['data']
     last_stage = n_stage - 1
     back_perm = [(source, source - 1) for source in range(1, n_stage)]
-    fwd_perm = [(source, source + 1) for source in range(last_stage)]
 
     def backward_stages(my_stage, stage_in, grad_last, w_up, w_down, acc_up, acc_down):
         def run_stage(operands):
@@ -69,29 +195,6 @@
             if step < last_stage:
                 grad_buf = lax.ppermute(d_in, 'stage', back_perm)
         return acc_up, acc_down
-
-    def forward_stages(my_stage, micro_in, w_up, w_down):
-        def run_block(block):
-            return stage_forward(block, w_up, w_down)
-
-        def keep_block(block):
-            return block
-
-        n_micro = micro_in.shape[0]
-        n_steps = n_micro + last_stage
-        received = jnp.zeros_like(micro_in[0])
-        results = []
-        for step in range(n_steps):
-            stage_in = jnp.where(my_stage == 0, micro_in[min(step, n_micro - 1)], received)
-            active = (my_stage <= step) & (my_stage > step - n_micro)
-            stage_out = lax.cond(active, run_block, keep_block, stage_in)
-            if step >= last_stage:
-                results.append(stage_out)
-            if step < n_steps - 1:
-                received = lax.ppermute(stage_out, 'stage', fwd_perm)
-        stacked = jnp.stack(results)
-        own_part = jnp.where(my_stage == last_stage, stacked, jnp.zeros_like(stacked))
-        return lax.psum(own_part, 'stage')
 
     def step_body(master_up, master_down, moment1_up, moment2_up, moment1_down, moment2_down,
                   compute_up, compute_down, accum_up, accum_down, stage_acts, loss_grad, next_micro,
@@ -108,7 +211,9 @@
         new_down, mom1_down, mom2_down = adamw_update(master_down[0], moment1_down[0], moment2_down[0], clip * shard_down, learn_rate)
         full_up = lax.all_gather(new_up.astype(jnp.bfloat16), 'data', axis=0, tiled=True)
         full_down = lax.all_gather(new_down.astype(jnp.bfloat16), 'data', axis=0, tiled=True)
-        last_acts = forward_stages(my_stage, next_micro, full_up, full_down)
+        both_up = lax.all_gather(full_up.T, 'stage')
+        both_down = lax.all_gather(full_down.T, 'stage')
+        last_acts = forward_all(next_micro, both_up, both_down)
         return (new_up[None], new_down[None], mom1_up[None], mom2_up[None],
                 mom1_down[None], mom2_down[None], last_acts)
 

time: 938 us -> 510 us (0.54)
  matrix products: 257 us -> 44.4 us
  Pallas kernels: 0 us -> 168 us
  waiting for transfers between devices: 345 us -> 205 us
  local copies, waits for them, and re-layouts: 148 us -> 29.3 us
  other arithmetic: 76.7 us -> 10.7 us
  starting transfers between devices: 58.4 us -> 2.62 us
    dot_general x16 -> x0, matrix products: 213 us -> none  [stage_forward(): branch = jnp.dot(hidden, w_down, preferred_element_type=jnp.float32)]
    pallas_call x0 -> x4, Pallas kernels: none -> 168 us  [forward_chunk(): pl.pallas_call(body, grid_spec=pltpu.PrefetchScalarGridSpec(num_scalar_pr...]
    psum x1 -> x0, waiting for transfers between devices: 117 us -> none  [forward_stages(): return lax.psum(own_part, 'stage')]
    cond x31 -> x0, local copies, waits for them, and re-layouts: 67 us -> none
    select_n x18 -> x0, other arithmetic: 66 us -> none  [the longest x17 53.5 us: forward_stages(): jnp.where(my_stage == 0, micro_in[min(step, n_micro - 1)], received)]
    unnamed x67 -> x22, local copies, waits for them, and re-layouts: 79.9 us -> 18.1 us
    ppermute x16 -> x4, starting transfers between devices: 56.9 us -> 1.11 us  [forward_all(): received.append((lax.ppermute(part, 'stage', swap), base))]
    ppermute x16 -> x4, waiting for transfers between devices: 42.5 us -> 0.87 us  [forward_all(): received.append((lax.ppermute(part, 'stage', swap), base))]
  transfers between devices with their start and end apart: 22 -> 11, of which waited for: 20 -> 8; matrix products, arithmetic and copies ran while one was open for 5% -> 3% of each run, Pallas kernels for 0% -> 18%
where the time goes in v1:
time: 510 us; the launch traced here: 501 us
  waiting for transfers between devices  205 us (40%)
  Pallas kernels  168 us (33%)
  matrix products  44.4 us (9%)
  local copies, waits for them, and re-layouts  29.3 us (6%)
  blocking collectives  22.2 us (4%)
  between operations  18.2 us (4%)
  other arithmetic  10.7 us (2%)
    pallas_call x4, Pallas kernels, forward_chunk(): pl.pallas_call(body, grid_spec=pltpu.PrefetchScalarGridSpec(num_scalar_pr...  168 us
    ppermute x1, waiting for transfers between devices, backward_stages(): grad_buf = lax.ppermute(d_in, 'stage', back_perm)  48.4 us
    reduce_scatter x1, waiting for transfers between devices, step_body(): lax.psum_scatter(sum_down, 'data', scatter_dimension=0, tiled=True) / n_data  43 us
    reduce_scatter x1, waiting for transfers between devices, step_body(): lax.psum_scatter(sum_up, 'data', scatter_dimension=0, tiled=True) / n_data  40.7 us
    all_gather x1, waiting for transfers between devices, step_body(): lax.all_gather(new_down.astype(jnp.bfloat16), 'data', axis=0, tiled=True)  28.1 us
    all_gather x1, waiting for transfers between devices, step_body(): lax.all_gather(new_up.astype(jnp.bfloat16), 'data', axis=0, tiled=True)  26.2 us
    dot_general x1, matrix products, stage_backward(): lax.dot_general(stage_in, d_pre, DOT_ROWS, preferred_element_type=jnp.flo...  26.1 us
    psum x1, blocking collectives, step_body(): total_sq = lax.psum(local_sq, ('stage', 'data'))  22.2 us
  transfers between devices with their start and end apart: 11, of which 8 were waited for; matrix products, arithmetic and copies ran while one was open for 3% of the time, Pallas kernels for 18%

profile of v1, /device:TPU:0, one launch (start us, length us, event | category | flops | bytes accessed | tf_op | source)
XLA Modules:
  0.0 501.0 jit_solution(18300131852005250601)
XLA Ops:
  7.2 0.0 reduce-scatter.3.cloned.1.call-start
  7.2 0.0 copy-start.8
  7.2 4.1 copy.53
  11.4 0.0 copy-done.8
  11.4 0.0 copy-start.3
  11.4 1.4 copy.55
  12.8 4.4 copy.29
  17.2 4.4 copy.30
  21.5 0.0 copy-done.3
  21.6 1.3 collective-permute-start
  22.8 48.4 %collective-permute-done = bf16[2048,576]{0,1:T(8,128)(2,1)} collective-permute-done((bf16[2048,576]{0,1:T(8,128)(2,1)}, bf16[2048,576]{0,1:T(8,128)(2,1)}, u32[]{:S(2)}, u32[]{:S(2)}) %collective-permute-start) | collective-permute-done | bytes 2359328 | tf_op jit(solution)/shard_map/ppermute | solution.py:196
  71.3 44.8 %conditional.3 = ((f32[576,1536]{1,0:T(8,128)}, f32[1536,576]{0,1:T(8,128)S(1)})) conditional(s32[]{:T(128)} %convert_element_type.30, (f32[576,1536]{1,0:T(8,128)}, f32[1536,576]{0,1:T(8,128)S(1)}) %tuple.24, (bf16[2048,576]{0,1:T(8,128)(2,1)}, bf16[1536,576]{1,0:T(8,128)(2,1)}, bf16[2048,576]{1,0:T(8,128)(2,1)}, bf16[576,1536]{1,0:T(8,128)(2,1)}, ...), branch_computations={%region_2.0_spmd, %region_3.0_spmd} | conditional | flops 14588510208 | bytes 64880664 | solution.py:193
  71.4 9.8 %fusion.52 = f32[2048,1536]{1,0:T(8,128)} fusion(bf16[2048,576]{1,0:T(8,128)(2,1)} %get-tuple-element.43, bf16[576,1536]{1,0:T(8,128)(2,1)} %get-tuple-element.44), kind=kOutput, calls=%fused_computation.73 | convolution fusion | flops 3623878656 | bytes 16711680 | tf_op jit(solution)/shard_map/cond/branch_1_fun/dot_general | solution.py:25
  81.2 26.1 %bitcast_add_fusion.1 = f32[576,1536]{1,0:T(8,128)} fusion(f32[576,1536]{1,0:T(8,128)} %get-tuple-element.40, bf16[2048,576]{1,0:T(8,128)(2,1)} %get-tuple-element.43, f32[2048,1536]{1,0:T(8,128)} %fusion.52, bf16[2048,576]{0,1:T(8,128)(2,1)} %get-tuple-element.79, bf16[1536,576]{1,0:T(8,128)(2,1)} %get-tuple-element.42), kind=kOutput, calls=%fused_computation.36 | convolution fusion | flops 7311556608 | bytes 26148864 | tf_op jit(solution)/shard_map/cond/branch_1_fun/dot_general | solution.py:31
  107.3 8.5 %fusion.28 = f32[1536,576]{0,1:T(8,128)S(1)} fusion(f32[1536,576]{0,1:T(8,128)S(1)} %get-tuple-element.45, bf16[2048,576]{0,1:T(8,128)(2,1)} %get-tuple-element.79, f32[2048,1536]{1,0:T(8,128)} %fusion.52), kind=kOutput, calls=%fused_computation.37 | convolution fusion | flops 3653074944 | bytes 22020096 | tf_op jit(solution)/shard_map/cond/branch_1_fun/dot_general | solution.py:28
  116.0 0.0 copy-start.2
  116.1 0.0 reduce-scatter.3.cloned.1.call-update
  116.1 0.0 reduce-scatter.5.cloned.1.call-start
  116.1 1.7 copy-done.2
  117.8 0.0 reduce-scatter.5.cloned.1.call-update
  117.9 0.0 copy-start.12
  117.9 0.0 copy-start.13
  117.9 0.0 copy-start.14
  117.9 0.0 all-gather.7.cloned.1.call-start
  118.8 40.7 %reduce-scatter.3.cloned.1.call-done = f32[144,1536]{1,0:T(8,128)} async-done(((f32[576,1536]{1,0:T(8,128)}), f32[144,1536]{1,0:T(8,128)}) %reduce-scatter.3.cloned.1.call-update) | async-done | bytes 884752 | tf_op jit(solution)/shard_map/reduce_scatter | solution.py:205
  159.4 2.0 multiply_reduce_fusion.1
  161.4 43.0 %reduce-scatter.5.cloned.1.call-done = f32[384,576]{0,1:T(8,128)} async-done(((f32[1536,576]{0,1:T(8,128)}), f32[384,576]{0,1:T(8,128)}) %reduce-scatter.5.cloned.1.call-update) | async-done | bytes 884752 | tf_op jit(solution)/shard_map/reduce_scatter | solution.py:206
  204.5 0.0 copy-start.6
  204.5 2.1 multiply_reduce_fusion
  208.5 22.2 %psum.7 = f32[]{:T(128)} all-reduce(f32[]{:T(128)S(6)} %add.96), channel_id=1, replica_groups=mesh['data'=4,'stage'=2] {'stage','data'}, use_global_device_ids=true, to_apply=%region_8.0 | all-reduce | flops 1 | bytes 8 | tf_op jit(solution)/shard_map/psum | solution.py:208
  231.5 4.3 fusion.50
  235.8 0.0 all-gather.7.cloned.1.call-update
  235.8 0.0 all-gather.9.cloned.1.call-start
  235.8 0.0 copy-done.12
  235.8 0.0 copy-done.13
  235.9 0.0 copy-done.14
  235.9 0.0 copy-done.6
  235.9 2.3 fusion.49
  238.2 0.0 all-gather.9.cloned.1.call-update
  238.2 0.0 all-gather.11.cloned.1.call-start
  238.3 26.2 %all-gather.7.cloned.1.call-done = bf16[576,1536]{1,0:T(8,128)(2,1)} async-done(((bf16[144,1536]{1,0:T(8,128)(2,1)}), bf16[576,1536]{1,0:T(8,128)(2,1)}) %all-gather.7.cloned.1.call-update) | async-done | bytes 1769488 | tf_op jit(solution)/shard_map/all_gather | solution.py:212
  264.5 0.0 all-gather.11.cloned.1.call-update
  264.5 0.0 all-gather.13.cloned.1.call-start
  264.5 28.1 %all-gather.9.cloned.1.call-done = bf16[1536,576]{0,1:T(8,128)(2,1)} async-done(((bf16[384,576]{0,1:T(8,128)(2,1)}), bf16[1536,576]{0,1:T(8,128)(2,1)}) %all-gather.9.cloned.1.call-update) | async-done | bytes 1769488 | tf_op jit(solution)/shard_map/all_gather | solution.py:213
  292.6 0.0 all-gather.13.cloned.1.call-update
  292.6 11.5 %all-gather.11.cloned.1.call-done = bf16[3072,576]{0,1:T(8,128)(2,1)} async-done(((bf16[1536,576]{0,1:T(8,128)(2,1)}), bf16[3072,576]{0,1:T(8,128)(2,1)}) %all-gather.11.cloned.1.call-update) | async-done | bytes 3538960 | tf_op jit(solution)/shard_map/all_gather | solution.py:214
  304.2 6.3 %copy.32 = bf16[3072,576]{1,0:T(8,128)(2,1)} copy(bf16[3072,576]{0,1:T(8,128)(2,1)} %all-gather.11.cloned.1.call-done) | data formatting | bytes 7077888 | tf_op jit(solution)/shard_map/all_gather | solution.py:214
  310.5 6.4 %all-gather.13.cloned.1.call-done = bf16[1152,1536]{1,0:T(8,128)(2,1)} async-done(((bf16[576,1536]{1,0:T(8,128)(2,1)}), bf16[1152,1536]{1,0:T(8,128)(2,1)}) %all-gather.13.cloned.1.call-update) | async-done | bytes 3538960 | tf_op jit(solution)/shard_map/all_gather | solution.py:215
  316.9 2.0 copy-done
  318.9 79.3 %fwd_0.1 = (bf16[16,576,2048]{2,1,0:T(8,128)(2,1)}, bf16[4,576,2048]{2,1,0:T(8,128)(2,1)}) custom-call(s32[1]{0:T(128)} %bitcast.26.first, bf16[16,576,2048]{2,1,0:T(8,128)(2,1)} %bitcast.96, bf16[2,1536,576]{2,1,0:T(8,128)(2,1)} %bitcast.101, bf16[2,576,1536]{2,1,0:T(8,128)(2,1)S(1)} %bitcast.92), custom_call_target="tpu_custom_call" | custom-call | flops 57982058496 | bytes 18874368 | tf_op jit(solution)/shard_map/fwd_0/pallas_call | solution.py:138
  398.2 0.2 collective-permute-start.2
  398.5 0.0 copy-done.1
  398.5 41.6 %fwd_4.1 = (bf16[16,576,2048]{2,1,0:T(8,128)(2,1)}, bf16[2,576,2048]{2,1,0:T(8,128)(2,1)}) custom-call(s32[1]{0:T(128)} %bitcast.25.first, bf16[16,576,2048]{2,1,0:T(8,128)(2,1)} %bitcast.97, bf16[2,1536,576]{2,1,0:T(8,128)(2,1)} %bitcast.102, bf16[2,576,1536]{2,1,0:T(8,128)(2,1)S(1)} %bitcast.93, ...), custom_call_target="tpu_custom_call", output_to_operand_aliasing={{0}: (4, {})} | custom-call | flops 28991029248 | bytes 9437184 | tf_op jit(solution)/shard_map/fwd_4/pallas_call | solution.py:138
  440.0 0.3 collective-permute-start.1
  440.4 0.0 collective-permute-done.2.refs_3_
  440.4 23.8 %fwd_6.1 = (bf16[16,576,2048]{2,1,0:T(8,128)(2,1)}, bf16[1,576,2048]{2,1,0:T(8,128)(2,1)}) custom-call(s32[1]{0:T(128)} %bitcast.27.first, bf16[16,576,2048]{2,1,0:T(8,128)(2,1)} %bitcast.98, bf16[2,1536,576]{2,1,0:T(8,128)(2,1)} %bitcast.103, bf16[2,576,1536]{2,1,0:T(8,128)(2,1)S(1)} %bitcast.94, ...), custom_call_target="tpu_custom_call", output_to_operand_aliasing={{0}: (5, {})} | custom-call | flops 14495514624 | bytes 4718592 | tf_op jit(solution)/shard_map/fwd_6/pallas_call | solution.py:138
  464.2 0.2 collective-permute-start.3
  464.4 0.0 collective-permute-done.1.refs_3_
  464.4 23.1 %fwd_7.1 = (bf16[16,576,2048]{2,1,0:T(8,128)(2,1)}, bf16[1,576,2048]{2,1,0:T(8,128)(2,1)}) custom-call(s32[1]{0:T(128)} %bitcast.19.first, bf16[16,576,2048]{2,1,0:T(8,128)(2,1)} %bitcast.99, bf16[2,1536,576]{2,1,0:T(8,128)(2,1)} %bitcast.104, bf16[2,576,1536]{2,1,0:T(8,128)(2,1)S(1)} %bitcast.95, ...), custom_call_target="tpu_custom_call", output_to_operand_aliasing={{0}: (5, {})} | custom-call | flops 14495514624 | bytes 4718592 | tf_op jit(solution)/shard_map/fwd_7/pallas_call | solution.py:138
  487.6 0.3 collective-permute-start.4
  487.9 0.0 collective-permute-done.3
  487.9 3.4 constant_dynamic-update-slice_fusion.1
  491.3 0.9 collective-permute-done.4
  492.1 1.6 constant_dynamic-update-slice_fusion
  (3 shorter events, 0.0 us)
Async XLA Ops:
  7.2 152.3 %reduce-scatter.3.cloned.1.call-start = ((), (), s32[]{:S(2)}) async-start(), calls=%async_computation.2 | async-start | bytes 4423680 | tf_op jit(solution)/shard_map/reduce_scatter | solution.py:205
  7.2 4.1 copy-start.8
  11.4 10.2 %copy-start.3 = (f32[1,1,1536,576]{2,3,1,0:T(8,128)S(1)}, f32[1,1,1536,576]{2,3,1,0:T(8,128)}, u32[]{:S(2)}) copy-start(f32[1,1,1536,576]{2,3,1,0:T(8,128)} %param.28) | copy-start | bytes 10616836
  21.6 49.7 %collective-permute-start = (bf16[2048,576]{0,1:T(8,128)(2,1)}, bf16[2048,576]{0,1:T(8,128)(2,1)}, u32[]{:S(2)}, u32[]{:S(2)}) collective-permute-start(bf16[2048,576]{0,1:T(8,128)(2,1)} %get-tuple-element.68), channel_id=1, source_target_pairs={{1,0},{3,2},{5,4},{7,6}} | collective-permute-start | bytes 7077896 | tf_op jit(solution)/shard_map/ppermute | solution.py:196
  116.0 1.8 copy-start.2
  116.1 88.4 %reduce-scatter.5.cloned.1.call-start = ((), (), s32[]{:S(2)}) async-start(), calls=%async_computation.3 | async-start | bytes 4423680 | tf_op jit(solution)/shard_map/reduce_scatter | solution.py:206
  117.9 118.0 %copy-start.12 = (f32[1,384,576]{1,2,0:T(8,128)S(1)}, f32[1,384,576]{1,2,0:T(8,128)}, u32[]{:S(2)}) copy-start(f32[1,384,576]{1,2,0:T(8,128)} %param.24) | copy-start | bytes 2654212
  117.9 118.0 %copy-start.13 = (f32[1,384,576]{1,2,0:T(8,128)S(1)}, f32[1,384,576]{1,2,0:T(8,128)}, u32[]{:S(2)}) copy-start(f32[1,384,576]{1,2,0:T(8,128)} %param.23) | copy-start | bytes 2654212
  117.9 118.0 %copy-start.14 = (f32[1,384,576]{1,2,0:T(8,128)S(1)}, f32[1,384,576]{1,2,0:T(8,128)}, u32[]{:S(2)}) copy-start(f32[1,384,576]{1,2,0:T(8,128)} %param.20) | copy-start | bytes 2654212
  117.9 146.6 %all-gather.7.cloned.1.call-start = ((), (), s32[]{:S(2)}) async-start(), calls=%async_computation.4 | async-start | bytes 2211840 | tf_op jit(solution)/shard_map/all_gather | solution.py:212
  204.5 31.4 %copy-start.6 = (f32[384,576]{0,1:T(8,128)S(1)}, f32[384,576]{0,1:T(8,128)}, u32[]{:S(2)}) copy-start(f32[384,576]{0,1:T(8,128)} %reduce-scatter.5.cloned.1.call-done) | copy-start | bytes 2654212
  235.8 56.8 %all-gather.9.cloned.1.call-start = ((), (), s32[]{:S(2)}) async-start(), calls=%async_computation.5 | async-start | bytes 2211840 | tf_op jit(solution)/shard_map/all_gather | solution.py:213
  238.2 65.9 %all-gather.11.cloned.1.call-start = ((), (), s32[]{:S(2)}) async-start(), calls=%async_computation.6 | async-start | bytes 5308416 | tf_op jit(solution)/shard_map/all_gather | solution.py:214
  264.5 52.4 %all-gather.13.cloned.1.call-start = ((), (), s32[]{:S(2)}) async-start(), calls=%async_computation.7 | async-start | bytes 5308416 | tf_op jit(solution)/shard_map/all_gather | solution.py:215
  316.9 2.0 copy-start
  318.9 79.6 %copy-start.1 = (bf16[1152,1536]{1,0:T(8,128)(2,1)S(1)}, bf16[1152,1536]{1,0:T(8,128)(2,1)}, u32[]{:S(2)}) copy-start(bf16[1152,1536]{1,0:T(8,128)(2,1)} %all-gather.13.cloned.1.call-done) | copy-start | bytes 10616836
  398.2 42.1 %collective-permute-start.2 = (bf16[4,576,2048]{2,1,0:T(8,128)(2,1)}, bf16[4,576,2048]{2,1,0:T(8,128)(2,1)}, u32[]{:S(2)}, u32[]{:S(2)}) collective-permute-start(bf16[4,576,2048]{2,1,0:T(8,128)(2,1)} %get-tuple-element.73), channel_id=1, source_target_pairs={{0,1},{1,0},{2,3},{3,2},{4,5},{5,4},{6,7},{7,6}} | collective-permute-start | bytes 28311560 | tf_op jit(solution)/shard_map/ppermute | solution.py:168
  440.0 24.4 %collective-permute-start.1 = (bf16[2,576,2048]{2,1,0:T(8,128)(2,1)}, bf16[2,576,2048]{2,1,0:T(8,128)(2,1)}, u32[]{:S(2)}, u32[]{:S(2)}) collective-permute-start(bf16[2,576,2048]{2,1,0:T(8,128)(2,1)} %get-tuple-element.72), channel_id=1, source_target_pairs={{0,1},{1,0},{2,3},{3,2},{4,5},{5,4},{6,7},{7,6}} | collective-permute-start | bytes 14155784 | tf_op jit(solution)/shard_map/ppermute | solution.py:168
  464.2 23.7 %collective-permute-start.3 = (bf16[1,576,2048]{2,1,0:T(8,128)(2,1)}, bf16[1,576,2048]{2,1,0:T(8,128)(2,1)}, u32[]{:S(2)}, u32[]{:S(2)}) collective-permute-start(bf16[1,576,2048]{2,1,0:T(8,128)(2,1)} %get-tuple-element.77), channel_id=1, source_target_pairs={{0,1},{1,0},{2,3},{3,2},{4,5},{5,4},{6,7},{7,6}} | collective-permute-start | bytes 7077896 | tf_op jit(solution)/shard_map/ppermute | solution.py:168
  487.6 4.6 collective-permute-start.4
Sparse Core Ops, SparseCore 0:
  116.2 43.1 reduce-scatter.2
  163.0 41.3 reduce-scatter.4
  235.9 28.5 all-gather.6
  266.1 26.4 all-gather.8
  294.0 10.1 all-gather.10
  305.5 11.3 all-gather.12

commit v2 on v1

--- a/solution.py
+++ b/solution.py
@@ -13,24 +13,6 @@
 STEP_NUM = 10
 BIAS_ONE = 1.0 - BETA_ONE ** STEP_NUM
 BIAS_TWO = 1.0 - BETA_TWO ** STEP_NUM
-DOT_ROWS = (((0,), (0,)), ((), ()))
-DOT_COLS = (((1,), (1,)), ((), ()))
-
-
-def gelu_tanh(pre_act):
-    return jax.nn.gelu(pre_act, approximate=True)
-
-
-def stage_backward(stage_in, grad_in, w_up, w_down):
-    pre_act = jnp.dot(stage_in, w_up, preferred_element_type=jnp.float32)
-    hidden, gelu_pull = jax.vjp(gelu_tanh, pre_act)
-    hidden = hidden.astype(jnp.bfloat16)
-    dw_down = lax.dot_general(hidden, grad_in, DOT_ROWS, preferred_element_type=jnp.float32)
-    d_hidden = lax.dot_general(grad_in, w_down, DOT_COLS, preferred_element_type=jnp.float32)
-    d_pre = gelu_pull(d_hidden)[0].astype(jnp.bfloat16)
-    dw_up = lax.dot_general(stage_in, d_pre, DOT_ROWS, preferred_element_type=jnp.float32)
-    d_in = grad_in.astype(jnp.float32) + lax.dot_general(d_pre, w_up, DOT_COLS, preferred_element_type=jnp.float32)
-    return dw_up, dw_down, d_in.astype(jnp.bfloat16)
 
 
 def adamw_update(master, moment_one, moment_two, grad_step, learn_rate):
@@ -41,6 +23,8 @@
     return new_master, mom_one, mom_two
 
 
+MESH_ID = pl.DeviceIdType.MESH
+GRAD_TILE = 512
 GELU_LIN = 0.7978845608028654
 GELU_CUB = GELU_LIN * 0.044715
 ROW_TILE = 512
@@ -173,49 +157,290 @@
     return jnp.swapaxes(out, 1, 2)
 
 
+def gelu_pair(pre_act):
+    square = pre_act * pre_act
+    tanh_in = jnp.tanh(pre_act * (GELU_LIN + GELU_CUB * square))
+    half = 0.5 * pre_act
+    value = half + half * tanh_in
+    slope = 0.5 + 0.5 * tanh_in + half * (1.0 - tanh_in * tanh_in) * (GELU_LIN + 3.0 * GELU_CUB * square)
+    return value, slope
+
+
+def update_kernel(n_data, mst_up, mst_dn, mo1_up, mo2_up, mo1_dn, mo2_dn, cmp_up, cmp_dn, acc_up, acc_dn, acts_in, grad_in,
+                  rate_ref, norm_ref,
+                  new_up, new_dn, out1_up, out2_up, out1_dn, out2_dn, w_up_out, w_dn_out,
+                  wts, acts, acts_row, grad, grad_row, d_pre, sums, part, fwd_up, fwd_dn, last_up, last_dn,
+                  st_up, st_dn, norm_tiles, turned, send_sem, recv_sem, load_sem, store_sem):
+    chip = lax.axis_index('data')
+    core = lax.axis_index('stage')
+    peer = 1 - core
+    pos_x, pos_y = lax.rem(chip, 2), chip // 2
+    chip_x = pos_y * 2 + (1 - pos_x)
+    chip_y = (1 - pos_y) * 2 + pos_x
+    chip_d = 3 - chip
+    me = chip * 2 + core
+    n_dev = 2 * n_data
+    half_rows = grad.shape[1]
+    ff_width = wts.shape[3]
+    up_rows = st_up.shape[1]
+    dn_cols = st_dn.shape[2]
+    n_tile = ff_width // GRAD_TILE
+
+    def cols_of(index, size):
+        return pl.ds(pl.multiple_of(index * size, size), size)
+
+    def rows_of(index):
+        return pl.ds(pl.multiple_of(index * up_rows, 8), up_rows)
+
+    def remote(src, dst, index, device):
+        return pltpu.make_async_remote_copy(src_ref=src, dst_ref=dst, send_sem=send_sem.at[index], recv_sem=recv_sem.at[index],
+                                            device_id=device, device_id_type=MESH_ID)
+
+    to_peer, to_x, to_y = (chip, peer), (chip_x, core), (chip_y, core)
+
+    barrier = pltpu.get_barrier_semaphore()
+    for offset in range(1, n_dev):
+        other = lax.rem(me + offset, n_dev)
+        pl.semaphore_signal(barrier, inc=1, device_id=(other // 2, lax.rem(other, 2)), device_id_type=MESH_ID)
+    pl.semaphore_wait(barrier, n_dev - 1)
+
+    swap_in = [remote(acts_in.at[:, cols_of(peer, half_rows)], acts.at[core], 0, to_peer),
+               remote(cmp_up, wts.at[core, 0], 1, to_peer),
+               remote(cmp_dn, wts.at[core, 1], 2, to_peer)]
+    for copy in swap_in:
+        copy.start()
+    loads = [pltpu.make_async_copy(src, dst, load_sem.at[index]) for index, (src, dst) in enumerate([
+        (grad_in.at[:, cols_of(core, half_rows)], grad), (acts_in.at[:, cols_of(core, half_rows)], acts.at[core]),
+        (cmp_up, wts.at[core, 0]), (cmp_dn, wts.at[core, 1]),
+        (acc_up, sums.at[core, 0]), (acc_dn, sums.at[core, 1]),
+        (mst_up, st_up.at[0]), (mo1_up, st_up.at[1]), (mo2_up, st_up.at[2]),
+        (mst_dn, st_dn.at[0]), (mo1_dn, st_dn.at[1]), (mo2_dn, st_dn.at[2])])]
+    for copy in loads:
+        copy.start()
+
+    def part_copy(kind, tile):
+        cols = cols_of(tile, GRAD_TILE)
+        return remote(sums.at[peer, kind, :, cols], part.at[kind, :, cols], 3 + kind * n_tile + tile, to_peer)
+
+    up_first = [remote(sums.at[core, 0, rows_of(row * 2 + 1 - pos_x)], fwd_up.at[slot], 9 + slot, to_x)
+                for slot, row in enumerate((1 - pos_y, pos_y))]
+    dn_first = [remote(sums.at[core, 1, :, cols_of((1 - pos_y) * 2 + col, dn_cols)], fwd_dn.at[slot], 12 + slot, to_y)
+                for slot, col in enumerate((1 - pos_x, pos_x))]
+    up_next = remote(sums.at[core, 0, rows_of(chip_y)], last_up, 11, to_y)
+    dn_next = remote(sums.at[core, 1, :, cols_of(chip_x, dn_cols)], last_dn, 14, to_x)
+
+    def add_up(index):
+        sums[core, 0, rows_of(index)] += part[0, rows_of(index)]
+
+    def add_dn(index):
+        cols = cols_of(index, dn_cols)
+        sums[core, 1, :, cols] += part[1, :, cols]
+
+    def begin_scatter():
+        for kind in range(2):
+            for tile in range(n_tile):
+                part_copy(kind, tile).wait_recv()
+        for slot in range(2):
+            add_up((1 - pos_y if slot == 0 else pos_y) * 2 + 1 - pos_x)
+            up_first[slot].start()
+            add_dn((1 - pos_y) * 2 + (1 - pos_x if slot == 0 else pos_x))
+            dn_first[slot].start()
+        add_up(chip_y)
+        add_dn(chip_x)
+        add_up(chip)
+        add_dn(chip)
+
+    loads[0].wait()
+    for block in (1, 0):
+        own = core == block
+
+        @pl.when(own)
+        def _():
+            for copy in loads[1:6]:
+                copy.wait()
+
+        @pl.when(jnp.logical_not(own))
+        def _():
+            for copy in swap_in:
+                copy.wait_recv()
+
+        acts_row[...] = acts[block].T
+        grad_row[...] = grad[...].T
+
+        def tile_step(tile, carry, block=block, own=own):
+            cols = cols_of(tile, GRAD_TILE)
+            pre_act = jnp.dot(acts_row[...], wts[block, 0, :, cols], preferred_element_type=jnp.float32)
+            hidden, slope = gelu_pair(pre_act)
+            dw_down = jnp.dot(grad[...], hidden.astype(jnp.bfloat16), preferred_element_type=jnp.float32)
+            d_hidden = jnp.dot(grad_row[...], wts[block, 1, :, cols], preferred_element_type=jnp.float32)
+            d_pre[:, cols] = (d_hidden * slope).astype(jnp.bfloat16)
+            dw_up = jnp.dot(acts[block], d_pre[:, cols], preferred_element_type=jnp.float32)
+
+            @pl.when(own)
+            def _():
+                sums[block, 0, :, cols] += dw_up
+                sums[block, 1, :, cols] += dw_down
+
+            @pl.when(jnp.logical_not(own))
+            def _():
+                sums[block, 0, :, cols] = dw_up
+                sums[block, 1, :, cols] = dw_down
+                part_copy(0, tile).start()
+                part_copy(1, tile).start()
+            return carry
+
+        if block == 1:
+            lax.fori_loop(0, n_tile, tile_step, 0)
+            d_in = lax.dot_general(wts[1, 0], d_pre[...], (((1,), (1,)), ((), ())), preferred_element_type=jnp.float32)
+            grad[...] = (grad[...].astype(jnp.float32) + d_in).astype(jnp.bfloat16)
+        else:
+            lax.fori_loop(0, 1, tile_step, 0)
+            pl.when(core == 1)(begin_scatter)
+            lax.fori_loop(1, n_tile, tile_step, 0)
+    pl.when(core == 0)(begin_scatter)
+
+    up_first[0].wait_recv()
+    sums[core, 0, rows_of(chip_y)] += fwd_up[0]
+    up_next.start()
+    dn_first[0].wait_recv()
+    sums[core, 1, :, cols_of(chip_x, dn_cols)] += fwd_dn[0]
+    dn_next.start()
+    up_first[1].wait_recv()
+    dn_first[1].wait_recv()
+    up_next.wait_recv()
+    scale = 1.0 / n_data
+    mean_up = (sums[core, 0, rows_of(chip)] + fwd_up[1] + last_up[...]) * scale
+    last_up[...] = mean_up
+    square = jnp.sum((mean_up * mean_up).reshape(up_rows // 8, 8, ff_width), axis=0)
+    dn_next.wait_recv()
+    mean_dn = (sums[core, 1, :, cols_of(chip, dn_cols)] + fwd_dn[1] + last_dn[...]) * scale
+    last_dn[...] = mean_dn
+    square_dn = jnp.sum((mean_dn * mean_dn).reshape(st_dn.shape[1] // 8, 8, dn_cols), axis=0)
+    tile_sum = sum(square[:, first:first + 128] for first in range(0, ff_width, 128))
+    tile_sum = tile_sum + sum(square_dn[:, first:first + 128] for first in range(0, dn_cols, 128))
+    norm_tiles[me] = tile_sum
+    norm_copies = []
+    for offset in range(1, n_dev):
+        other = lax.rem(me + offset, n_dev)
+        norm_copies.append(remote(norm_tiles.at[me], norm_tiles.at[me], 14 + offset, (other // 2, lax.rem(other, 2))))
+    for copy in norm_copies:
+        copy.start()
+    for copy in loads[6:]:
+        copy.wait()
+    for copy in norm_copies:
+        copy.wait_recv()
+    total_sq = jnp.sum(jnp.sum(norm_tiles[...], axis=0), keepdims=True)
+    clip = jnp.minimum(1.0, norm_ref[0] / (jnp.sqrt(total_sq) + NORM_EPS))
+    rate = rate_ref[0]
+
+    own_up, own_dn = rows_of(chip), cols_of(chip, dn_cols)
+    state = adamw_update(st_up[0], st_up[1], st_up[2], clip * last_up[...], rate)
+    wts[core, 0, own_up] = state[0].astype(jnp.bfloat16)
+    for index in range(3):
+        st_up[index] = state[index]
+    up_at = [wts.at[core, 0, rows_of(index)] for index in (chip, chip_x, chip_y, chip_d)]
+    dn_at = [wts.at[core, 1, :, cols_of(index, dn_cols)] for index in (chip, chip_x, chip_y, chip_d)]
+    up_x, up_y, up_relay = remote(up_at[0], up_at[0], 22, to_x), remote(up_at[0], up_at[0], 24, to_y), remote(up_at[1], up_at[1], 26, to_y)
+    dn_x, dn_y, dn_relay = remote(dn_at[0], dn_at[0], 23, to_x), remote(dn_at[0], dn_at[0], 25, to_y), remote(dn_at[2], dn_at[2], 27, to_x)
+    up_peer = [remote(up_at[index], up_at[index], 28 + index, to_peer) for index in range(4)]
+    dn_peer = [remote(dn_at[index], dn_at[index], 32 + index, to_peer) for index in range(4)]
+    up_x.start()
+    up_y.start()
+    up_peer[0].start()
+    state = adamw_update(st_dn[0], st_dn[1], st_dn[2], clip * last_dn[...], rate)
+    wts[core, 1, :, own_dn] = state[0].astype(jnp.bfloat16)
+    for index in range(3):
+        st_dn[index] = state[index]
+    dn_y.start()
+    dn_x.start()
+    dn_peer[0].start()
+    stores = [pltpu.make_async_copy(src, dst, store_sem.at[index]) for index, (src, dst) in enumerate([
+        (st_up.at[0], new_up), (st_up.at[1], out1_up), (st_up.at[2], out2_up),
+        (st_dn.at[0], new_dn), (st_dn.at[1], out1_dn), (st_dn.at[2], out2_dn)])]
+    for copy in stores:
+        copy.start()
+    up_x.wait_recv()
+    up_relay.start()
+    up_peer[1].start()
+    dn_y.wait_recv()
+    dn_relay.start()
+    dn_peer[2].start()
+    up_y.wait_recv()
+    up_peer[2].start()
+    dn_x.wait_recv()
+    dn_peer[1].start()
+    up_relay.wait_recv()
+    up_peer[3].start()
+    dn_relay.wait_recv()
+    dn_peer[3].start()
+    for copy in up_peer + dn_peer:
+        copy.wait_recv()
+    finals = []
+    for block in range(2):
+        finals.append(pltpu.make_async_copy(wts.at[block, 1], w_dn_out.at[block], store_sem.at[6 + block]))
+        finals[-1].start()
+    for block in range(2):
+        if block:
+            finals[-1].wait()
+        turned[...] = wts[block, 0].T
+        finals.append(pltpu.make_async_copy(turned, w_up_out.at[block], store_sem.at[8 + block]))
+        finals[-1].start()
+    for copy in swap_in + up_first + dn_first + [up_next, dn_next] + norm_copies:
+        copy.wait_send()
+    for kind in range(2):
+        for tile in range(n_tile):
+            part_copy(kind, tile).wait_send()
+    for copy in [up_x, up_y, up_relay, dn_x, dn_y, dn_relay] + up_peer + dn_peer:
+        copy.wait_send()
+    for copy in stores + finals[:2] + finals[3:]:
+        copy.wait()
+
+
+def update_weights(n_data, arrays, learn_rate, max_norm):
+    width, ff_width = arrays[6].shape
+    half_rows = arrays[11].shape[1] // 2
+    up_rows, dn_cols = arrays[0].shape[0], arrays[1].shape[1]
+    f32, bf16 = jnp.float32, jnp.bfloat16
+    up_state, dn_state = jax.ShapeDtypeStruct((up_rows, ff_width), f32), jax.ShapeDtypeStruct((width, dn_cols), f32)
+    any_spec = pl.BlockSpec(memory_space=pl.ANY)
+    smem_spec = pl.BlockSpec(memory_space=pltpu.SMEM)
+
+    def body(*refs):
+        update_kernel(n_data, *refs)
+
+    return pl.pallas_call(
+        body,
+        in_specs=[any_spec] * 12 + [smem_spec] * 2,
+        out_specs=[any_spec] * 8,
+        out_shape=[up_state, dn_state, up_state, up_state, dn_state, dn_state,
+                   jax.ShapeDtypeStruct((2, ff_width, width), bf16), jax.ShapeDtypeStruct((2, width, ff_width), bf16)],
+        scratch_shapes=[
+            pltpu.VMEM((2, 2, width, ff_width), bf16), pltpu.VMEM((2, width, half_rows), bf16),
+            pltpu.VMEM((half_rows, width), bf16), pltpu.VMEM((width, half_rows), bf16), pltpu.VMEM((half_rows, width), bf16),
+            pltpu.VMEM((half_rows, ff_width), bf16), pltpu.VMEM((2, 2, width, ff_width), f32), pltpu.VMEM((2, width, ff_width), f32),
+            pltpu.VMEM((2, up_rows, ff_width), f32), pltpu.VMEM((2, width, dn_cols), f32),
+            pltpu.VMEM((up_rows, ff_width), f32), pltpu.VMEM((width, dn_cols), f32),
+            pltpu.VMEM((3, up_rows, ff_width), f32), pltpu.VMEM((3, width, dn_cols), f32), pltpu.VMEM((2 * n_data, 8, 128), f32),
+            pltpu.VMEM((ff_width, width), bf16),
+            pltpu.SemaphoreType.DMA((36,)), pltpu.SemaphoreType.DMA((36,)), pltpu.SemaphoreType.DMA((12,)),
+            pltpu.SemaphoreType.DMA((10,))],
+        compiler_params=pltpu.CompilerParams(collective_id=0, has_side_effects=True, vmem_limit_bytes=67000000),
+        cost_estimate=pl.CostEstimate(flops=20 * half_rows * width * ff_width, bytes_accessed=40000000, transcendentals=0),
+        name="update",
+    )(*arrays, learn_rate.reshape(1), max_norm.reshape(1))
+
+
 def solution(mesh):
-    n_stage = mesh.shape['stage']
     n_data = mesh.shape['data']
-    last_stage = n_stage - 1
-    back_perm = [(source, source - 1) for source in range(1, n_stage)]
-
-    def backward_stages(my_stage, stage_in, grad_last, w_up, w_down, acc_up, acc_down):
-        def run_stage(operands):
-            grad_in, sum_up, sum_down = operands
-            dw_up, dw_down, d_in = stage_backward(stage_in, grad_in, w_up, w_down)
-            return sum_up + dw_up, sum_down + dw_down, d_in
-
-        def pass_through(operands):
-            return operands[1], operands[2], operands[0]
-
-        grad_buf = grad_last
-        for step in range(n_stage):
-            acc_up, acc_down, d_in = lax.cond(my_stage == last_stage - step, run_stage, pass_through,
-                                              (grad_buf, acc_up, acc_down))
-            if step < last_stage:
-                grad_buf = lax.ppermute(d_in, 'stage', back_perm)
-        return acc_up, acc_down
 
     def step_body(master_up, master_down, moment1_up, moment2_up, moment1_down, moment2_down,
                   compute_up, compute_down, accum_up, accum_down, stage_acts, loss_grad, next_micro,
                   learn_rate, max_norm):
-        my_stage = lax.axis_index('stage')
-        sum_up, sum_down = backward_stages(my_stage, stage_acts[0], loss_grad, compute_up[0], compute_down[0],
-                                           accum_up[0, 0], accum_down[0, 0])
-        shard_up = lax.psum_scatter(sum_up, 'data', scatter_dimension=0, tiled=True) / n_data
-        shard_down = lax.psum_scatter(sum_down, 'data', scatter_dimension=0, tiled=True) / n_data
-        local_sq = jnp.sum(shard_up * shard_up) + jnp.sum(shard_down * shard_down)
-        total_sq = lax.psum(local_sq, ('stage', 'data'))
-        clip = jnp.minimum(1.0, max_norm / (jnp.sqrt(total_sq) + NORM_EPS))
-        new_up, mom1_up, mom2_up = adamw_update(master_up[0], moment1_up[0], moment2_up[0], clip * shard_up, learn_rate)
-        new_down, mom1_down, mom2_down = adamw_update(master_down[0], moment1_down[0], moment2_down[0], clip * shard_down, learn_rate)
-        full_up = lax.all_gather(new_up.astype(jnp.bfloat16), 'data', axis=0, tiled=True)
-        full_down = lax.all_gather(new_down.astype(jnp.bfloat16), 'data', axis=0, tiled=True)
-        both_up = lax.all_gather(full_up.T, 'stage')
-        both_down = lax.all_gather(full_down.T, 'stage')
-        last_acts = forward_all(next_micro, both_up, both_down)
-        return (new_up[None], new_down[None], mom1_up[None], mom2_up[None],
-                mom1_down[None], mom2_down[None], last_acts)
+        arrays = (master_up[0], master_down[0].T, moment1_up[0], moment2_up[0], moment1_down[0].T, moment2_down[0].T,
+                  compute_up[0], compute_down[0].T, accum_up[0, 0], accum_down[0, 0].T, stage_acts[0].T, loss_grad.T)
+        new_up, new_dn, out1_up, out2_up, out1_dn, out2_dn, w_up_t, w_dn_t = update_weights(n_data, arrays, learn_rate, max_norm)
+        last_acts = forward_all(next_micro, w_up_t, w_dn_t)
+        return (new_up[None], new_dn.T[None], out1_up[None], out2_up[None], out1_dn.T[None], out2_dn.T[None], last_acts)
 
     shard_spec = P('stage', 'data', None)
     whole_spec = P('stage', None, None)

time: 510 us -> 314 us (0.62); the launches traced: 501 us -> 314 us
  waiting for transfers between devices: 205 us -> 0.75 us
  Pallas kernels: 168 us -> 296 us
  matrix products: 44.4 us -> 0 us
  blocking collectives: 22.2 us -> 0 us
  local copies, waits for them, and re-layouts: 29.3 us -> 12.5 us
  between operations: 18.2 us -> 2 us
  other arithmetic: 10.7 us -> 0 us
    pallas_call x0 -> x1, Pallas kernels: none -> 128 us  [update_weights(): pl.pallas_call(body, in_specs=[any_spec] * 12 + [smem_spec] * 2, out_spec...]
    reduce_scatter x2 -> x0, waiting for transfers between devices: 83.7 us -> none  [the longest x1 43 us: step_body(): lax.psum_scatter(sum_down, 'data', scatter_dimension=0, tiled=True) / n_data]
    all_gather x4 -> x0, waiting for transfers between devices: 72.2 us -> none  [the longest x1 28.1 us: step_body(): lax.all_gather(new_down.astype(jnp.bfloat16), 'data', axis=0, tiled=True)]
    ppermute x1 -> x0, waiting for transfers between devices: 48.4 us -> none  [backward_stages(): grad_buf = lax.ppermute(d_in, 'stage', back_perm)]
    dot_general x3 -> x0, matrix products: 44.4 us -> none  [the longest x1 26.1 us: stage_backward(): lax.dot_general(stage_in, d_pre, DOT_ROWS, preferred_element_type=jnp.flo...]
    psum x1 -> x0, blocking collectives: 22.2 us -> none  [step_body(): total_sq = lax.psum(local_sq, ('stage', 'data'))]
    unnamed x22, local copies, waits for them, and re-layouts: 18.1 us -> 7.49 us
    convert_element_type x2 -> x0, other arithmetic: 6.65 us -> none  [the longest x1 4.3 us: step_body(): new_up.astype(jnp.bfloat16)]
  transfers between devices with their start and end apart: 11 -> 4, of which waited for: 8 -> 1; matrix products, arithmetic and copies ran while one was open for 3% -> 1% of each run, Pallas kernels for 18% -> 28%
where the time goes in v2:
time: 314 us
  Pallas kernels  296 us (94%)
  local copies, waits for them, and re-layouts  12.5 us (4%)
    pallas_call x4, Pallas kernels, forward_chunk(): pl.pallas_call(body, grid_spec=pltpu.PrefetchScalarGridSpec(num_scalar_pr...  168 us
    pallas_call x1, Pallas kernels, update_weights(): pl.pallas_call(body, in_specs=[any_spec] * 12 + [smem_spec] * 2, out_spec...  128 us
    unnamed x22, local copies, waits for them, and re-layouts  7.49 us
  transfers between devices with their start and end apart: 4, of which 1 were waited for; matrix products, arithmetic and copies ran while one was open for 1% of the time, Pallas kernels for 28%

profile of v2, /device:TPU:0, one launch (start us, length us, event | category | flops | bytes accessed | tf_op | source)
XLA Modules:
  0.0 313.8 jit_solution(8177753208489006087)
XLA Ops:
  1.9 128.3 %update.1 = (f32[144,1536]{1,0:T(8,128)}, f32[576,384]{1,0:T(8,128)}, f32[144,1536]{1,0:T(8,128)}, f32[144,1536]{1,0:T(8,128)}, f32[576,384]{1,0:T(8,128)}, /*in...) custom-call(f32[144,1536]{1,0:T(8,128)} %bitcast.63, f32[576,384]{1,0:T(8,128)} %bitcast.64, ...), custom_call_target="tpu_custom_call" | custom-call | flops 18119393280 | bytes 40000000 | tf_op jit(solution)/shard_map/update/pallas_call | solution.py:411
  130.3 0.0 copy-start
  130.3 2.0 copy-done
  132.3 0.0 copy-start.1
  132.3 79.3 %fwd_0.1 = (bf16[16,576,2048]{2,1,0:T(8,128)(2,1)}, bf16[4,576,2048]{2,1,0:T(8,128)(2,1)}) custom-call(s32[1]{0:T(128)} %bitcast.32.first, bf16[16,576,2048]{2,1,0:T(8,128)(2,1)} %bitcast.46, bf16[2,1536,576]{2,1,0:T(8,128)(2,1)} %get-tuple-element.29.refs_1_, bf16[2,576,1536]{2,1,0:T(8,128)(2,1)S(1)} %copy-done), custom_call_target="tpu_custom_call" | custom-call | flops 57982058496 | bytes 18874368 | tf_op jit(solution)/shard_map/fwd_0/pallas_call | solution.py:122
  211.6 1.6 collective-permute-start.1
  213.3 0.0 copy-done.1
  213.3 41.6 %fwd_4.1 = (bf16[16,576,2048]{2,1,0:T(8,128)(2,1)}, bf16[2,576,2048]{2,1,0:T(8,128)(2,1)}) custom-call(s32[1]{0:T(128)} %bitcast.31.first, bf16[16,576,2048]{2,1,0:T(8,128)(2,1)} %bitcast.47, bf16[2,1536,576]{2,1,0:T(8,128)(2,1)} %get-tuple-element.29.refs_1_, bf16[2,576,1536]{2,1,0:T(8,128)(2,1)S(1)} %copy-done.1, ...), custom_call_target="tpu_custom_call", output_to_operand_aliasing={{0}: (4, {})} | custom-call | flops 28991029248 | bytes 9437184 | tf_op jit(solution)/shard_map/fwd_4/pallas_call | solution.py:122
  254.9 0.1 collective-permute-start
  254.9 0.0 collective-permute-done.1.refs_3_
  254.9 23.5 %fwd_6.1 = (bf16[16,576,2048]{2,1,0:T(8,128)(2,1)}, bf16[1,576,2048]{2,1,0:T(8,128)(2,1)}) custom-call(s32[1]{0:T(128)} %bitcast.33.first, bf16[16,576,2048]{2,1,0:T(8,128)(2,1)} %bitcast.48, bf16[2,1536,576]{2,1,0:T(8,128)(2,1)} %get-tuple-element.29.refs_1_, bf16[2,576,1536]{2,1,0:T(8,128)(2,1)S(1)} %copy-done.1, ...), custom_call_target="tpu_custom_call", output_to_operand_aliasing={{0}: (5, {})} | custom-call | flops 14495514624 | bytes 4718592 | tf_op jit(solution)/shard_map/fwd_6/pallas_call | solution.py:122
  278.5 0.5 collective-permute-start.2
  278.9 0.0 collective-permute-done.refs_3_
  278.9 23.2 %fwd_7.1 = (bf16[16,576,2048]{2,1,0:T(8,128)(2,1)}, bf16[1,576,2048]{2,1,0:T(8,128)(2,1)}) custom-call(s32[1]{0:T(128)} %bitcast.29.first, bf16[16,576,2048]{2,1,0:T(8,128)(2,1)} %bitcast.49, bf16[2,1536,576]{2,1,0:T(8,128)(2,1)} %get-tuple-element.29.refs_1_, bf16[2,576,1536]{2,1,0:T(8,128)(2,1)S(1)} %copy-done.1, ...), custom_call_target="tpu_custom_call", output_to_operand_aliasing={{0}: (5, {})} | custom-call | flops 14495514624 | bytes 4718592 | tf_op jit(solution)/shard_map/fwd_7/pallas_call | solution.py:122
  302.2 0.3 collective-permute-start.3
  302.5 0.0 collective-permute-done.2
  302.5 0.0 copy-start.7
  302.5 0.0 copy-start.6
  302.5 3.5 %constant_dynamic-update-slice_fusion.1 = bf16[16,576,2048]{2,1,0:T(8,128)(2,1)} fusion(bf16[16,576,2048]{2,1,0:T(8,128)(2,1)} %get-tuple-element.36, bf16[1,576,2048]{2,1,0:T(8,128)(2,1)} %collective-permute-done.2, s32[]{:T(128)S(6)} %select_n.6), kind=kLoop, calls=%fused_computation.1 | loop fusion | bytes 4718596 | tf_op jit(solution)/shard_map/dynamic_update_slice | solution.py:156
  306.0 0.0 copy-start.5
  306.0 0.0 copy-start.4
  306.0 0.7 collective-permute-done.3
  306.7 1.6 constant_dynamic-update-slice_fusion
  308.3 0.0 copy-start.3
  308.3 0.0 copy-start.2
  308.3 0.0 copy-done.7
  308.3 0.9 copy.38
  309.2 0.0 copy-done.6
  309.2 0.9 copy.39
  310.1 0.0 copy-done.5
  310.1 0.9 copy.40
  311.0 0.0 copy-done.4
  311.0 0.9 copy.41
  311.9 0.0 copy-done.3
  311.9 0.9 copy.42
  312.9 0.0 copy-done.2
  312.9 0.9 copy.43
Async XLA Ops:
  130.3 2.0 copy-start
  132.3 81.0 %copy-start.1 = (bf16[2,576,1536]{2,1,0:T(8,128)(2,1)S(1)}, bf16[2,576,1536]{2,1,0:T(8,128)(2,1)}, u32[]{:S(2)}) copy-start(bf16[2,576,1536]{2,1,0:T(8,128)(2,1)} %get-tuple-element.30.refs_2_) | copy-start | bytes 10616836
  211.6 43.3 %collective-permute-start.1 = (bf16[4,576,2048]{2,1,0:T(8,128)(2,1)}, bf16[4,576,2048]{2,1,0:T(8,128)(2,1)}, u32[]{:S(2)}, u32[]{:S(2)}) collective-permute-start(bf16[4,576,2048]{2,1,0:T(8,128)(2,1)} %get-tuple-element.33), channel_id=1, source_target_pairs={{0,1},{1,0},{2,3},{3,2},{4,5},{5,4},{6,7},{7,6}} | collective-permute-start | bytes 28311560 | tf_op jit(solution)/shard_map/ppermute | solution.py:152
  254.9 24.1 %collective-permute-start = (bf16[2,576,2048]{2,1,0:T(8,128)(2,1)}, bf16[2,576,2048]{2,1,0:T(8,128)(2,1)}, u32[]{:S(2)}, u32[]{:S(2)}) collective-permute-start(bf16[2,576,2048]{2,1,0:T(8,128)(2,1)} %get-tuple-element.32), channel_id=1, source_target_pairs={{0,1},{1,0},{2,3},{3,2},{4,5},{5,4},{6,7},{7,6}} | collective-permute-start | bytes 14155784 | tf_op jit(solution)/shard_map/ppermute | solution.py:152
  278.5 24.0 %collective-permute-start.2 = (bf16[1,576,2048]{2,1,0:T(8,128)(2,1)}, bf16[1,576,2048]{2,1,0:T(8,128)(2,1)}, u32[]{:S(2)}, u32[]{:S(2)}) collective-permute-start(bf16[1,576,2048]{2,1,0:T(8,128)(2,1)} %get-tuple-element.37), channel_id=1, source_target_pairs={{0,1},{1,0},{2,3},{3,2},{4,5},{5,4},{6,7},{7,6}} | collective-permute-start | bytes 7077896 | tf_op jit(solution)/shard_map/ppermute | solution.py:152
  302.2 4.6 %collective-permute-start.3 = (bf16[1,576,2048]{2,1,0:T(8,128)(2,1)}, bf16[1,576,2048]{2,1,0:T(8,128)(2,1)S(1)}, u32[]{:S(2)}, u32[]{:S(2)}) collective-permute-start(bf16[1,576,2048]{2,1,0:T(8,128)(2,1)} %get-tuple-element.38), channel_id=1, source_target_pairs={{0,1},{1,0},{2,3},{3,2},{4,5},{5,4},{6,7},{7,6}} | collective-permute-start | bytes 7077896 | tf_op jit(solution)/shard_map/ppermute | solution.py:152
  302.5 5.8 %copy-start.7 = (f32[144,1536]{1,0:T(8,128)S(1)}, f32[144,1536]{1,0:T(8,128)}, u32[]{:S(2)}) copy-start(f32[144,1536]{1,0:T(8,128)} %get-tuple-element.23) | copy-start | bytes 2654212
  302.5 6.7 %copy-start.6 = (f32[576,384]{1,0:T(8,128)S(1)}, f32[576,384]{1,0:T(8,128)}, u32[]{:S(2)}) copy-start(f32[576,384]{1,0:T(8,128)} %get-tuple-element.24) | copy-start | bytes 2654212
  306.0 4.2 %copy-start.5 = (f32[144,1536]{1,0:T(8,128)S(1)}, f32[144,1536]{1,0:T(8,128)}, u32[]{:S(2)}) copy-start(f32[144,1536]{1,0:T(8,128)} %get-tuple-element.25) | copy-start | bytes 2654212
  306.0 5.1 %copy-start.4 = (f32[144,1536]{1,0:T(8,128)S(1)}, f32[144,1536]{1,0:T(8,128)}, u32[]{:S(2)}) copy-start(f32[144,1536]{1,0:T(8,128)} %get-tuple-element.26) | copy-start | bytes 2654212
  308.3 3.7 %copy-start.3 = (f32[576,384]{1,0:T(8,128)S(1)}, f32[576,384]{1,0:T(8,128)}, u32[]{:S(2)}) copy-start(f32[576,384]{1,0:T(8,128)} %get-tuple-element.27) | copy-start | bytes 2654212
  308.3 4.6 %copy-start.2 = (f32[576,384]{1,0:T(8,128)S(1)}, f32[576,384]{1,0:T(8,128)}, u32[]{:S(2)}) copy-start(f32[576,384]{1,0:T(8,128)} %get-tuple-element.28) | copy-start | bytes 2654212

commit v3 on v2

v3 whole, which is shorter than its diff:
```python
import jax
import jax.numpy as jnp
from jax import lax
from jax.experimental import pallas as pl
from jax.experimental.pallas import tpu as pltpu
from jax.sharding import PartitionSpec as P

BETA_ONE = 0.9
BETA_TWO = 0.95
ADAM_EPS = 1e-8
WEIGHT_DECAY = 0.1
NORM_EPS = 1e-6
STEP_NUM = 10
BIAS_ONE = 1.0 - BETA_ONE ** STEP_NUM
BIAS_TWO = 1.0 - BETA_TWO ** STEP_NUM


def adamw_update(master, moment_one, moment_two, grad_step, learn_rate):
    mom_one = BETA_ONE * moment_one + (1.0 - BETA_ONE) * grad_step
    mom_two = BETA_TWO * moment_two + (1.0 - BETA_TWO) * grad_step * grad_step
    step_dir = (mom_one / BIAS_ONE) / (jnp.sqrt(mom_two / BIAS_TWO) + ADAM_EPS)
    new_master = master - learn_rate * (step_dir + WEIGHT_DECAY * master)
    return new_master, mom_one, mom_two


MESH_ID = pl.DeviceIdType.MESH
GRAD_HALF = 768
GRAD_TILE = 256
GELU_LIN = 0.7978845608028654
GELU_CUB = GELU_LIN * 0.044715
ROW_TILE = 512
FF_TILE = 512
CHUNKS = (4, 1, 1)
N_FIRST = 2


def gelu_half(pre_act):
    inner = pre_act * (GELU_LIN + GELU_CUB * (pre_act * pre_act))
    half = 0.5 * pre_act
    return half + half * jnp.tanh(inner)


def block_forward(cols_in, w_up_t, w_down_t, block, hidden_ref):
    ff_width = w_up_t.shape[1]
    for start in range(0, ff_width, FF_TILE):
        pre_act = jnp.dot(w_up_t[block, start:start + FF_TILE, :], cols_in, preferred_element_type=jnp.float32)
        hidden_ref[start:start + FF_TILE, :] = gelu_half(pre_act).astype(jnp.bfloat16)
    branch = jnp.dot(w_down_t[block], hidden_ref[...], preferred_element_type=jnp.float32)
    return (cols_in.astype(jnp.float32) + branch).astype(jnp.bfloat16)


def forward_kernel(has_prev, copies, n_state, base, n_own, n_tiles, *refs):
    refs = list(refs)
    x_ref, w_up_t, w_down_t = refs[:3]
    refs = refs[3:]
    n_copy = len(copies)
    copy_refs, refs = refs[:n_copy], refs[n_copy:]
    state_in, refs = refs[:n_state], refs[n_state:]
    if has_prev:
        refs.pop(0)
    out_ref, y_ref = refs[:2]
    state_out, refs = refs[2:2 + n_state], refs[2 + n_state:]
    hidden_ref, y_buf, y_sem, copy_sem, state_sem = refs[:5]
    state_buf = refs[5:]
    mine = lax.axis_index('stage')
    micro, tile = pl.program_id(0), pl.program_id(1)
    step = micro * n_tiles + tile
    n_steps = pl.num_programs(0) * n_tiles
    slot = lax.rem(step, 2)
    tile_cols = pl.ds(pl.multiple_of(tile * ROW_TILE, ROW_TILE), ROW_TILE)

    def y_copy(which):
        return pltpu.make_async_copy(y_buf.at[which], out_ref.at[mine * n_own + base + micro, :, tile_cols], y_sem.at[which])

    def tile_copy(index):
        from_peer, first, count = copies[index]
        owner = 1 - mine if from_peer else mine
        return pltpu.make_async_copy(copy_refs[index], out_ref.at[pl.ds(owner * n_own + first, count), :, tile_cols], copy_sem.at[index])

    def state_copy(index, leaving):
        src, dst = (state_buf[index], state_out[index]) if leaving else (state_in[index], state_buf[index])
        return pltpu.make_async_copy(src, dst, state_sem.at[index])

    if n_copy:
        @pl.when(micro == 0)
        def _():
            for index in range(n_copy):
                tile_copy(index).start()

    if n_state:
        @pl.when(step == 0)
        def _():
            for index in range(n_state):
                state_copy(index, False).start()

        @pl.when(step == 1)
        def _():
            for index in range(n_state):
                state_copy(index, False).wait()
                state_copy(index, True).start()

    cols = x_ref[0]
    for block in range(2):
        cols = block_forward(cols, w_up_t, w_down_t, block, hidden_ref)

    @pl.when(step >= 2)
    def _():
        y_copy(slot).wait()

    y_buf[slot] = cols
    y_ref[0] = cols
    y_copy(slot).start()
    if n_copy:
        @pl.when(micro == 0)
        def _():
            for index in range(n_copy):
                tile_copy(index).wait()

    @pl.when(step == n_steps - 1)
    def _():
        y_copy(slot).wait()
        y_copy(1 - slot).wait()
        for index in range(n_state):
            state_copy(index, True).wait()


def forward_chunk(base, n_chunk, micro_t, w_up_t, w_down_t, prev_out, copied, states):
    n_micro, width, n_rows = micro_t.shape
    n_own = n_micro // 2
    n_tiles = n_rows // ROW_TILE
    ff_width = w_up_t.shape[1]
    mine = lax.axis_index('stage')
    any_spec = pl.BlockSpec(memory_space=pl.ANY)
    scalar = jnp.full((1,), mine * n_own + base, jnp.int32)
    in_specs = [pl.BlockSpec((1, width, ROW_TILE), lambda i, j, first: (first[0] + i, 0, j)),
                pl.BlockSpec((2, ff_width, width), lambda i, j, first: (0, 0, 0)),
                pl.BlockSpec((2, width, ff_width), lambda i, j, first: (0, 0, 0))]
    operands = [micro_t, w_up_t, w_down_t]
    for array, _, _ in copied:
        in_specs.append(pl.BlockSpec((array.shape[0], width, ROW_TILE), lambda i, j, first: (0, 0, jnp.where(i == 0, j, n_tiles - 1))))
        operands.append(array)
    for array in states:
        in_specs.append(any_spec)
        operands.append(array)
    aliases = {}
    if prev_out is not None:
        in_specs.append(any_spec)
        operands.append(prev_out)
        aliases = {len(operands): 0}
    copies = [(from_peer, first, array.shape[0]) for array, from_peer, first in copied]

    def body(first, *refs):
        forward_kernel(prev_out is not None, copies, len(states), base, n_own, n_tiles, *refs)

    flops = 8 * n_chunk * n_rows * width * ff_width
    return pl.pallas_call(
        body,
        grid_spec=pltpu.PrefetchScalarGridSpec(
            num_scalar_prefetch=1, grid=(n_chunk, n_tiles), in_specs=in_specs,
            out_specs=[any_spec, pl.BlockSpec((1, width, ROW_TILE), lambda i, j, first: (i, 0, j))] + [any_spec] * len(states),
            scratch_shapes=[pltpu.VMEM((ff_width, ROW_TILE), jnp.bfloat16), pltpu.VMEM((2, width, ROW_TILE), jnp.bfloat16),
                            pltpu.SemaphoreType.DMA((2,)), pltpu.SemaphoreType.DMA((2,)), pltpu.SemaphoreType.DMA((6,))]
            + [pltpu.VMEM(array.shape, array.dtype) for array in states]),
        out_shape=[jax.ShapeDtypeStruct(micro_t.shape, jnp.bfloat16),
                   jax.ShapeDtypeStruct((n_chunk, width, n_rows), jnp.bfloat16)]
        + [jax.ShapeDtypeStruct(array.shape, array.dtype) for array in states],
        input_output_aliases=aliases,
        compiler_params=pltpu.CompilerParams(dimension_semantics=("arbitrary", "arbitrary"),
                                             vmem_limit_bytes=52 * 1024 * 1024),
        cost_estimate=pl.CostEstimate(flops=flops, bytes_accessed=4 * n_chunk * n_rows * width, transcendentals=0),
        name=f"fwd_{base}",
    )(scalar, *operands)


def forward_rest(micro_t, w_up_t, w_down_t, own_first, peer_first, states):
    n_own = micro_t.shape[0] // 2
    swap = [(0, 1), (1, 0)]
    mine = lax.axis_index('stage')
    out, base = None, own_first.shape[0]
    received, results = [], []
    for number, n_chunk in enumerate(CHUNKS):
        copied, passed = [], []
        if number == 0:
            copied, passed = [(own_first, False, 0), (peer_first, True, 0)], states
        elif number >= 2:
            copied = [received[number - 2]]
            received[number - 2] = None
        out, part, *handed = forward_chunk(base, n_chunk, micro_t, w_up_t, w_down_t, out, copied, passed)
        results += handed
        received.append((lax.ppermute(part, 'stage', swap), True, base))
        base += n_chunk
    for item in received:
        if item is not None:
            out = lax.dynamic_update_slice(out, item[0], ((1 - mine) * n_own + item[2], 0, 0))
    return jnp.swapaxes(out, 1, 2), results


def gelu_pair(pre_act):
    square = pre_act * pre_act
    tanh_in = jnp.tanh(pre_act * (GELU_LIN + GELU_CUB * square))
    half = 0.5 * pre_act
    value = half + half * tanh_in
    slope = 0.5 + 0.5 * tanh_in + half * (1.0 - tanh_in * tanh_in) * (GELU_LIN + 3.0 * GELU_CUB * square)
    return value, slope


def update_kernel(n_data, mst_up, mst_dn, mo1_up, mo2_up, mo1_dn, mo2_dn, cmp_up, cmp_dn, acc_up, acc_dn, acts_in, grad_in,
                  micro_in, rate_ref, norm_ref,
                  new_up, new_dn, out1_up, out2_up, out1_dn, out2_dn, w_up_out, w_dn_out, own_first, peer_first,
                  wts, acts, acts_row, grad, grad_row, d_pre, sums, part, fwd_up, fwd_dn, last_up, last_dn,
                  norm_tiles, turned, hidden_ref, send_sem, recv_sem, load_sem, store_sem, tile_sem):
    chip = lax.axis_index('data')
    core = lax.axis_index('stage')
    peer = 1 - core
    pos_x, pos_y = lax.rem(chip, 2), chip // 2
    chip_x = pos_y * 2 + (1 - pos_x)
    chip_y = (1 - pos_y) * 2 + pos_x
    chip_d = 3 - chip
    me = chip * 2 + core
    n_dev = 2 * n_data
    half_rows = grad.shape[1]
    width, ff_width = wts.shape[2:]
    up_rows, dn_cols = last_up.shape[0], last_dn.shape[1]
    n_own = micro_in.shape[0] // 2
    n_tiles = micro_in.shape[2] // ROW_TILE
    n_sub = GRAD_HALF // GRAD_TILE
    halves = (1 - pos_y, pos_y)

    def cols_of(index, size):
        return pl.ds(pl.multiple_of(index * size, size), size)

    def rows_of(index):
        return pl.ds(pl.multiple_of(index * up_rows, 8), up_rows)

    def remote(src, dst, index, device):
        return pltpu.make_async_remote_copy(src_ref=src, dst_ref=dst, send_sem=send_sem.at[index], recv_sem=recv_sem.at[index],
                                            device_id=device, device_id_type=MESH_ID)

    to_peer, to_x, to_y = (chip, peer), (chip_x, core), (chip_y, core)

    loads = [pltpu.make_async_copy(src, dst, load_sem.at[index]) for index, (src, dst) in enumerate([
        (grad_in.at[:, cols_of(core, half_rows)], grad), (acts_in.at[:, cols_of(core, half_rows)], acts.at[core]),
        (cmp_up, wts.at[core, 0]), (cmp_dn, wts.at[core, 1]),
        (acc_up, sums.at[core, 0]), (acc_dn, sums.at[core, 1]),
        (mst_up, part.at[0, 0:up_rows]), (mo1_up, part.at[0, up_rows:2 * up_rows]), (mo2_up, part.at[0, 2 * up_rows:3 * up_rows]),
        (mst_dn, part.at[1, :, 0:dn_cols]), (mo1_dn, part.at[1, :, dn_cols:2 * dn_cols]),
        (mo2_dn, part.at[1, :, 2 * dn_cols:3 * dn_cols])])]
    for copy in loads[:6]:
        copy.start()

    barrier = pltpu.get_barrier_semaphore()
    for offset in range(1, n_dev):
        other = lax.rem(me + offset, n_dev)
        pl.semaphore_signal(barrier, inc=1, device_id=(other // 2, lax.rem(other, 2)), device_id_type=MESH_ID)
    pl.semaphore_wait(barrier, n_dev - 1)

    swap_acts = remote(acts_in.at[:, cols_of(peer, half_rows)], acts.at[core], 0, to_peer)
    swap_wts = [[remote((cmp_up, cmp_dn)[kind].at[:, cols_of(half, GRAD_HALF)], wts.at[core, kind, :, cols_of(half, GRAD_HALF)],
                        1 + order * 2 + kind, to_peer) for kind in range(2)] for order, half in enumerate(halves)]
    swap_acts.start()
    for order in range(2):
        for kind in range(2):
            swap_wts[order][kind].start()

    def part_copy(kind, order, tile):
        cols = cols_of(halves[order] * n_sub + tile, GRAD_TILE)
        return remote(sums.at[peer, kind, :, cols], part.at[kind, :, cols], 5 + (kind * 2 + order) * n_sub + tile, to_peer)

    up_first = [[remote(sums.at[core, 0, rows_of(row * 2 + 1 - pos_x), cols_of(half, GRAD_HALF)],
                        fwd_up.at[slot, :, cols_of(half, GRAD_HALF)], 17 + order * 2 + slot, to_x)
                 for slot, row in enumerate(halves)] for order, half in enumerate(halves)]
    dn_first = [remote(sums.at[core, 1, :, cols_of((1 - pos_y) * 2 + col, dn_cols)], fwd_dn.at[slot], 21 + slot, to_y)
                for slot, col in enumerate((1 - pos_x, pos_x))]
    up_next = [remote(sums.at[core, 0, rows_of(chip_y), cols_of(half, GRAD_HALF)], last_up.at[:, cols_of(half, GRAD_HALF)],
                      23 + order, to_y) for order, half in enumerate(halves)]
    dn_next = remote(sums.at[core, 1, :, cols_of(chip_x, dn_cols)], last_dn, 25, to_x)

    def add_up(index, order):
        cols = cols_of(halves[order], GRAD_HALF)
        sums[core, 0, rows_of(index), cols] += part[0, rows_of(index), cols]

    def add_dn(index):
        cols = cols_of(index, dn_cols)
        sums[core, 1, :, cols] += part[1, :, cols]

    def scatter_half(order):
        for kind in range(2):
            for tile in range(n_sub):
                part_copy(kind, order, tile).wait_recv()
        for slot in range(2):
            add_up((halves[slot]) * 2 + 1 - pos_x, order)
            up_first[order][slot].start()
            if order == 0:
                add_dn((1 - pos_y) * 2 + (1 - pos_x if slot == 0 else pos_x))
                dn_first[slot].start()
        add_up(chip_y, order)
        if order == 1:
            add_dn(chip_x)
            add_dn(chip)
        add_up(chip, order)

    loads[0].wait()
    for block in (1, 0):
        own = core == block

        @pl.when(own)
        def _():
            for copy in loads[1:6]:
                copy.wait()

        @pl.when(jnp.logical_not(own))
        def _():
            swap_acts.wait_recv()

        acts_row[...] = acts[block].T
        grad_row[...] = grad[...].T
        for order in range(2):
            @pl.when(jnp.logical_not(own))
            def _(order=order):
                for copy in swap_wts[order]:
                    copy.wait_recv()

            def tile_step(tile, carry, block=block, own=own, order=order):
                cols = cols_of(halves[order] * n_sub + tile, GRAD_TILE)
                pre_act = jnp.dot(acts_row[...], wts[block, 0, :, cols], preferred_element_type=jnp.float32)
                d_hidden = jnp.dot(grad_row[...], wts[block, 1, :, cols], preferred_element_type=jnp.float32)
                hidden, slope = gelu_pair(pre_act)
                dw_down = jnp.dot(grad[...], hidden.astype(jnp.bfloat16), preferred_element_type=jnp.float32)
                d_tile = (d_hidden * slope).astype(jnp.bfloat16)
                if block == 1:
                    d_pre[:, cols] = d_tile
                dw_up = jnp.dot(acts[block], d_tile, preferred_element_type=jnp.float32)

                @pl.when(own)
                def _():
                    sums[block, 0, :, cols] += dw_up
                    sums[block, 1, :, cols] += dw_down

                @pl.when(jnp.logical_not(own))
                def _():
                    sums[block, 0, :, cols] = dw_up
                    sums[block, 1, :, cols] = dw_down
                    part_copy(0, order, tile).start()
                    part_copy(1, order, tile).start()
                return carry

            lax.fori_loop(0, n_sub, tile_step, 0)
            if block == 0 and order == 0:
                pl.when(core == 1)(lambda: scatter_half(1))
        if block == 1:
            d_in = lax.dot_general(wts[1, 0], d_pre[...], (((1,), (1,)), ((), ())), preferred_element_type=jnp.float32)
            grad[...] = (grad[...].astype(jnp.float32) + d_in).astype(jnp.bfloat16)
            pl.when(core == 1)(lambda: scatter_half(0))

    @pl.when(core == 0)
    def _():
        scatter_half(0)
        scatter_half(1)

    for copy in loads[6:]:
        copy.start()

    def x_slot(tile):
        slot = lax.rem(tile, 4)
        return acts.at[slot // 2, :, cols_of(lax.rem(slot, 2), ROW_TILE)]

    def x_load(tile):
        return pltpu.make_async_copy(micro_in.at[core * n_own + tile // n_tiles, :, cols_of(lax.rem(tile, n_tiles), ROW_TILE)],
                                     x_slot(tile), tile_sem.at[0, lax.rem(tile, 4)])

    for tile in range(4):
        x_load(tile).start()

    up_first[0][0].wait_recv()
    cols = cols_of(halves[0], GRAD_HALF)
    sums[core, 0, rows_of(chip_y), cols] += fwd_up[0, :, cols]
    up_next[0].start()
    dn_first[0].wait_recv()
    sums[core, 1, :, cols_of(chip_x, dn_cols)] += fwd_dn[0]
    dn_next.start()
    up_first[1][0].wait_recv()
    cols = cols_of(halves[1], GRAD_HALF)
    sums[core, 0, rows_of(chip_y), cols] += fwd_up[0, :, cols]
    up_next[1].start()
    for order in range(2):
        up_first[order][1].wait_recv()
        up_next[order].wait_recv()
    dn_first[1].wait_recv()
    scale = 1.0 / n_data
    mean_up = (sums[core, 0, rows_of(chip)] + fwd_up[1] + last_up[...]) * scale
    last_up[...] = mean_up
    square = jnp.sum((mean_up * mean_up).reshape(up_rows // 8, 8, ff_width), axis=0)
    dn_next.wait_recv()
    mean_dn = (sums[core, 1, :, cols_of(chip, dn_cols)] + fwd_dn[1] + last_dn[...]) * scale
    last_dn[...] = mean_dn
    square_dn = jnp.sum((mean_dn * mean_dn).reshape(width // 8, 8, dn_cols), axis=0)
    tile_sum = sum(square[:, first:first + 128] for first in range(0, ff_width, 128))
    tile_sum = tile_sum + sum(square_dn[:, first:first + 128] for first in range(0, dn_cols, 128))
    norm_tiles[me] = tile_sum
    norm_copies = []
    for offset in range(1, n_dev):
        other = lax.rem(me + offset, n_dev)
        norm_copies.append(remote(norm_tiles.at[me], norm_tiles.at[me], 25 + offset, (other // 2, lax.rem(other, 2))))
    for copy in norm_copies:
        copy.start()
    for copy in loads[6:]:
        copy.wait()
    for copy in norm_copies:
        copy.wait_recv()
    total_sq = jnp.sum(jnp.sum(norm_tiles[...], axis=0), keepdims=True)
    clip = jnp.minimum(1.0, norm_ref[0] / (jnp.sqrt(total_sq) + NORM_EPS))
    rate = rate_ref[0]

    chips = (chip, chip_x, chip_y, chip_d)
    up_at = [wts.at[core, 0, rows_of(index)] for index in chips]
    dn_at = [wts.at[core, 1, :, cols_of(index, dn_cols)] for index in chips]
    up_x, up_y, up_relay = remote(up_at[0], up_at[0], 33, to_x), remote(up_at[0], up_at[0], 34, to_y), remote(up_at[1], up_at[1], 35, to_y)
    dn_x, dn_y, dn_relay = remote(dn_at[0], dn_at[0], 36, to_x), remote(dn_at[0], dn_at[0], 37, to_y), remote(dn_at[2], dn_at[2], 38, to_x)
    up_peer = [remote(up_at[index], up_at[index], 39 + index, to_peer) for index in range(4)]
    dn_peer = [remote(dn_at[index], dn_at[index], 43 + index, to_peer) for index in range(4)]

    def gather_up():
        up_x.start()
        up_y.start()
        up_peer[0].start()

    def gather_dn():
        dn_y.start()
        dn_x.start()
        dn_peer[0].start()

    def gather_relay():
        up_x.wait_recv()
        up_relay.start()
        up_peer[1].start()
        dn_y.wait_recv()
        dn_relay.start()
        dn_peer[2].start()

    def gather_near():
        up_y.wait_recv()
        up_peer[2].start()
        dn_x.wait_recv()
        dn_peer[1].start()

    def gather_far():
        up_relay.wait_recv()
        up_peer[3].start()
        dn_relay.wait_recv()
        dn_peer[3].start()

    def gather_peer():
        for copy in up_peer + dn_peer:
            copy.wait_recv()

    state = adamw_update(part[0, 0:up_rows], part[0, up_rows:2 * up_rows], part[0, 2 * up_rows:3 * up_rows], clip * last_up[...], rate)
    wts[core, 0, rows_of(chip)] = state[0].astype(jnp.bfloat16)
    for index in range(3):
        part[0, index * up_rows:(index + 1) * up_rows] = state[index]
    pl.when(core == 0)(gather_up)
    state = adamw_update(part[1, :, 0:dn_cols], part[1, :, dn_cols:2 * dn_cols], part[1, :, 2 * dn_cols:3 * dn_cols], clip * last_dn[...], rate)
    wts[core, 1, :, cols_of(chip, dn_cols)] = state[0].astype(jnp.bfloat16)
    for index in range(3):
        part[1, :, index * dn_cols:(index + 1) * dn_cols] = state[index]
    pl.when(core == 0)(gather_dn)
    stores = [pltpu.make_async_copy(src, dst, store_sem.at[index]) for index, (src, dst) in enumerate([
        (part.at[0, 0:up_rows], new_up), (part.at[0, up_rows:2 * up_rows], out1_up), (part.at[0, 2 * up_rows:3 * up_rows], out2_up),
        (part.at[1, :, 0:dn_cols], new_dn), (part.at[1, :, dn_cols:2 * dn_cols], out1_dn),
        (part.at[1, :, 2 * dn_cols:3 * dn_cols], out2_dn)])]
    for copy in stores:
        copy.start()

    @pl.when(core == 0)
    def _():
        gather_relay()
        gather_near()
        gather_far()

    @pl.when(core == 1)
    def _():
        gather_peer()
        gather_up()
        gather_dn()

    swap_acts.wait_send()
    for order in range(2):
        for copy in swap_wts[order] + up_first[order] + [up_next[order]]:
            copy.wait_send()
        for kind in range(2):
            for tile in range(n_sub):
                part_copy(kind, order, tile).wait_send()
    for copy in dn_first + [dn_next] + norm_copies:
        copy.wait_send()

    def weights_out(block):
        return [pltpu.make_async_copy(turned, w_up_out.at[block], store_sem.at[6 + block]),
                pltpu.make_async_copy(wts.at[block, 1], w_dn_out.at[block], store_sem.at[8 + block])]

    def forward_tile(cols_in, block):
        for start in range(0, ff_width, FF_TILE):
            pre_act = jnp.dot(turned[start:start + FF_TILE, :], cols_in, preferred_element_type=jnp.float32)
            hidden_ref[start:start + FF_TILE, :] = gelu_half(pre_act).astype(jnp.bfloat16)
        branch = jnp.dot(wts[block, 1], hidden_ref[...], preferred_element_type=jnp.float32)
        return (cols_in.astype(jnp.float32) + branch).astype(jnp.bfloat16)

    n_first = own_first.shape[0] * n_tiles
    per_row = ff_width // ROW_TILE

    def mid_slot(tile):
        row = tile // per_row
        return row // 2, lax.rem(row, 2), slice(None), cols_of(lax.rem(tile, per_row), ROW_TILE)

    turned[...] = wts[0, 0].T
    for copy in weights_out(0):
        copy.start()

    def first_block(tile, carry):
        @pl.when(jnp.logical_and(core == 1, tile == 3))
        def _():
            gather_relay()

        @pl.when(jnp.logical_and(core == 1, tile == 5))
        def _():
            gather_near()

        @pl.when(jnp.logical_and(core == 1, tile == 7))
        def _():
            gather_far()

        x_load(tile).wait()
        slot = lax.rem(tile, 4)
        mid = forward_tile(acts[slot // 2, :, cols_of(lax.rem(slot, 2), ROW_TILE)], 0)
        sums[mid_slot(tile)] = mid.astype(jnp.float32)

        @pl.when(tile + 4 < n_first)
        def _():
            x_load(tile + 4).start()
        return carry

    lax.fori_loop(0, n_first, first_block, 0)
    pl.when(core == 0)(gather_peer)
    weights_out(0)[0].wait()
    turned[...] = wts[1, 0].T
    for copy in weights_out(1):
        copy.start()

    def y_slot(tile):
        return grad.at[:, cols_of(lax.rem(tile, 2), ROW_TILE)]

    def y_out(tile):
        place = (tile // n_tiles, slice(None), cols_of(lax.rem(tile, n_tiles), ROW_TILE))
        keep = pltpu.make_async_copy(y_slot(tile), own_first.at[place], tile_sem.at[1, lax.rem(tile, 2)])
        give = pltpu.make_async_remote_copy(src_ref=y_slot(tile), dst_ref=peer_first.at[place], send_sem=tile_sem.at[2, lax.rem(tile, 2)],
                                            recv_sem=recv_sem.at[47 + tile], device_id=to_peer, device_id_type=MESH_ID)
        return keep, give

    def second_block(tile, carry):
        result = forward_tile(sums[mid_slot(tile)].astype(jnp.bfloat16), 1)

        @pl.when(tile >= 2)
        def _():
            keep, give = y_out(tile - 2)
            keep.wait()
            give.wait_send()

        grad[:, cols_of(lax.rem(tile, 2), ROW_TILE)] = result
        for copy in y_out(tile):
            copy.start()
        return carry

    lax.fori_loop(0, n_first, second_block, 0)
    for tile in range(n_first - 2, n_first):
        keep, give = y_out(tile)
        keep.wait()
        give.wait_send()
    for tile in range(n_first):
        y_out(tile)[1].wait_recv()

    for copy in [up_x, up_y, up_relay, dn_x, dn_y, dn_relay] + up_peer + dn_peer:
        copy.wait_send()
    for copy in stores + weights_out(0)[1:] + weights_out(1):
        copy.wait()


def update_weights(n_data, arrays, learn_rate, max_norm):
    width, ff_width = arrays[6].shape
    n_rows = arrays[11].shape[1]
    half_rows = n_rows // 2
    up_rows, dn_cols = arrays[0].shape[0], arrays[1].shape[1]
    f32, bf16 = jnp.float32, jnp.bfloat16
    up_state, dn_state = jax.ShapeDtypeStruct((up_rows, ff_width), f32), jax.ShapeDtypeStruct((width, dn_cols), f32)
    first = jax.ShapeDtypeStruct((N_FIRST, width, n_rows), bf16)
    any_spec = pl.BlockSpec(memory_space=pl.ANY)
    smem_spec = pl.BlockSpec(memory_space=pltpu.SMEM)
    n_sem = 47 + N_FIRST * n_rows // ROW_TILE

    def body(*refs):
        update_kernel(n_data, *refs)

    flops = 20 * half_rows * width * ff_width + 8 * N_FIRST * n_rows * width * ff_width
    return pl.pallas_call(
        body,
        in_specs=[any_spec] * 13 + [smem_spec] * 2,
        out_specs=[any_spec] * 10,
        out_shape=[up_state, dn_state, up_state, up_state, dn_state, dn_state,
                   jax.ShapeDtypeStruct((2, ff_width, width), bf16), jax.ShapeDtypeStruct((2, width, ff_width), bf16), first, first],
        scratch_shapes=[
            pltpu.VMEM((2, 2, width, ff_width), bf16), pltpu.VMEM((2, width, half_rows), bf16),
            pltpu.VMEM((half_rows, width), bf16), pltpu.VMEM((width, half_rows), bf16), pltpu.VMEM((half_rows, width), bf16),
            pltpu.VMEM((half_rows, ff_width), bf16), pltpu.VMEM((2, 2, width, ff_width), f32), pltpu.VMEM((2, width, ff_width), f32),
            pltpu.VMEM((2, up_rows, ff_width), f32), pltpu.VMEM((2, width, dn_cols), f32),
            pltpu.VMEM((up_rows, ff_width), f32), pltpu.VMEM((width, dn_cols), f32), pltpu.VMEM((2 * n_data, 8, 128), f32),
            pltpu.VMEM((ff_width, width), bf16), pltpu.VMEM((ff_width, ROW_TILE), bf16),
            pltpu.SemaphoreType.DMA((n_sem,)), pltpu.SemaphoreType.DMA((n_sem,)), pltpu.SemaphoreType.DMA((12,)),
            pltpu.SemaphoreType.DMA((10,)), pltpu.SemaphoreType.DMA((3, 4))],
        compiler_params=pltpu.CompilerParams(collective_id=0, has_side_effects=True, vmem_limit_bytes=67000000),
        cost_estimate=pl.CostEstimate(flops=flops, bytes_accessed=60000000, transcendentals=0),
        name="update",
    )(*arrays, learn_rate.reshape(1), max_norm.reshape(1))


def solution(mesh):
    n_data = mesh.shape['data']

    def step_body(master_up, master_down, moment1_up, moment2_up, moment1_down, moment2_down,
                  compute_up, compute_down, accum_up, accum_down, stage_acts, loss_grad, next_micro,
                  learn_rate, max_norm):
        arrays = (master_up[0], master_down[0].T, moment1_up[0], moment2_up[0], moment1_down[0].T, moment2_down[0].T,
                  compute_up[0], compute_down[0].T, accum_up[0, 0], accum_down[0, 0].T, stage_acts[0].T, loss_grad.T,
                  jnp.swapaxes(next_micro, 1, 2))
        *states, w_up_t, w_dn_t, own_first, peer_first = update_weights(n_data, arrays, learn_rate, max_norm)
        last_acts, states = forward_rest(arrays[12], w_up_t, w_dn_t, own_first, peer_first, states)
        new_up, new_dn, out1_up, out2_up, out1_dn, out2_dn = states
        return (new_up[None], new_dn.T[None], out1_up[None], out2_up[None], out1_dn.T[None], out2_dn.T[None], last_acts)

    shard_spec = P('stage', 'data', None)
    whole_spec = P('stage', None, None)
    accum_spec = P('data', 'stage', None, None)
    micro_spec = P(None, 'data', None)
    in_specs = (shard_spec,) * 6 + (whole_spec, whole_spec, accum_spec, accum_spec,
                                    P('stage', 'data', None), P('data', None), micro_spec, P(), P())
    out_specs = (shard_spec,) * 6 + (micro_spec,)
    return jax.shard_map(step_body, mesh=mesh, in_specs=in_specs, out_specs=out_specs, check_vma=False)
```

time: 314 us -> 302 us (0.962)
  Pallas kernels: 296 us -> 289 us
  local copies, waits for them, and re-layouts: 12.5 us -> 7.25 us
    pallas_call x4 -> x3, Pallas kernels: 168 us -> 131 us  [forward_chunk(): pl.pallas_call(body, grid_spec=pltpu.PrefetchScalarGridSpec(num_scalar_pr...]
    pallas_call x1, Pallas kernels: 128 us -> 158 us  [update_weights(): pl.pallas_call(body, in_specs=[any_spec] * 13 + [smem_spec] * 2, out_spec...]
    unnamed x22 -> x4, local copies, waits for them, and re-layouts: 7.49 us -> 2.33 us
  transfers between devices with their start and end apart: 4 -> 3, of which waited for: 1 -> 1; matrix products, arithmetic and copies ran while one was open for 1% -> 1% of each run, Pallas kernels for 28% -> 16%
where the time goes in v3:
time: 302 us
  Pallas kernels  289 us (96%)
  local copies, waits for them, and re-layouts  7.25 us (2%)
    pallas_call x1, Pallas kernels, update_weights(): pl.pallas_call(body, in_specs=[any_spec] * 13 + [smem_spec] * 2, out_spec...  158 us
    pallas_call x3, Pallas kernels, forward_chunk(): pl.pallas_call(body, grid_spec=pltpu.PrefetchScalarGridSpec(num_scalar_pr...  131 us
  transfers between devices with their start and end apart: 3, of which 1 were waited for; matrix products, arithmetic and copies ran while one was open for 1% of the time, Pallas kernels for 16%

profile of v3, /device:TPU:0, one launch (start us, length us, event | category | flops | bytes accessed | tf_op | source)
XLA Modules:
  0.0 301.7 jit_solution(3547556281973164872)
XLA Ops:
  1.9 157.6 %update.1 = (f32[144,1536]{1,0:T(8,128)}, f32[576,384]{1,0:T(8,128)}, f32[144,1536]{1,0:T(8,128)}, f32[144,1536]{1,0:T(8,128)}, f32[576,384]{1,0:T(8,128)}, /*in...) custom-call(f32[144,1536]{1,0:T(8,128)} %bitcast.56, ...), custom_call_target="tpu_custom_call" | custom-call | flops 47110422528 | bytes 60000000 | tf_op jit(solution)/shard_map/update/pallas_call | solution.py:601
  159.5 0.0 copy-start
  159.5 1.2 copy-done
  160.7 0.0 copy-start.1
  160.7 1.2 copy-done.1
  161.9 82.8 %fwd_2.1 = (bf16[16,576,2048]{2,1,0:T(8,128)(2,1)}, bf16[4,576,2048]{2,1,0:T(8,128)(2,1)}, f32[144,1536]{1,0:T(8,128)}, f32[576,384]{1,0:T(8,128)}, f32[144,1536...) custom-call(s32[1]{0:T(128)} %bitcast.first, bf16[16,576,2048]{2,1,0:T(8,128)(2,1)} %bitcast.46, ...), custom_call_target="tpu_custom_call" | custom-call | flops 57982058496 | bytes 18874368 | tf_op jit(solution)/shard_map/fwd_2/pallas_call | solution.py:156
  244.7 0.2 collective-permute-start
  244.9 24.0 %fwd_6.1 = (bf16[16,576,2048]{2,1,0:T(8,128)(2,1)}, bf16[1,576,2048]{2,1,0:T(8,128)(2,1)}) custom-call(s32[1]{0:T(128)} %bitcast.32.first, bf16[16,576,2048]{2,1,0:T(8,128)(2,1)} %bitcast.47, bf16[2,1536,576]{2,1,0:T(8,128)(2,1)} %get-tuple-element.29.refs_1_, bf16[2,576,1536]{2,1,0:T(8,128)(2,1)} %get-tuple-element.30.refs_2_, ...), custom_call_target="tpu_custom_call", output_to_operand_aliasing={{0}: (4, {})} | custom-call | flops 14495514624 | bytes 4718592 | tf_op jit(solution)/shard_map/fwd_6/pallas_call | solution.py:156
  268.9 0.3 collective-permute-start.1
  269.2 0.0 collective-permute-done.refs_3_
  269.2 24.6 %fwd_7.1 = (bf16[16,576,2048]{2,1,0:T(8,128)(2,1)}, bf16[1,576,2048]{2,1,0:T(8,128)(2,1)}) custom-call(s32[1]{0:T(128)} %bitcast.31.first, bf16[16,576,2048]{2,1,0:T(8,128)(2,1)} %bitcast.48, bf16[2,1536,576]{2,1,0:T(8,128)(2,1)} %get-tuple-element.29.refs_1_, bf16[2,576,1536]{2,1,0:T(8,128)(2,1)} %get-tuple-element.30.refs_2_, ...), custom_call_target="tpu_custom_call", output_to_operand_aliasing={{0}: (5, {})} | custom-call | flops 14495514624 | bytes 4718592 | tf_op jit(solution)/shard_map/fwd_7/pallas_call | solution.py:156
  293.8 0.3 collective-permute-start.2
  294.1 0.0 collective-permute-done.1
  294.1 1.6 constant_dynamic-update-slice_fusion.1
  295.7 2.7 collective-permute-done.2
  298.3 3.4 %constant_dynamic-update-slice_fusion = bf16[16,576,2048]{2,1,0:T(8,128)(2,1)} fusion(bf16[16,576,2048]{2,1,0:T(8,128)(2,1)} %constant_dynamic-update-slice_fusion.1, bf16[1,576,2048]{2,1,0:T(8,128)(2,1)} %collective-permute-done.2, s32[]{:T(128)S(6)} %select_n.7), kind=kLoop, calls=%fused_computation | loop fusion | bytes 4718596 | tf_op jit(solution)/shard_map/dynamic_update_slice | solution.py:194
Async XLA Ops:
  159.5 1.2 copy-start
  160.7 1.2 copy-start.1
  244.7 24.5 %collective-permute-start = (bf16[4,576,2048]{2,1,0:T(8,128)(2,1)}, bf16[4,576,2048]{2,1,0:T(8,128)(2,1)}, u32[]{:S(2)}, u32[]{:S(2)}) collective-permute-start(bf16[4,576,2048]{2,1,0:T(8,128)(2,1)} %get-tuple-element.45), channel_id=1, source_target_pairs={{0,1},{1,0},{2,3},{3,2},{4,5},{5,4},{6,7},{7,6}} | collective-permute-start | bytes 28311560 | tf_op jit(solution)/shard_map/ppermute | solution.py:190
  268.9 25.2 %collective-permute-start.1 = (bf16[1,576,2048]{2,1,0:T(8,128)(2,1)}, bf16[1,576,2048]{2,1,0:T(8,128)(2,1)S(1)}, u32[]{:S(2)}, u32[]{:S(2)}) collective-permute-start(bf16[1,576,2048]{2,1,0:T(8,128)(2,1)} %get-tuple-element.49), channel_id=1, source_target_pairs={{0,1},{1,0},{2,3},{3,2},{4,5},{5,4},{6,7},{7,6}} | collective-permute-start | bytes 7077896 | tf_op jit(solution)/shard_map/ppermute | solution.py:190
  293.8 4.5 %collective-permute-start.2 = (bf16[1,576,2048]{2,1,0:T(8,128)(2,1)}, bf16[1,576,2048]{2,1,0:T(8,128)(2,1)}, u32[]{:S(2)}, u32[]{:S(2)}) collective-permute-start(bf16[1,576,2048]{2,1,0:T(8,128)(2,1)} %get-tuple-element.50), channel_id=1, source_target_pairs={{0,1},{1,0},{2,3},{3,2},{4,5},{5,4},{6,7},{7,6}} | collective-permute-start | bytes 7077896 | tf_op jit(solution)/shard_map/ppermute | solution.py:190

commit v4 on v3

--- a/solution.py
+++ b/solution.py
@@ -1,3 +1,5 @@
+import functools
+
 import jax
 import jax.numpy as jnp
 from jax import lax
@@ -29,9 +31,10 @@
 GELU_LIN = 0.7978845608028654
 GELU_CUB = GELU_LIN * 0.044715
 ROW_TILE = 512
+UNIT = 2 * ROW_TILE
 FF_TILE = 512
-CHUNKS = (4, 1, 1)
-N_FIRST = 2
+CHUNKS = (7, 2, 1)
+N_FIRST = 6
 
 
 def gelu_half(pre_act):
@@ -40,16 +43,20 @@
     return half + half * jnp.tanh(inner)
 
 
-def block_forward(cols_in, w_up_t, w_down_t, block, hidden_ref):
-    ff_width = w_up_t.shape[1]
-    for start in range(0, ff_width, FF_TILE):
-        pre_act = jnp.dot(w_up_t[block, start:start + FF_TILE, :], cols_in, preferred_element_type=jnp.float32)
-        hidden_ref[start:start + FF_TILE, :] = gelu_half(pre_act).astype(jnp.bfloat16)
-    branch = jnp.dot(w_down_t[block], hidden_ref[...], preferred_element_type=jnp.float32)
-    return (cols_in.astype(jnp.float32) + branch).astype(jnp.bfloat16)
-
-
-def forward_kernel(has_prev, copies, n_state, base, n_own, n_tiles, *refs):
+def pair_forward(pair, up_rows_of, w_down, hidden_ref):
+    ff_width = hidden_ref.shape[1]
+    for half, cols_in in enumerate(pair):
+        for start in range(0, ff_width, FF_TILE):
+            pre_act = jnp.dot(up_rows_of(start), cols_in, preferred_element_type=jnp.float32)
+            hidden_ref[half, start:start + FF_TILE, :] = gelu_half(pre_act).astype(jnp.bfloat16)
+    results = []
+    for half, cols_in in enumerate(pair):
+        branch = jnp.dot(w_down, hidden_ref[half], preferred_element_type=jnp.float32)
+        results.append((cols_in.astype(jnp.float32) + branch).astype(jnp.bfloat16))
+    return results
+
+
+def forward_kernel(is_short, has_prev, copies, n_state, base, n_own, *refs):
     refs = list(refs)
     x_ref, w_up_t, w_down_t = refs[:3]
     refs = refs[3:]
@@ -60,33 +67,46 @@
         refs.pop(0)
     out_ref, y_ref = refs[:2]
     state_out, refs = refs[2:2 + n_state], refs[2 + n_state:]
-    hidden_ref, y_buf, y_sem, copy_sem, state_sem = refs[:5]
-    state_buf = refs[5:]
+    hidden_ref, mid_ref, y_buf, y_sem, in_sem, out_sem, state_sem = refs[:7]
+    copy_bufs, state_buf = refs[7:7 + n_copy], refs[7 + n_copy:]
     mine = lax.axis_index('stage')
-    micro, tile = pl.program_id(0), pl.program_id(1)
-    step = micro * n_tiles + tile
-    n_steps = pl.num_programs(0) * n_tiles
+    step, n_steps = pl.program_id(0), pl.num_programs(0)
     slot = lax.rem(step, 2)
-    tile_cols = pl.ds(pl.multiple_of(tile * ROW_TILE, ROW_TILE), ROW_TILE)
+
+    def out_at(owner, unit):
+        return out_ref.at[owner * n_own + unit // 2, :, pl.ds(pl.multiple_of(lax.rem(unit, 2) * UNIT, UNIT), UNIT)]
 
     def y_copy(which):
-        return pltpu.make_async_copy(y_buf.at[which], out_ref.at[mine * n_own + base + micro, :, tile_cols], y_sem.at[which])
-
-    def tile_copy(index):
-        from_peer, first, count = copies[index]
+        return pltpu.make_async_copy(y_buf.at[which], out_at(mine, base + step), y_sem.at[which])
+
+    def enter(index):
+        share = copies[index][3]
+        return pltpu.make_async_copy(copy_refs[index].at[pl.ds(step * share, share)], copy_bufs[index], in_sem.at[index])
+
+    def leave(index):
+        from_peer, first, _, share = copies[index]
         owner = 1 - mine if from_peer else mine
-        return pltpu.make_async_copy(copy_refs[index], out_ref.at[pl.ds(owner * n_own + first, count), :, tile_cols], copy_sem.at[index])
+        return [pltpu.make_async_copy(copy_bufs[index].at[unit], out_at(owner, first + step * share + unit), out_sem.at[index, unit])
+                for unit in range(share)]
 
     def state_copy(index, leaving):
         src, dst = (state_buf[index], state_out[index]) if leaving else (state_in[index], state_buf[index])
         return pltpu.make_async_copy(src, dst, state_sem.at[index])
 
-    if n_copy:
-        @pl.when(micro == 0)
-        def _():
-            for index in range(n_copy):
-                tile_copy(index).start()
-
+    def for_copies(action):
+        for index in range(n_copy):
+            pl.when(step * copies[index][3] < copies[index][2])(functools.partial(action, index))
+
+    def leave_start(index):
+        enter(index).wait()
+        for copy in leave(index):
+            copy.start()
+
+    def leave_wait(index):
+        for copy in leave(index):
+            copy.wait()
+
+    for_copies(lambda index: enter(index).start())
     if n_state:
         @pl.when(step == 0)
         def _():
@@ -99,75 +119,90 @@
                 state_copy(index, False).wait()
                 state_copy(index, True).start()
 
-    cols = x_ref[0]
-    for block in range(2):
-        cols = block_forward(cols, w_up_t, w_down_t, block, hidden_ref)
+    half_cols = UNIT // 2
+    sides = (slice(0, half_cols), slice(half_cols, UNIT))
+    pair = [x_ref[0, :, cols] for cols in sides]
+
+    def block_step(block, carry):
+        inputs = [mid_ref[:, cols] for cols in sides]
+        results = pair_forward(inputs, lambda start: w_up_t[block, start:start + FF_TILE, :], w_down_t[block], hidden_ref)
+        for half in range(2):
+            mid_ref[:, sides[half]] = results[half]
+        pl.when(block == 0)(lambda: for_copies(leave_start))
+        return carry
+
+    if is_short:
+        mid_ref[...] = x_ref[0]
+        lax.fori_loop(0, 2, block_step, 0)
+        pair = [mid_ref[:, cols] for cols in sides]
+    for block in range(0 if is_short else 2):
+        pair = pair_forward(pair, lambda start, block=block: w_up_t[block, start:start + FF_TILE, :], w_down_t[block], hidden_ref)
+        if block == 0:
+            for_copies(leave_start)
 
     @pl.when(step >= 2)
     def _():
         y_copy(slot).wait()
 
-    y_buf[slot] = cols
-    y_ref[0] = cols
+    for half in range(2):
+        cols = slice(half * half_cols, (half + 1) * half_cols)
+        y_buf[slot, :, cols] = pair[half]
+        y_ref[0, :, cols] = pair[half]
     y_copy(slot).start()
-    if n_copy:
-        @pl.when(micro == 0)
-        def _():
-            for index in range(n_copy):
-                tile_copy(index).wait()
+    for_copies(leave_wait)
 
     @pl.when(step == n_steps - 1)
     def _():
         y_copy(slot).wait()
-        y_copy(1 - slot).wait()
         for index in range(n_state):
             state_copy(index, True).wait()
+
+    @pl.when(jnp.logical_and(step == n_steps - 1, step >= 1))
+    def _():
+        y_copy(1 - slot).wait()
 
 
 def forward_chunk(base, n_chunk, micro_t, w_up_t, w_down_t, prev_out, copied, states):
     n_micro, width, n_rows = micro_t.shape
     n_own = n_micro // 2
-    n_tiles = n_rows // ROW_TILE
     ff_width = w_up_t.shape[1]
     mine = lax.axis_index('stage')
     any_spec = pl.BlockSpec(memory_space=pl.ANY)
-    scalar = jnp.full((1,), mine * n_own + base, jnp.int32)
-    in_specs = [pl.BlockSpec((1, width, ROW_TILE), lambda i, j, first: (first[0] + i, 0, j)),
-                pl.BlockSpec((2, ff_width, width), lambda i, j, first: (0, 0, 0)),
-                pl.BlockSpec((2, width, ff_width), lambda i, j, first: (0, 0, 0))]
-    operands = [micro_t, w_up_t, w_down_t]
-    for array, _, _ in copied:
-        in_specs.append(pl.BlockSpec((array.shape[0], width, ROW_TILE), lambda i, j, first: (0, 0, jnp.where(i == 0, j, n_tiles - 1))))
-        operands.append(array)
-    for array in states:
-        in_specs.append(any_spec)
-        operands.append(array)
+    scalar = jnp.full((1,), mine * n_own, jnp.int32)
+    in_specs = [pl.BlockSpec((1, width, UNIT), lambda i, first: (first[0] + (base + i) // 2, 0, lax.rem(base + i, 2))),
+                pl.BlockSpec((2, ff_width, width), lambda i, first: (0, 0, 0)),
+                pl.BlockSpec((2, width, ff_width), lambda i, first: (0, 0, 0))]
+    operands = [micro_t, w_up_t, w_down_t] + [array for array, _, _ in copied] + list(states)
+    in_specs += [any_spec] * (len(copied) + len(states))
     aliases = {}
     if prev_out is not None:
         in_specs.append(any_spec)
         operands.append(prev_out)
         aliases = {len(operands): 0}
-    copies = [(from_peer, first, array.shape[0]) for array, from_peer, first in copied]
+    copies = [(from_peer, first, array.shape[0], pl.cdiv(array.shape[0], n_chunk)) for array, from_peer, first in copied]
+    max_share = max([1] + [share for *_, share in copies])
 
     def body(first, *refs):
-        forward_kernel(prev_out is not None, copies, len(states), base, n_own, n_tiles, *refs)
-
-    flops = 8 * n_chunk * n_rows * width * ff_width
+        forward_kernel(n_chunk <= 2, prev_out is not None, copies, len(states), base, n_own, *refs)
+
+    flops = 8 * n_chunk * UNIT * width * ff_width
     return pl.pallas_call(
         body,
         grid_spec=pltpu.PrefetchScalarGridSpec(
-            num_scalar_prefetch=1, grid=(n_chunk, n_tiles), in_specs=in_specs,
-            out_specs=[any_spec, pl.BlockSpec((1, width, ROW_TILE), lambda i, j, first: (i, 0, j))] + [any_spec] * len(states),
-            scratch_shapes=[pltpu.VMEM((ff_width, ROW_TILE), jnp.bfloat16), pltpu.VMEM((2, width, ROW_TILE), jnp.bfloat16),
-                            pltpu.SemaphoreType.DMA((2,)), pltpu.SemaphoreType.DMA((2,)), pltpu.SemaphoreType.DMA((6,))]
+            num_scalar_prefetch=1, grid=(n_chunk,), in_specs=in_specs,
+            out_specs=[any_spec, pl.BlockSpec((1, width, UNIT), lambda i, first: (i, 0, 0))] + [any_spec] * len(states),
+            scratch_shapes=[pltpu.VMEM((2, ff_width, UNIT // 2), jnp.bfloat16), pltpu.VMEM((width, UNIT), jnp.bfloat16),
+                            pltpu.VMEM((2, width, UNIT), jnp.bfloat16),
+                            pltpu.SemaphoreType.DMA((2,)), pltpu.SemaphoreType.DMA((2,)), pltpu.SemaphoreType.DMA((2, max_share)),
+                            pltpu.SemaphoreType.DMA((6,))]
+            + [pltpu.VMEM((share, width, UNIT), jnp.bfloat16) for *_, share in copies]
             + [pltpu.VMEM(array.shape, array.dtype) for array in states]),
         out_shape=[jax.ShapeDtypeStruct(micro_t.shape, jnp.bfloat16),
-                   jax.ShapeDtypeStruct((n_chunk, width, n_rows), jnp.bfloat16)]
+                   jax.ShapeDtypeStruct((n_chunk, width, UNIT), jnp.bfloat16)]
         + [jax.ShapeDtypeStruct(array.shape, array.dtype) for array in states],
         input_output_aliases=aliases,
-        compiler_params=pltpu.CompilerParams(dimension_semantics=("arbitrary", "arbitrary"),
-                                             vmem_limit_bytes=52 * 1024 * 1024),
-        cost_estimate=pl.CostEstimate(flops=flops, bytes_accessed=4 * n_chunk * n_rows * width, transcendentals=0),
+        compiler_params=pltpu.CompilerParams(dimension_semantics=("arbitrary",), vmem_limit_bytes=50 * 1024 * 1024),
+        cost_estimate=pl.CostEstimate(flops=flops, bytes_accessed=4 * n_chunk * UNIT * width, transcendentals=0),
         name=f"fwd_{base}",
     )(scalar, *operands)
 
@@ -191,7 +226,9 @@
         base += n_chunk
     for item in received:
         if item is not None:
-            out = lax.dynamic_update_slice(out, item[0], ((1 - mine) * n_own + item[2], 0, 0))
+            for index in range(item[0].shape[0]):
+                unit = item[2] + index
+                out = lax.dynamic_update_slice(out, item[0][index:index + 1], ((1 - mine) * n_own + unit // 2, 0, unit % 2 * UNIT))
     return jnp.swapaxes(out, 1, 2), results
 
 
@@ -222,7 +259,6 @@
     width, ff_width = wts.shape[2:]
     up_rows, dn_cols = last_up.shape[0], last_dn.shape[1]
     n_own = micro_in.shape[0] // 2
-    n_tiles = micro_in.shape[2] // ROW_TILE
     n_sub = GRAD_HALF // GRAD_TILE
     halves = (1 - pos_y, pos_y)
 
@@ -255,25 +291,32 @@
     pl.semaphore_wait(barrier, n_dev - 1)
 
     swap_acts = remote(acts_in.at[:, cols_of(peer, half_rows)], acts.at[core], 0, to_peer)
-    swap_wts = [[remote((cmp_up, cmp_dn)[kind].at[:, cols_of(half, GRAD_HALF)], wts.at[core, kind, :, cols_of(half, GRAD_HALF)],
-                        1 + order * 2 + kind, to_peer) for kind in range(2)] for order, half in enumerate(halves)]
+    def swap_piece(kind, tile):
+        cols = cols_of(halves[0] * n_sub + tile, GRAD_TILE)
+        return remote((cmp_up, cmp_dn)[kind].at[:, cols], wts.at[core, kind, :, cols], 1 + kind * n_sub + tile, to_peer)
+
+    swap_late = [remote((cmp_up, cmp_dn)[kind].at[:, cols_of(halves[1], GRAD_HALF)], wts.at[core, kind, :, cols_of(halves[1], GRAD_HALF)],
+                        1 + 2 * n_sub + kind, to_peer) for kind in range(2)]
     swap_acts.start()
-    for order in range(2):
+    for tile in range(n_sub):
         for kind in range(2):
-            swap_wts[order][kind].start()
-
-    def part_copy(kind, order, tile):
-        cols = cols_of(halves[order] * n_sub + tile, GRAD_TILE)
-        return remote(sums.at[peer, kind, :, cols], part.at[kind, :, cols], 5 + (kind * 2 + order) * n_sub + tile, to_peer)
+            swap_piece(kind, tile).start()
+    for copy in swap_late:
+        copy.start()
+
+    def part_copy(kind, step):
+        late = step // n_sub
+        cols = cols_of((1 - pos_y + late * (2 * pos_y - 1)) * n_sub + lax.rem(step, n_sub), GRAD_TILE)
+        return remote(sums.at[peer, kind, :, cols], part.at[kind, :, cols], 9 + kind * 2 * n_sub + step, to_peer)
 
     up_first = [[remote(sums.at[core, 0, rows_of(row * 2 + 1 - pos_x), cols_of(half, GRAD_HALF)],
-                        fwd_up.at[slot, :, cols_of(half, GRAD_HALF)], 17 + order * 2 + slot, to_x)
+                        fwd_up.at[slot, :, cols_of(half, GRAD_HALF)], 21 + order * 2 + slot, to_x)
                  for slot, row in enumerate(halves)] for order, half in enumerate(halves)]
-    dn_first = [remote(sums.at[core, 1, :, cols_of((1 - pos_y) * 2 + col, dn_cols)], fwd_dn.at[slot], 21 + slot, to_y)
+    dn_first = [remote(sums.at[core, 1, :, cols_of((1 - pos_y) * 2 + col, dn_cols)], fwd_dn.at[slot], 25 + slot, to_y)
                 for slot, col in enumerate((1 - pos_x, pos_x))]
     up_next = [remote(sums.at[core, 0, rows_of(chip_y), cols_of(half, GRAD_HALF)], last_up.at[:, cols_of(half, GRAD_HALF)],
-                      23 + order, to_y) for order, half in enumerate(halves)]
-    dn_next = remote(sums.at[core, 1, :, cols_of(chip_x, dn_cols)], last_dn, 25, to_x)
+                      27 + order, to_y) for order, half in enumerate(halves)]
+    dn_next = remote(sums.at[core, 1, :, cols_of(chip_x, dn_cols)], last_dn, 29, to_x)
 
     def add_up(index, order):
         cols = cols_of(halves[order], GRAD_HALF)
@@ -286,7 +329,7 @@
     def scatter_half(order):
         for kind in range(2):
             for tile in range(n_sub):
-                part_copy(kind, order, tile).wait_recv()
+                part_copy(kind, order * n_sub + tile).wait_recv()
         for slot in range(2):
             add_up((halves[slot]) * 2 + 1 - pos_x, order)
             up_first[order][slot].start()
@@ -305,7 +348,7 @@
 
         @pl.when(own)
         def _():
-            for copy in loads[1:6]:
+            for copy in loads[1:4]:
                 copy.wait()
 
         @pl.when(jnp.logical_not(own))
@@ -314,43 +357,54 @@
 
         acts_row[...] = acts[block].T
         grad_row[...] = grad[...].T
-        for order in range(2):
+        def tile_step(step, carry, block=block, own=own):
+            late = step // n_sub
+            cols = cols_of((1 - pos_y + late * (2 * pos_y - 1)) * n_sub + lax.rem(step, n_sub), GRAD_TILE)
+
+            @pl.when(jnp.logical_and(jnp.logical_not(own), step < n_sub))
+            def _():
+                swap_piece(0, step).wait_recv()
+                swap_piece(1, step).wait_recv()
+
+            @pl.when(jnp.logical_and(jnp.logical_not(own), step == n_sub))
+            def _():
+                for copy in swap_late:
+                    copy.wait_recv()
+
+            half, at_step = (0, 2 * n_sub - 1) if block == 1 else (1, n_sub)
+            pl.when(jnp.logical_and(core == 1, step == at_step))(functools.partial(scatter_half, half))
+
+            pre_act = jnp.dot(acts_row[...], wts[block, 0, :, cols], preferred_element_type=jnp.float32)
+            d_hidden = jnp.dot(grad_row[...], wts[block, 1, :, cols], preferred_element_type=jnp.float32)
+            hidden, slope = gelu_pair(pre_act)
+            dw_down = jnp.dot(grad[...], hidden.astype(jnp.bfloat16), preferred_element_type=jnp.float32)
+            d_tile = (d_hidden * slope).astype(jnp.bfloat16)
+            if block == 1:
+                d_pre[:, cols] = d_tile
+            dw_up = jnp.dot(acts[block], d_tile, preferred_element_type=jnp.float32)
+
+            @pl.when(jnp.logical_and(own, step == 0))
+            def _():
+                for copy in loads[4:6]:
+                    copy.wait()
+
+            @pl.when(own)
+            def _():
+                sums[block, 0, :, cols] += dw_up
+                sums[block, 1, :, cols] += dw_down
+
             @pl.when(jnp.logical_not(own))
-            def _(order=order):
-                for copy in swap_wts[order]:
-                    copy.wait_recv()
-
-            def tile_step(tile, carry, block=block, own=own, order=order):
-                cols = cols_of(halves[order] * n_sub + tile, GRAD_TILE)
-                pre_act = jnp.dot(acts_row[...], wts[block, 0, :, cols], preferred_element_type=jnp.float32)
-                d_hidden = jnp.dot(grad_row[...], wts[block, 1, :, cols], preferred_element_type=jnp.float32)
-                hidden, slope = gelu_pair(pre_act)
-                dw_down = jnp.dot(grad[...], hidden.astype(jnp.bfloat16), preferred_element_type=jnp.float32)
-                d_tile = (d_hidden * slope).astype(jnp.bfloat16)
-                if block == 1:
-                    d_pre[:, cols] = d_tile
-                dw_up = jnp.dot(acts[block], d_tile, preferred_element_type=jnp.float32)
-
-                @pl.when(own)
-                def _():
-                    sums[block, 0, :, cols] += dw_up
-                    sums[block, 1, :, cols] += dw_down
-
-                @pl.when(jnp.logical_not(own))
-                def _():
-                    sums[block, 0, :, cols] = dw_up
-                    sums[block, 1, :, cols] = dw_down
-                    part_copy(0, order, tile).start()
-                    part_copy(1, order, tile).start()
-                return carry
-
-            lax.fori_loop(0, n_sub, tile_step, 0)
-            if block == 0 and order == 0:
-                pl.when(core == 1)(lambda: scatter_half(1))
+            def _():
+                sums[block, 0, :, cols] = dw_up
+                sums[block, 1, :, cols] = dw_down
+                part_copy(0, step).start()
+                part_copy(1, step).start()
+            return carry
+
+        lax.fori_loop(0, 2 * n_sub, tile_step, 0)
         if block == 1:
             d_in = lax.dot_general(wts[1, 0], d_pre[...], (((1,), (1,)), ((), ())), preferred_element_type=jnp.float32)
             grad[...] = (grad[...].astype(jnp.float32) + d_in).astype(jnp.bfloat16)
-            pl.when(core == 1)(lambda: scatter_half(0))
 
     @pl.when(core == 0)
     def _():
@@ -360,16 +414,12 @@
     for copy in loads[6:]:
         copy.start()
 
-    def x_slot(tile):
-        slot = lax.rem(tile, 4)
-        return acts.at[slot // 2, :, cols_of(lax.rem(slot, 2), ROW_TILE)]
-
-    def x_load(tile):
-        return pltpu.make_async_copy(micro_in.at[core * n_own + tile // n_tiles, :, cols_of(lax.rem(tile, n_tiles), ROW_TILE)],
-                                     x_slot(tile), tile_sem.at[0, lax.rem(tile, 4)])
-
-    for tile in range(4):
-        x_load(tile).start()
+    def x_load(pair):
+        return pltpu.make_async_copy(micro_in.at[core * n_own + pair // 2, :, cols_of(lax.rem(pair, 2), UNIT)],
+                                     acts.at[lax.rem(pair, 2)], tile_sem.at[0, lax.rem(pair, 2)])
+
+    for pair in range(2):
+        x_load(pair).start()
 
     up_first[0][0].wait_recv()
     cols = cols_of(halves[0], GRAD_HALF)
@@ -400,7 +450,7 @@
     norm_copies = []
     for offset in range(1, n_dev):
         other = lax.rem(me + offset, n_dev)
-        norm_copies.append(remote(norm_tiles.at[me], norm_tiles.at[me], 25 + offset, (other // 2, lax.rem(other, 2))))
+        norm_copies.append(remote(norm_tiles.at[me], norm_tiles.at[me], 29 + offset, (other // 2, lax.rem(other, 2))))
     for copy in norm_copies:
         copy.start()
     for copy in loads[6:]:
@@ -414,10 +464,10 @@
     chips = (chip, chip_x, chip_y, chip_d)
     up_at = [wts.at[core, 0, rows_of(index)] for index in chips]
     dn_at = [wts.at[core, 1, :, cols_of(index, dn_cols)] for index in chips]
-    up_x, up_y, up_relay = remote(up_at[0], up_at[0], 33, to_x), remote(up_at[0], up_at[0], 34, to_y), remote(up_at[1], up_at[1], 35, to_y)
-    dn_x, dn_y, dn_relay = remote(dn_at[0], dn_at[0], 36, to_x), remote(dn_at[0], dn_at[0], 37, to_y), remote(dn_at[2], dn_at[2], 38, to_x)
-    up_peer = [remote(up_at[index], up_at[index], 39 + index, to_peer) for index in range(4)]
-    dn_peer = [remote(dn_at[index], dn_at[index], 43 + index, to_peer) for index in range(4)]
+    up_x, up_y, up_relay = remote(up_at[0], up_at[0], 37, to_x), remote(up_at[0], up_at[0], 38, to_y), remote(up_at[1], up_at[1], 39, to_y)
+    dn_x, dn_y, dn_relay = remote(dn_at[0], dn_at[0], 40, to_x), remote(dn_at[0], dn_at[0], 41, to_y), remote(dn_at[2], dn_at[2], 42, to_x)
+    up_peer = [remote(up_at[index], up_at[index], 43 + index, to_peer) for index in range(4)]
+    dn_peer = [remote(dn_at[index], dn_at[index], 47 + index, to_peer) for index in range(4)]
 
     def gather_up():
         up_x.start()
@@ -484,27 +534,24 @@
 
     swap_acts.wait_send()
     for order in range(2):
-        for copy in swap_wts[order] + up_first[order] + [up_next[order]]:
+        for copy in up_first[order] + [up_next[order]]:
             copy.wait_send()
         for kind in range(2):
             for tile in range(n_sub):
-                part_copy(kind, order, tile).wait_send()
-    for copy in dn_first + [dn_next] + norm_copies:
+                part_copy(kind, order * n_sub + tile).wait_send()
+    for copy in dn_first + [dn_next] + norm_copies + swap_late + [swap_piece(kind, tile) for kind in range(2) for tile in range(n_sub)]:
         copy.wait_send()
 
     def weights_out(block):
         return [pltpu.make_async_copy(turned, w_up_out.at[block], store_sem.at[6 + block]),
                 pltpu.make_async_copy(wts.at[block, 1], w_dn_out.at[block], store_sem.at[8 + block])]
 
-    def forward_tile(cols_in, block):
-        for start in range(0, ff_width, FF_TILE):
-            pre_act = jnp.dot(turned[start:start + FF_TILE, :], cols_in, preferred_element_type=jnp.float32)
-            hidden_ref[start:start + FF_TILE, :] = gelu_half(pre_act).astype(jnp.bfloat16)
-        branch = jnp.dot(wts[block, 1], hidden_ref[...], preferred_element_type=jnp.float32)
-        return (cols_in.astype(jnp.float32) + branch).astype(jnp.bfloat16)
-
-    n_first = own_first.shape[0] * n_tiles
+    def unit_forward(pair, block):
+        return pair_forward(pair, lambda start: turned[start:start + FF_TILE, :], wts[block, 1], hidden_ref)
+
+    n_first = own_first.shape[0]
     per_row = ff_width // ROW_TILE
+    sides = (slice(0, ROW_TILE), slice(ROW_TILE, UNIT))
 
     def mid_slot(tile):
         row = tile // per_row
@@ -514,27 +561,18 @@
     for copy in weights_out(0):
         copy.start()
 
-    def first_block(tile, carry):
-        @pl.when(jnp.logical_and(core == 1, tile == 3))
+    def first_block(pair, carry):
+        for number, action in ((2, gather_relay), (3, gather_near), (4, gather_far)):
+            pl.when(jnp.logical_and(core == 1, pair == number))(action)
+        x_load(pair).wait()
+        slot = lax.rem(pair, 2)
+        mids = unit_forward([acts[slot, :, cols] for cols in sides], 0)
+        for half in range(2):
+            sums[mid_slot(2 * pair + half)] = mids[half].astype(jnp.float32)
+
+        @pl.when(pair + 2 < n_first)
         def _():
-            gather_relay()
-
-        @pl.when(jnp.logical_and(core == 1, tile == 5))
-        def _():
-            gather_near()
-
-        @pl.when(jnp.logical_and(core == 1, tile == 7))
-        def _():
-            gather_far()
-
-        x_load(tile).wait()
-        slot = lax.rem(tile, 4)
-        mid = forward_tile(acts[slot // 2, :, cols_of(lax.rem(slot, 2), ROW_TILE)], 0)
-        sums[mid_slot(tile)] = mid.astype(jnp.float32)
-
-        @pl.when(tile + 4 < n_first)
-        def _():
-            x_load(tile + 4).start()
+            x_load(pair + 2).start()
         return carry
 
     lax.fori_loop(0, n_first, first_block, 0)
@@ -544,37 +582,30 @@
     for copy in weights_out(1):
         copy.start()
 
-    def y_slot(tile):
-        return grad.at[:, cols_of(lax.rem(tile, 2), ROW_TILE)]
-
-    def y_out(tile):
-        place = (tile // n_tiles, slice(None), cols_of(lax.rem(tile, n_tiles), ROW_TILE))
-        keep = pltpu.make_async_copy(y_slot(tile), own_first.at[place], tile_sem.at[1, lax.rem(tile, 2)])
-        give = pltpu.make_async_remote_copy(src_ref=y_slot(tile), dst_ref=peer_first.at[place], send_sem=tile_sem.at[2, lax.rem(tile, 2)],
-                                            recv_sem=recv_sem.at[47 + tile], device_id=to_peer, device_id_type=MESH_ID)
+    def y_out(pair):
+        keep = pltpu.make_async_copy(grad, own_first.at[pair], tile_sem.at[1, 0])
+        give = pltpu.make_async_remote_copy(src_ref=grad, dst_ref=peer_first.at[pair], send_sem=tile_sem.at[1, 1],
+                                            recv_sem=recv_sem.at[51 + pair], device_id=to_peer, device_id_type=MESH_ID)
         return keep, give
 
-    def second_block(tile, carry):
-        result = forward_tile(sums[mid_slot(tile)].astype(jnp.bfloat16), 1)
-
-        @pl.when(tile >= 2)
-        def _():
-            keep, give = y_out(tile - 2)
-            keep.wait()
-            give.wait_send()
-
-        grad[:, cols_of(lax.rem(tile, 2), ROW_TILE)] = result
-        for copy in y_out(tile):
+    def y_wait(pair):
+        keep, give = y_out(pair)
+        keep.wait()
+        give.wait_send()
+
+    def second_block(pair, carry):
+        results = unit_forward([sums[mid_slot(2 * pair + half)].astype(jnp.bfloat16) for half in range(2)], 1)
+        pl.when(pair >= 1)(lambda: y_wait(pair - 1))
+        for half in range(2):
+            grad[:, sides[half]] = results[half]
+        for copy in y_out(pair):
             copy.start()
         return carry
 
     lax.fori_loop(0, n_first, second_block, 0)
-    for tile in range(n_first - 2, n_first):
-        keep, give = y_out(tile)
-        keep.wait()
-        give.wait_send()
-    for tile in range(n_first):
-        y_out(tile)[1].wait_recv()
+    y_wait(n_first - 1)
+    for pair in range(n_first):
+        y_out(pair)[1].wait_recv()
 
     for copy in [up_x, up_y, up_relay, dn_x, dn_y, dn_relay] + up_peer + dn_peer:
         copy.wait_send()
@@ -589,15 +620,15 @@
     up_rows, dn_cols = arrays[0].shape[0], arrays[1].shape[1]
     f32, bf16 = jnp.float32, jnp.bfloat16
     up_state, dn_state = jax.ShapeDtypeStruct((up_rows, ff_width), f32), jax.ShapeDtypeStruct((width, dn_cols), f32)
-    first = jax.ShapeDtypeStruct((N_FIRST, width, n_rows), bf16)
+    first = jax.ShapeDtypeStruct((N_FIRST, width, UNIT), bf16)
     any_spec = pl.BlockSpec(memory_space=pl.ANY)
     smem_spec = pl.BlockSpec(memory_space=pltpu.SMEM)
-    n_sem = 47 + N_FIRST * n_rows // ROW_TILE
+    n_sem = 51 + N_FIRST
 
     def body(*refs):
         update_kernel(n_data, *refs)
 
-    flops = 20 * half_rows * width * ff_width + 8 * N_FIRST * n_rows * width * ff_width
+    flops = 20 * half_rows * width * ff_width + 8 * N_FIRST * UNIT * width * ff_width
     return pl.pallas_call(
         body,
         in_specs=[any_spec] * 13 + [smem_spec] * 2,
@@ -610,9 +641,9 @@
             pltpu.VMEM((half_rows, ff_width), bf16), pltpu.VMEM((2, 2, width, ff_width), f32), pltpu.VMEM((2, width, ff_width), f32),
             pltpu.VMEM((2, up_rows, ff_width), f32), pltpu.VMEM((2, width, dn_cols), f32),
             pltpu.VMEM((up_rows, ff_width), f32), pltpu.VMEM((width, dn_cols), f32), pltpu.VMEM((2 * n_data, 8, 128), f32),
-            pltpu.VMEM((ff_width, width), bf16), pltpu.VMEM((ff_width, ROW_TILE), bf16),
+            pltpu.VMEM((ff_width, width), bf16), pltpu.VMEM((2, ff_width, ROW_TILE), bf16),
             pltpu.SemaphoreType.DMA((n_sem,)), pltpu.SemaphoreType.DMA((n_sem,)), pltpu.SemaphoreType.DMA((12,)),
-            pltpu.SemaphoreType.DMA((10,)), pltpu.SemaphoreType.DMA((3, 4))],
+            pltpu.SemaphoreType.DMA((10,)), pltpu.SemaphoreType.DMA((2, 2))],
         compiler_params=pltpu.CompilerParams(collective_id=0, has_side_effects=True, vmem_limit_bytes=67000000),
         cost_estimate=pl.CostEstimate(flops=flops, bytes_accessed=60000000, transcendentals=0),
         name="update",

time: 302 us -> 309 us (1.023)
  local copies, waits for them, and re-layouts: 7.25 us -> 14.9 us
    pallas_call x1, Pallas kernels: 158 us -> 172 us  [update_weights(): pl.pallas_call(body, in_specs=[any_spec] * 13 + [smem_spec] * 2, out_spec...]
    pallas_call x3, Pallas kernels: 131 us -> 119 us  [forward_chunk(): pl.pallas_call(body, grid_spec=pltpu.PrefetchScalarGridSpec(num_scalar_pr...]
    unnamed x4 -> x10, local copies, waits for them, and re-layouts: 2.33 us -> 7.84 us
    dynamic_update_slice x2 -> x3, local copies, waits for them, and re-layouts: 4.92 us -> 7.09 us  [forward_rest(): lax.dynamic_update_slice(out, item[0][index:index + 1], ((1 - mine) * n_o...]
  transfers between devices with their start and end apart: 3 -> 3, of which waited for: 1 -> 0; matrix products, arithmetic and copies ran while one was open for 1% -> 2% of each run, Pallas kernels for 16% -> 12%
where the time goes in v4:
time: 309 us
  Pallas kernels  291 us (94%)
  local copies, waits for them, and re-layouts  14.9 us (5%)
    pallas_call x1, Pallas kernels, update_weights(): pl.pallas_call(body, in_specs=[any_spec] * 13 + [smem_spec] * 2, out_spec...  172 us
    pallas_call x3, Pallas kernels, forward_chunk(): pl.pallas_call(body, grid_spec=pltpu.PrefetchScalarGridSpec(num_scalar_pr...  119 us
    unnamed x10, local copies, waits for them, and re-layouts  7.84 us
    dynamic_update_slice x3, local copies, waits for them, and re-layouts, forward_rest(): lax.dynamic_update_slice(out, item[0][index:index + 1], ((1 - mine) * n_o...  7.09 us
  transfers between devices with their start and end apart: 3, of which 0 were waited for; matrix products, arithmetic and copies ran while one was open for 2% of the time, Pallas kernels for 12%

profile of v4, /device:TPU:0, one launch (start us, length us, event | category | flops | bytes accessed | tf_op | source)
XLA Modules:
  0.0 308.5 jit_solution(10296919335302238535)
XLA Ops:
  1.9 172.1 %update.1 = (f32[144,1536]{1,0:T(8,128)}, f32[576,384]{1,0:T(8,128)}, f32[144,1536]{1,0:T(8,128)}, f32[144,1536]{1,0:T(8,128)}, f32[576,384]{1,0:T(8,128)}, /*in...) custom-call(f32[144,1536]{1,0:T(8,128)} %bitcast.54, ...), custom_call_target="tpu_custom_call" | custom-call | flops 61605937152 | bytes 60000000 | tf_op jit(solution)/shard_map/update/pallas_call | solution.py:632
  174.0 0.0 copy-start
  174.0 1.2 copy-done
  175.2 0.0 copy-start.1
  175.2 1.2 copy-done.1
  176.4 0.0 copy-start.2
  176.4 1.2 copy-done.2
  177.5 0.0 copy-start.3
  177.5 1.2 copy-done.3
  178.7 80.6 %fwd_6.1 = (bf16[16,576,2048]{2,1,0:T(8,128)(2,1)}, bf16[7,576,1024]{2,1,0:T(8,128)(2,1)}, f32[144,1536]{1,0:T(8,128)}, f32[576,384]{1,0:T(8,128)}, f32[144,1536...) custom-call(s32[1]{0:T(128)} %bitcast.first, bf16[16,576,2048]{2,1,0:T(8,128)(2,1)} %bitcast.44, ...), custom_call_target="tpu_custom_call" | custom-call | flops 50734301184 | bytes 16515072 | tf_op jit(solution)/shard_map/fwd_6/pallas_call | solution.py:189
  259.3 0.2 collective-permute-start
  259.5 23.7 %fwd_13.1 = (bf16[16,576,2048]{2,1,0:T(8,128)(2,1)}, bf16[2,576,1024]{2,1,0:T(8,128)(2,1)S(1)}) custom-call(s32[1]{0:T(128)} %bitcast.first, bf16[16,576,2048]{2,1,0:T(8,128)(2,1)} %bitcast.45, bf16[2,1536,576]{2,1,0:T(8,128)(2,1)} %get-tuple-element.29.refs_1_, bf16[2,576,1536]{2,1,0:T(8,128)(2,1)} %get-tuple-element.30.refs_2_, ...), custom_call_target="tpu_custom_call", output_to_operand_aliasing={{0}: (4, {})} | custom-call | flops 14495514624 | bytes 4718592 | tf_op jit(solution)/shard_map/fwd_13/pallas_call | solution.py:189
  283.2 0.3 collective-permute-start.1
  283.5 0.0 collective-permute-done.refs_3_
  283.5 0.0 copy-start.4
  283.6 3.2 %copy-done.4 = bf16[7,576,1024]{2,1,0:T(8,128)(2,1)} copy-done((bf16[7,576,1024]{2,1,0:T(8,128)(2,1)}, bf16[7,576,1024]{2,1,0:T(8,128)(2,1)S(1)}, u32[]{:S(2)}) %copy-start.4) | copy-done | bytes 8257560
  286.7 14.5 %fwd_15.1 = (bf16[16,576,2048]{2,1,0:T(8,128)(2,1)}, bf16[1,576,1024]{2,1,0:T(8,128)(2,1)S(1)}) custom-call(s32[1]{0:T(128)} %bitcast.first, bf16[16,576,2048]{2,1,0:T(8,128)(2,1)} %bitcast.46, bf16[2,1536,576]{2,1,0:T(8,128)(2,1)} %get-tuple-element.29.refs_1_, bf16[2,576,1536]{2,1,0:T(8,128)(2,1)} %get-tuple-element.30.refs_2_, ...), custom_call_target="tpu_custom_call", output_to_operand_aliasing={{0}: (5, {})} | custom-call | flops 7247757312 | bytes 2359296 | tf_op jit(solution)/shard_map/fwd_15/pallas_call | solution.py:189
  301.2 0.2 collective-permute-start.2
  301.4 0.0 collective-permute-done.1
  301.4 2.4 slice_dynamic-update-slice_fusion.1
  303.8 2.4 slice_dynamic-update-slice_fusion
  306.2 0.0 collective-permute-done.2
  306.2 2.4 constant_dynamic-update-slice_fusion
Async XLA Ops:
  174.0 1.2 copy-start
  175.2 1.2 copy-start.1
  176.4 1.2 copy-start.2
  177.5 1.2 copy-start.3
  259.3 24.3 %collective-permute-start = (bf16[7,576,1024]{2,1,0:T(8,128)(2,1)}, bf16[7,576,1024]{2,1,0:T(8,128)(2,1)S(1)}, u32[]{:S(2)}, u32[]{:S(2)}) collective-permute-start(bf16[7,576,1024]{2,1,0:T(8,128)(2,1)} %get-tuple-element.45), channel_id=1, source_target_pairs={{0,1},{1,0},{2,3},{3,2},{4,5},{5,4},{6,7},{7,6}} | collective-permute-start | bytes 24772616 | tf_op jit(solution)/shard_map/ppermute | solution.py:225
  283.2 18.2 %collective-permute-start.1 = (bf16[2,576,1024]{2,1,0:T(8,128)(2,1)S(1)}, bf16[2,576,1024]{2,1,0:T(8,128)(2,1)}, u32[]{:S(2)}, u32[]{:S(2)}) collective-permute-start(bf16[2,576,1024]{2,1,0:T(8,128)(2,1)S(1)} %get-tuple-element.49), channel_id=1, source_target_pairs={{0,1},{1,0},{2,3},{3,2},{4,5},{5,4},{6,7},{7,6}} | collective-permute-start | bytes 7077896 | tf_op jit(solution)/shard_map/ppermute | solution.py:225
  283.5 3.2 %copy-start.4 = (bf16[7,576,1024]{2,1,0:T(8,128)(2,1)}, bf16[7,576,1024]{2,1,0:T(8,128)(2,1)S(1)}, u32[]{:S(2)}) copy-start(bf16[7,576,1024]{2,1,0:T(8,128)(2,1)S(1)} %collective-permute-done.refs_3_) | copy-start | bytes 24772612
  301.2 5.0 %collective-permute-start.2 = (bf16[1,576,1024]{2,1,0:T(8,128)(2,1)S(1)}, bf16[1,576,1024]{2,1,0:T(8,128)(2,1)}, u32[]{:S(2)}, u32[]{:S(2)}) collective-permute-start(bf16[1,576,1024]{2,1,0:T(8,128)(2,1)S(1)} %get-tuple-element.50), channel_id=1, source_target_pairs={{0,1},{1,0},{2,3},{3,2},{4,5},{5,4},{6,7},{7,6}} | collective-permute-start | bytes 3538952 | tf_op jit(solution)/shard_map/ppermute | solution.py:225

commit v5 on v4

--- a/solution.py
+++ b/solution.py
@@ -31,10 +31,10 @@
 GELU_LIN = 0.7978845608028654
 GELU_CUB = GELU_LIN * 0.044715
 ROW_TILE = 512
-UNIT = 2 * ROW_TILE
 FF_TILE = 512
-CHUNKS = (7, 2, 1)
-N_FIRST = 6
+CHUNKS = ((15, 768), (4, 1536), (1, 512))
+N_FIRST = 12
+VMEM_LIMIT = 67000000
 
 
 def gelu_half(pre_act):
@@ -43,41 +43,48 @@
     return half + half * jnp.tanh(inner)
 
 
-def pair_forward(pair, up_rows_of, w_down, hidden_ref):
-    ff_width = hidden_ref.shape[1]
-    for half, cols_in in enumerate(pair):
-        for start in range(0, ff_width, FF_TILE):
-            pre_act = jnp.dot(up_rows_of(start), cols_in, preferred_element_type=jnp.float32)
-            hidden_ref[half, start:start + FF_TILE, :] = gelu_half(pre_act).astype(jnp.bfloat16)
-    results = []
-    for half, cols_in in enumerate(pair):
-        branch = jnp.dot(w_down, hidden_ref[half], preferred_element_type=jnp.float32)
-        results.append((cols_in.astype(jnp.float32) + branch).astype(jnp.bfloat16))
-    return results
-
-
-def forward_kernel(is_short, has_prev, copies, n_state, base, n_own, *refs):
+def tile_forward(cols_in, w_up_t, w_down_t, hidden_ref, ff_tile):
+    for start in range(0, hidden_ref.shape[0], ff_tile):
+        rows = pl.ds(start, ff_tile)
+        pre_act = jnp.dot(w_up_t[rows, :], cols_in, preferred_element_type=jnp.float32)
+        hidden_ref[rows, :] = gelu_half(pre_act).astype(jnp.bfloat16)
+    branch = jnp.dot(w_down_t[...], hidden_ref[...], preferred_element_type=jnp.float32)
+    return (cols_in.astype(jnp.float32) + branch).astype(jnp.bfloat16)
+
+
+def tile_place(n_own, per_micro, owner, tile):
+    return owner * n_own + tile // per_micro, slice(None), pl.ds(pl.multiple_of(lax.rem(tile, per_micro) * ROW_TILE, ROW_TILE), ROW_TILE)
+
+
+def start_all(copies):
+    for copy in copies:
+        copy.start()
+
+
+def wait_all(copies):
+    for copy in copies:
+        copy.wait()
+
+
+def forward_kernel(has_prev, ff_tile, copies, n_state, base, n_own, per_micro, *refs):
     refs = list(refs)
-    x_ref, w_up_t, w_down_t = refs[:3]
+    x_ref, w_up_in, w_dn_in = refs[:3]
     refs = refs[3:]
     n_copy = len(copies)
     copy_refs, refs = refs[:n_copy], refs[n_copy:]
     state_in, refs = refs[:n_state], refs[n_state:]
     if has_prev:
         refs.pop(0)
-    out_ref, y_ref = refs[:2]
-    state_out, refs = refs[2:2 + n_state], refs[2 + n_state:]
-    hidden_ref, mid_ref, y_buf, y_sem, in_sem, out_sem, state_sem = refs[:7]
-    copy_bufs, state_buf = refs[7:7 + n_copy], refs[7 + n_copy:]
+    out_ref, y_ref, refs = refs[0], refs[1], refs[2:]
+    state_out, refs = refs[:n_state], refs[n_state:]
+    w_up_t, w_dn_t, hidden_ref, y_buf, y_sem, wt_sem, in_sem, out_sem, state_sem, *refs = refs
+    copy_bufs, state_buf = refs[:n_copy], refs[n_copy:]
     mine = lax.axis_index('stage')
     step, n_steps = pl.program_id(0), pl.num_programs(0)
     slot = lax.rem(step, 2)
 
-    def out_at(owner, unit):
-        return out_ref.at[owner * n_own + unit // 2, :, pl.ds(pl.multiple_of(lax.rem(unit, 2) * UNIT, UNIT), UNIT)]
-
     def y_copy(which):
-        return pltpu.make_async_copy(y_buf.at[which], out_at(mine, base + step), y_sem.at[which])
+        return pltpu.make_async_copy(y_buf.at[which], out_ref.at[tile_place(n_own, per_micro, mine, base + step)], y_sem.at[which])
 
     def enter(index):
         share = copies[index][3]
@@ -86,12 +93,16 @@
     def leave(index):
         from_peer, first, _, share = copies[index]
         owner = 1 - mine if from_peer else mine
-        return [pltpu.make_async_copy(copy_bufs[index].at[unit], out_at(owner, first + step * share + unit), out_sem.at[index, unit])
-                for unit in range(share)]
-
-    def state_copy(index, leaving):
-        src, dst = (state_buf[index], state_out[index]) if leaving else (state_in[index], state_buf[index])
-        return pltpu.make_async_copy(src, dst, state_sem.at[index])
+        return [pltpu.make_async_copy(copy_bufs[index].at[tile], out_ref.at[tile_place(n_own, per_micro, owner, first + step * share + tile)],
+                                      out_sem.at[index, tile]) for tile in range(share)]
+
+    def weight_copies(block):
+        return [pltpu.make_async_copy(src.at[block], dst.at[block], wt_sem.at[block, kind])
+                for kind, (src, dst) in enumerate(((w_up_in, w_up_t), (w_dn_in, w_dn_t)))]
+
+    def state_copies(leaving):
+        pairs = zip(state_buf, state_out) if leaving else zip(state_in, state_buf)
+        return [pltpu.make_async_copy(src, dst, state_sem.at[index]) for index, (src, dst) in enumerate(pairs)]
 
     def for_copies(action):
         for index in range(n_copy):
@@ -99,81 +110,48 @@
 
     def leave_start(index):
         enter(index).wait()
-        for copy in leave(index):
-            copy.start()
-
-    def leave_wait(index):
-        for copy in leave(index):
-            copy.wait()
+        start_all(leave(index))
+
+    @pl.when(step == 0)
+    def _():
+        start_all(weight_copies(0) + weight_copies(1) + state_copies(False))
 
     for_copies(lambda index: enter(index).start())
+    cols = x_ref[0]
+    for block in range(2):
+        pl.when(step == 0)(lambda: wait_all(weight_copies(block)))
+        cols = tile_forward(cols, w_up_t.at[block], w_dn_t.at[block], hidden_ref, ff_tile)
+        if block == 0:
+            for_copies(leave_start)
+
+    pl.when(step >= 2)(lambda: y_copy(slot).wait())
+    y_buf[slot] = cols
+    y_ref[0] = cols
+    y_copy(slot).start()
+    for_copies(lambda index: wait_all(leave(index)))
     if n_state:
-        @pl.when(step == 0)
-        def _():
-            for index in range(n_state):
-                state_copy(index, False).start()
-
         @pl.when(step == 1)
         def _():
-            for index in range(n_state):
-                state_copy(index, False).wait()
-                state_copy(index, True).start()
-
-    half_cols = UNIT // 2
-    sides = (slice(0, half_cols), slice(half_cols, UNIT))
-    pair = [x_ref[0, :, cols] for cols in sides]
-
-    def block_step(block, carry):
-        inputs = [mid_ref[:, cols] for cols in sides]
-        results = pair_forward(inputs, lambda start: w_up_t[block, start:start + FF_TILE, :], w_down_t[block], hidden_ref)
-        for half in range(2):
-            mid_ref[:, sides[half]] = results[half]
-        pl.when(block == 0)(lambda: for_copies(leave_start))
-        return carry
-
-    if is_short:
-        mid_ref[...] = x_ref[0]
-        lax.fori_loop(0, 2, block_step, 0)
-        pair = [mid_ref[:, cols] for cols in sides]
-    for block in range(0 if is_short else 2):
-        pair = pair_forward(pair, lambda start, block=block: w_up_t[block, start:start + FF_TILE, :], w_down_t[block], hidden_ref)
-        if block == 0:
-            for_copies(leave_start)
-
-    @pl.when(step >= 2)
-    def _():
-        y_copy(slot).wait()
-
-    for half in range(2):
-        cols = slice(half * half_cols, (half + 1) * half_cols)
-        y_buf[slot, :, cols] = pair[half]
-        y_ref[0, :, cols] = pair[half]
-    y_copy(slot).start()
-    for_copies(leave_wait)
+            wait_all(state_copies(False))
+            start_all(state_copies(True))
 
     @pl.when(step == n_steps - 1)
     def _():
         y_copy(slot).wait()
-        for index in range(n_state):
-            state_copy(index, True).wait()
-
-    @pl.when(jnp.logical_and(step == n_steps - 1, step >= 1))
-    def _():
-        y_copy(1 - slot).wait()
-
-
-def forward_chunk(base, n_chunk, micro_t, w_up_t, w_down_t, prev_out, copied, states):
+        wait_all(state_copies(True))
+
+    pl.when(jnp.logical_and(step == n_steps - 1, step >= 1))(lambda: y_copy(1 - slot).wait())
+
+
+def forward_chunk(base, n_chunk, ff_tile, micro_t, w_up_t, w_down_t, prev_out, copied, states):
     n_micro, width, n_rows = micro_t.shape
-    n_own = n_micro // 2
+    n_own, per_micro = n_micro // 2, n_rows // ROW_TILE
     ff_width = w_up_t.shape[1]
-    mine = lax.axis_index('stage')
     any_spec = pl.BlockSpec(memory_space=pl.ANY)
-    scalar = jnp.full((1,), mine * n_own, jnp.int32)
-    in_specs = [pl.BlockSpec((1, width, UNIT), lambda i, first: (first[0] + (base + i) // 2, 0, lax.rem(base + i, 2))),
-                pl.BlockSpec((2, ff_width, width), lambda i, first: (0, 0, 0)),
-                pl.BlockSpec((2, width, ff_width), lambda i, first: (0, 0, 0))]
+    scalar = jnp.full((1,), lax.axis_index('stage') * n_own, jnp.int32)
+    in_specs = [pl.BlockSpec((1, width, ROW_TILE), lambda i, first: (first[0] + (base + i) // per_micro, 0, lax.rem(base + i, per_micro)))]
     operands = [micro_t, w_up_t, w_down_t] + [array for array, _, _ in copied] + list(states)
-    in_specs += [any_spec] * (len(copied) + len(states))
+    in_specs += [any_spec] * (len(operands) - 1)
     aliases = {}
     if prev_out is not None:
         in_specs.append(any_spec)
@@ -181,54 +159,69 @@
         aliases = {len(operands): 0}
     copies = [(from_peer, first, array.shape[0], pl.cdiv(array.shape[0], n_chunk)) for array, from_peer, first in copied]
     max_share = max([1] + [share for *_, share in copies])
+    dma = pltpu.SemaphoreType.DMA
 
     def body(first, *refs):
-        forward_kernel(n_chunk <= 2, prev_out is not None, copies, len(states), base, n_own, *refs)
-
-    flops = 8 * n_chunk * UNIT * width * ff_width
+        forward_kernel(prev_out is not None, ff_tile, copies, len(states), base, n_own, per_micro, *refs)
+
     return pl.pallas_call(
         body,
         grid_spec=pltpu.PrefetchScalarGridSpec(
             num_scalar_prefetch=1, grid=(n_chunk,), in_specs=in_specs,
-            out_specs=[any_spec, pl.BlockSpec((1, width, UNIT), lambda i, first: (i, 0, 0))] + [any_spec] * len(states),
-            scratch_shapes=[pltpu.VMEM((2, ff_width, UNIT // 2), jnp.bfloat16), pltpu.VMEM((width, UNIT), jnp.bfloat16),
-                            pltpu.VMEM((2, width, UNIT), jnp.bfloat16),
-                            pltpu.SemaphoreType.DMA((2,)), pltpu.SemaphoreType.DMA((2,)), pltpu.SemaphoreType.DMA((2, max_share)),
-                            pltpu.SemaphoreType.DMA((6,))]
-            + [pltpu.VMEM((share, width, UNIT), jnp.bfloat16) for *_, share in copies]
+            out_specs=[any_spec, pl.BlockSpec((1, width, ROW_TILE), lambda i, first: (i, 0, 0))] + [any_spec] * len(states),
+            scratch_shapes=[pltpu.VMEM(w_up_t.shape, jnp.bfloat16), pltpu.VMEM(w_down_t.shape, jnp.bfloat16),
+                            pltpu.VMEM((ff_width, ROW_TILE), jnp.bfloat16), pltpu.VMEM((2, width, ROW_TILE), jnp.bfloat16),
+                            dma((2,)), dma((2, 2)), dma((2,)), dma((2, max_share)), dma((6,))]
+            + [pltpu.VMEM((share, width, ROW_TILE), jnp.bfloat16) for *_, share in copies]
             + [pltpu.VMEM(array.shape, array.dtype) for array in states]),
         out_shape=[jax.ShapeDtypeStruct(micro_t.shape, jnp.bfloat16),
-                   jax.ShapeDtypeStruct((n_chunk, width, UNIT), jnp.bfloat16)]
+                   jax.ShapeDtypeStruct((n_chunk, width, ROW_TILE), jnp.bfloat16)]
         + [jax.ShapeDtypeStruct(array.shape, array.dtype) for array in states],
         input_output_aliases=aliases,
-        compiler_params=pltpu.CompilerParams(dimension_semantics=("arbitrary",), vmem_limit_bytes=50 * 1024 * 1024),
-        cost_estimate=pl.CostEstimate(flops=flops, bytes_accessed=4 * n_chunk * UNIT * width, transcendentals=0),
+        compiler_params=pltpu.CompilerParams(dimension_semantics=("arbitrary",), vmem_limit_bytes=VMEM_LIMIT),
+        cost_estimate=pl.CostEstimate(flops=8 * n_chunk * ROW_TILE * width * ff_width, bytes_accessed=n_chunk * ROW_TILE * width,
+                                      transcendentals=0),
         name=f"fwd_{base}",
     )(scalar, *operands)
 
 
+def place_tiles(out, tiles, first, n_own):
+    count, per_micro = tiles.shape[0], out.shape[2] // ROW_TILE
+    any_spec = pl.BlockSpec(memory_space=pl.ANY)
+
+    def body(tiles_ref, old_ref, out_ref, buf, in_sem, out_sem):
+        owner = 1 - lax.axis_index('stage')
+        enter = [pltpu.make_async_copy(tiles_ref.at[tile], buf.at[tile], in_sem.at[tile]) for tile in range(count)]
+        leave = [pltpu.make_async_copy(buf.at[tile], out_ref.at[tile_place(n_own, per_micro, owner, first + tile)], out_sem.at[tile])
+                 for tile in range(count)]
+        start_all(enter)
+        for tile in range(count):
+            enter[tile].wait()
+            leave[tile].start()
+        wait_all(leave)
+
+    return pl.pallas_call(
+        body, in_specs=[any_spec] * 2, out_specs=any_spec, out_shape=jax.ShapeDtypeStruct(out.shape, out.dtype),
+        scratch_shapes=[pltpu.VMEM(tiles.shape, tiles.dtype), pltpu.SemaphoreType.DMA((count,)), pltpu.SemaphoreType.DMA((count,))],
+        input_output_aliases={1: 0}, compiler_params=pltpu.CompilerParams(vmem_limit_bytes=VMEM_LIMIT), name=f"place_{first}")(tiles, out)
+
+
 def forward_rest(micro_t, w_up_t, w_down_t, own_first, peer_first, states):
     n_own = micro_t.shape[0] // 2
-    swap = [(0, 1), (1, 0)]
-    mine = lax.axis_index('stage')
     out, base = None, own_first.shape[0]
     received, results = [], []
-    for number, n_chunk in enumerate(CHUNKS):
+    for number, (n_chunk, ff_tile) in enumerate(CHUNKS):
         copied, passed = [], []
         if number == 0:
             copied, passed = [(own_first, False, 0), (peer_first, True, 0)], states
         elif number >= 2:
-            copied = [received[number - 2]]
-            received[number - 2] = None
-        out, part, *handed = forward_chunk(base, n_chunk, micro_t, w_up_t, w_down_t, out, copied, passed)
+            copied = [received.pop(0)]
+        out, part, *handed = forward_chunk(base, n_chunk, ff_tile, micro_t, w_up_t, w_down_t, out, copied, passed)
         results += handed
-        received.append((lax.ppermute(part, 'stage', swap), True, base))
+        received.append((lax.ppermute(part, 'stage', [(0, 1), (1, 0)]), True, base))
         base += n_chunk
-    for item in received:
-        if item is not None:
-            for index in range(item[0].shape[0]):
-                unit = item[2] + index
-                out = lax.dynamic_update_slice(out, item[0][index:index + 1], ((1 - mine) * n_own + unit // 2, 0, unit % 2 * UNIT))
+    for tiles, _, first in received:
+        out = place_tiles(out, tiles, first, n_own)
     return jnp.swapaxes(out, 1, 2), results
 
 
@@ -414,12 +407,17 @@
     for copy in loads[6:]:
         copy.start()
 
-    def x_load(pair):
-        return pltpu.make_async_copy(micro_in.at[core * n_own + pair // 2, :, cols_of(lax.rem(pair, 2), UNIT)],
-                                     acts.at[lax.rem(pair, 2)], tile_sem.at[0, lax.rem(pair, 2)])
-
-    for pair in range(2):
-        x_load(pair).start()
+    n_slot = 2 * half_rows // ROW_TILE
+    per_micro = micro_in.shape[2] // ROW_TILE
+
+    def x_slot(tile):
+        slot = lax.rem(tile, n_slot)
+        return acts.at[slot // 2, :, cols_of(lax.rem(slot, 2), ROW_TILE)]
+
+    def x_load(tile):
+        return pltpu.make_async_copy(micro_in.at[tile_place(n_own, per_micro, core, tile)], x_slot(tile), tile_sem.at[0, lax.rem(tile, n_slot)])
+
+    start_all([x_load(tile) for tile in range(n_slot)])
 
     up_first[0][0].wait_recv()
     cols = cols_of(halves[0], GRAD_HALF)
@@ -546,66 +544,56 @@
         return [pltpu.make_async_copy(turned, w_up_out.at[block], store_sem.at[6 + block]),
                 pltpu.make_async_copy(wts.at[block, 1], w_dn_out.at[block], store_sem.at[8 + block])]
 
-    def unit_forward(pair, block):
-        return pair_forward(pair, lambda start: turned[start:start + FF_TILE, :], wts[block, 1], hidden_ref)
-
     n_first = own_first.shape[0]
     per_row = ff_width // ROW_TILE
-    sides = (slice(0, ROW_TILE), slice(ROW_TILE, UNIT))
 
     def mid_slot(tile):
         row = tile // per_row
         return row // 2, lax.rem(row, 2), slice(None), cols_of(lax.rem(tile, per_row), ROW_TILE)
 
     turned[...] = wts[0, 0].T
-    for copy in weights_out(0):
-        copy.start()
-
-    def first_block(pair, carry):
-        for number, action in ((2, gather_relay), (3, gather_near), (4, gather_far)):
-            pl.when(jnp.logical_and(core == 1, pair == number))(action)
-        x_load(pair).wait()
-        slot = lax.rem(pair, 2)
-        mids = unit_forward([acts[slot, :, cols] for cols in sides], 0)
-        for half in range(2):
-            sums[mid_slot(2 * pair + half)] = mids[half].astype(jnp.float32)
-
-        @pl.when(pair + 2 < n_first)
-        def _():
-            x_load(pair + 2).start()
+    start_all(weights_out(0))
+
+    def first_block(tile, carry):
+        for number, action in ((4, gather_relay), (5, gather_near), (7, gather_far)):
+            pl.when(jnp.logical_and(core == 1, tile == number))(action)
+        x_load(tile).wait()
+        mid = tile_forward(x_slot(tile)[...], turned, wts.at[0, 1], hidden_ref, FF_TILE)
+        sums[mid_slot(tile)] = mid.astype(jnp.float32)
+        pl.when(tile + n_slot < n_first)(lambda: x_load(tile + n_slot).start())
         return carry
 
     lax.fori_loop(0, n_first, first_block, 0)
     pl.when(core == 0)(gather_peer)
     weights_out(0)[0].wait()
     turned[...] = wts[1, 0].T
-    for copy in weights_out(1):
-        copy.start()
-
-    def y_out(pair):
-        keep = pltpu.make_async_copy(grad, own_first.at[pair], tile_sem.at[1, 0])
-        give = pltpu.make_async_remote_copy(src_ref=grad, dst_ref=peer_first.at[pair], send_sem=tile_sem.at[1, 1],
-                                            recv_sem=recv_sem.at[51 + pair], device_id=to_peer, device_id_type=MESH_ID)
+    start_all(weights_out(1))
+
+    def y_out(tile):
+        slot = lax.rem(tile, 2)
+        y_slot = grad.at[:, cols_of(slot, ROW_TILE)]
+        keep = pltpu.make_async_copy(y_slot, own_first.at[tile], tile_sem.at[1, slot])
+        give = pltpu.make_async_remote_copy(src_ref=y_slot, dst_ref=peer_first.at[tile], send_sem=tile_sem.at[2, slot],
+                                            recv_sem=recv_sem.at[51 + tile], device_id=to_peer, device_id_type=MESH_ID)
         return keep, give
 
-    def y_wait(pair):
-        keep, give = y_out(pair)
+    def y_wait(tile):
+        keep, give = y_out(tile)
         keep.wait()
         give.wait_send()
 
-    def second_block(pair, carry):
-        results = unit_forward([sums[mid_slot(2 * pair + half)].astype(jnp.bfloat16) for half in range(2)], 1)
-        pl.when(pair >= 1)(lambda: y_wait(pair - 1))
-        for half in range(2):
-            grad[:, sides[half]] = results[half]
-        for copy in y_out(pair):
-            copy.start()
+    def second_block(tile, carry):
+        result = tile_forward(sums[mid_slot(tile)].astype(jnp.bfloat16), turned, wts.at[1, 1], hidden_ref, FF_TILE)
+        pl.when(tile >= 2)(lambda: y_wait(tile - 2))
+        grad[:, cols_of(lax.rem(tile, 2), ROW_TILE)] = result
+        start_all(y_out(tile))
         return carry
 
     lax.fori_loop(0, n_first, second_block, 0)
+    y_wait(n_first - 2)
     y_wait(n_first - 1)
-    for pair in range(n_first):
-        y_out(pair)[1].wait_recv()
+    for tile in range(n_first):
+        y_out(tile)[1].wait_recv()
 
     for copy in [up_x, up_y, up_relay, dn_x, dn_y, dn_relay] + up_peer + dn_peer:
         copy.wait_send()
@@ -620,7 +608,7 @@
     up_rows, dn_cols = arrays[0].shape[0], arrays[1].shape[1]
     f32, bf16 = jnp.float32, jnp.bfloat16
     up_state, dn_state = jax.ShapeDtypeStruct((up_rows, ff_width), f32), jax.ShapeDtypeStruct((width, dn_cols), f32)
-    first = jax.ShapeDtypeStruct((N_FIRST, width, UNIT), bf16)
+    first = jax.ShapeDtypeStruct((N_FIRST, width, ROW_TILE), bf16)
     any_spec = pl.BlockSpec(memory_space=pl.ANY)
     smem_spec = pl.BlockSpec(memory_space=pltpu.SMEM)
     n_sem = 51 + N_FIRST
@@ -628,7 +616,7 @@
     def body(*refs):
         update_kernel(n_data, *refs)
 
-    flops = 20 * half_rows * width * ff_width + 8 * N_FIRST * UNIT * width * ff_width
+    flops = 20 * half_rows * width * ff_width + 8 * N_FIRST * ROW_TILE * width * ff_width
     return pl.pallas_call(
         body,
         in_specs=[any_spec] * 13 + [smem_spec] * 2,
@@ -641,10 +629,10 @@
             pltpu.VMEM((half_rows, ff_width), bf16), pltpu.VMEM((2, 2, width, ff_width), f32), pltpu.VMEM((2, width, ff_width), f32),
             pltpu.VMEM((2, up_rows, ff_width), f32), pltpu.VMEM((2, width, dn_cols), f32),
             pltpu.VMEM((up_rows, ff_width), f32), pltpu.VMEM((width, dn_cols), f32), pltpu.VMEM((2 * n_data, 8, 128), f32),
-            pltpu.VMEM((ff_width, width), bf16), pltpu.VMEM((2, ff_width, ROW_TILE), bf16),
+            pltpu.VMEM((ff_width, width), bf16), pltpu.VMEM((ff_width, ROW_TILE), bf16),
             pltpu.SemaphoreType.DMA((n_sem,)), pltpu.SemaphoreType.DMA((n_sem,)), pltpu.SemaphoreType.DMA((12,)),
-            pltpu.SemaphoreType.DMA((10,)), pltpu.SemaphoreType.DMA((2, 2))],
-        compiler_params=pltpu.CompilerParams(collective_id=0, has_side_effects=True, vmem_limit_bytes=67000000),
+            pltpu.SemaphoreType.DMA((10,)), pltpu.SemaphoreType.DMA((3, 4))],
+        compiler_params=pltpu.CompilerParams(collective_id=0, has_side_effects=True, vmem_limit_bytes=VMEM_LIMIT),
         cost_estimate=pl.CostEstimate(flops=flops, bytes_accessed=60000000, transcendentals=0),
         name="update",
     )(*arrays, learn_rate.reshape(1), max_norm.reshape(1))

time: 309 us -> 310 us (level)
  Pallas kernels: 291 us -> 307 us
  local copies, waits for them, and re-layouts: 14.9 us -> 0 us
    pallas_call x3, Pallas kernels: 119 us -> 130 us  [forward_chunk(): pl.pallas_call(body, grid_spec=pltpu.PrefetchScalarGridSpec(num_scalar_pr...]
    unnamed x10 -> x0, local copies, waits for them, and re-layouts: 7.84 us -> none
    dynamic_update_slice x3 -> x0, local copies, waits for them, and re-layouts: 7.09 us -> none  [forward_rest(): lax.dynamic_update_slice(out, item[0][index:index + 1], ((1 - mine) * n_o...]
    pallas_call x0 -> x2, Pallas kernels: none -> 4.43 us  [place_tiles(): pl.pallas_call(body, in_specs=[any_spec] * 2, out_specs=any_spec, out_sha...]
  transfers between devices with their start and end apart: 3 -> 3, of which waited for: 0 -> 0; matrix products, arithmetic and copies ran while one was open for 2% -> 0% of each run, Pallas kernels for 12% -> 14%
where the time goes in v5:
time: 310 us
  Pallas kernels  307 us (99%)
    pallas_call x1, Pallas kernels, update_weights(): pl.pallas_call(body, in_specs=[any_spec] * 13 + [smem_spec] * 2, out_spec...  173 us
    pallas_call x3, Pallas kernels, forward_chunk(): pl.pallas_call(body, grid_spec=pltpu.PrefetchScalarGridSpec(num_scalar_pr...  130 us
  transfers between devices with their start and end apart: 3, of which 0 were waited for; matrix products, arithmetic and copies ran while one was open for 0% of the time, Pallas kernels for 14%

profile of v5, /device:TPU:0, one launch (start us, length us, event | category | flops | bytes accessed | tf_op | source)
XLA Modules:
  0.0 310.0 jit_solution(9533911590331215945)
XLA Ops:
  1.9 172.8 %update.1 = (f32[144,1536]{1,0:T(8,128)}, f32[576,384]{1,0:T(8,128)}, f32[144,1536]{1,0:T(8,128)}, f32[144,1536]{1,0:T(8,128)}, f32[576,384]{1,0:T(8,128)}, /*in...) custom-call(f32[144,1536]{1,0:T(8,128)} %bitcast.54, ...), custom_call_target="tpu_custom_call" | custom-call | flops 61605937152 | bytes 60000000 | tf_op jit(solution)/shard_map/update/pallas_call | solution.py:620
  174.7 89.8 %fwd_12.1 = (bf16[16,576,2048]{2,1,0:T(8,128)(2,1)}, bf16[15,576,512]{2,1,0:T(8,128)(2,1)}, f32[144,1536]{1,0:T(8,128)}, f32[576,384]{1,0:T(8,128)}, f32[144,153...) custom-call(s32[1]{0:T(128)} %bitcast.first, bf16[16,576,2048]{2,1,0:T(8,128)(2,1)} %bitcast.45, ...), custom_call_target="tpu_custom_call" | custom-call | flops 54358179840 | bytes 4423680 | tf_op jit(solution)/shard_map/fwd_12/pallas_call | solution.py:167
  264.5 0.2 collective-permute-start
  264.7 28.5 %fwd_27.1 = (bf16[16,576,2048]{2,1,0:T(8,128)(2,1)}, bf16[4,576,512]{2,1,0:T(8,128)(2,1)}) custom-call(s32[1]{0:T(128)} %bitcast.first, bf16[16,576,2048]{2,1,0:T(8,128)(2,1)} %bitcast.46, bf16[2,1536,576]{2,1,0:T(8,128)(2,1)} %get-tuple-element.29.refs_1_, bf16[2,576,1536]{2,1,0:T(8,128)(2,1)} %get-tuple-element.30.refs_2_, ...), custom_call_target="tpu_custom_call", output_to_operand_aliasing={{0}: (4, {})} | custom-call | flops 14495514624 | bytes 1179648 | tf_op jit(solution)/shard_map/fwd_27/pallas_call | solution.py:167
  293.2 0.3 collective-permute-start.2
  293.5 0.0 collective-permute-done.refs_3_
  293.5 11.6 %fwd_31.1 = (bf16[16,576,2048]{2,1,0:T(8,128)(2,1)}, bf16[1,576,512]{2,1,0:T(8,128)(2,1)}) custom-call(s32[1]{0:T(128)} %bitcast.first, bf16[16,576,2048]{2,1,0:T(8,128)(2,1)} %bitcast.47, bf16[2,1536,576]{2,1,0:T(8,128)(2,1)} %get-tuple-element.29.refs_1_, bf16[2,576,1536]{2,1,0:T(8,128)(2,1)} %get-tuple-element.30.refs_2_, ...), custom_call_target="tpu_custom_call", output_to_operand_aliasing={{0}: (5, {})} | custom-call | flops 3623878656 | bytes 294912 | tf_op jit(solution)/shard_map/fwd_31/pallas_call | solution.py:167
  305.1 0.3 collective-permute-start.1
  305.4 0.0 collective-permute-done.2.tiles_ref
  305.4 2.5 place_27.1.old_ref
  307.9 0.0 collective-permute-done.1.tiles_ref
  307.9 1.9 place_31.1
Async XLA Ops:
  264.5 29.0 %collective-permute-start = (bf16[15,576,512]{2,1,0:T(8,128)(2,1)}, bf16[15,576,512]{2,1,0:T(8,128)(2,1)}, u32[]{:S(2)}, u32[]{:S(2)}) collective-permute-start(bf16[15,576,512]{2,1,0:T(8,128)(2,1)} %get-tuple-element.45), channel_id=1, source_target_pairs={{0,1},{1,0},{2,3},{3,2},{4,5},{5,4},{6,7},{7,6}} | collective-permute-start | bytes 26542088 | tf_op jit(solution)/shard_map/ppermute | solution.py:221
  293.2 12.2 %collective-permute-start.2 = (bf16[4,576,512]{2,1,0:T(8,128)(2,1)}, bf16[4,576,512]{2,1,0:T(8,128)(2,1)}, u32[]{:S(2)}, u32[]{:S(2)}) collective-permute-start(bf16[4,576,512]{2,1,0:T(8,128)(2,1)} %get-tuple-element.49), channel_id=1, source_target_pairs={{0,1},{1,0},{2,3},{3,2},{4,5},{5,4},{6,7},{7,6}} | collective-permute-start | bytes 7077896 | tf_op jit(solution)/shard_map/ppermute | solution.py:221
  305.1 2.8 collective-permute-start.1

commit v6 on v5

--- a/solution.py
+++ b/solution.py
@@ -31,8 +31,8 @@
 GELU_LIN = 0.7978845608028654
 GELU_CUB = GELU_LIN * 0.044715
 ROW_TILE = 512
-FF_TILE = 512
-CHUNKS = ((15, 768), (4, 1536), (1, 512))
+FF_TILE = 256
+CHUNKS = ((12, 256), (5, 128), (3, 384))
 N_FIRST = 12
 VMEM_LIMIT = 67000000
 

time: 310 us -> 292 us (0.942)
  Pallas kernels: 307 us -> 288 us
    pallas_call x3, Pallas kernels: 130 us -> 115 us  [forward_chunk(): pl.pallas_call(body, grid_spec=pltpu.PrefetchScalarGridSpec(num_scalar_pr...]
    pallas_call x1, Pallas kernels: 173 us -> 168 us  [update_weights(): pl.pallas_call(body, in_specs=[any_spec] * 13 + [smem_spec] * 2, out_spec...]
  transfers between devices with their start and end apart: 3 -> 3, of which waited for: 0 -> 1; matrix products, arithmetic and copies ran while one was open for 0% -> 0% of each run, Pallas kernels for 14% -> 18%
where the time goes in v6:
time: 292 us
  Pallas kernels  288 us (99%)
    pallas_call x1, Pallas kernels, update_weights(): pl.pallas_call(body, in_specs=[any_spec] * 13 + [smem_spec] * 2, out_spec...  168 us
    pallas_call x3, Pallas kernels, forward_chunk(): pl.pallas_call(body, grid_spec=pltpu.PrefetchScalarGridSpec(num_scalar_pr...  115 us
  transfers between devices with their start and end apart: 3, of which 1 were waited for; matrix products, arithmetic and copies ran while one was open for 0% of the time, Pallas kernels for 18%

profile of v6, /device:TPU:0, one launch (start us, length us, event | category | flops | bytes accessed | tf_op | source)
XLA Modules:
  0.0 291.5 jit_solution(13641678653447584610)
XLA Ops:
  1.9 167.5 %update.1 = (f32[144,1536]{1,0:T(8,128)}, f32[576,384]{1,0:T(8,128)}, f32[144,1536]{1,0:T(8,128)}, f32[144,1536]{1,0:T(8,128)}, f32[576,384]{1,0:T(8,128)}, /*in...) custom-call(f32[144,1536]{1,0:T(8,128)} %bitcast.54, ...), custom_call_target="tpu_custom_call" | custom-call | flops 61605937152 | bytes 60000000 | tf_op jit(solution)/shard_map/update/pallas_call | solution.py:620
  169.5 65.4 %fwd_12.1 = (bf16[16,576,2048]{2,1,0:T(8,128)(2,1)}, bf16[12,576,512]{2,1,0:T(8,128)(2,1)}, f32[144,1536]{1,0:T(8,128)}, f32[576,384]{1,0:T(8,128)}, f32[144,153...) custom-call(s32[1]{0:T(128)} %bitcast.first, bf16[16,576,2048]{2,1,0:T(8,128)(2,1)} %bitcast.45, ...), custom_call_target="tpu_custom_call" | custom-call | flops 43486543872 | bytes 3538944 | tf_op jit(solution)/shard_map/fwd_12/pallas_call | solution.py:167
  234.9 0.2 collective-permute-start
  235.2 29.0 %fwd_24.1 = (bf16[16,576,2048]{2,1,0:T(8,128)(2,1)}, bf16[5,576,512]{2,1,0:T(8,128)(2,1)}) custom-call(s32[1]{0:T(128)} %bitcast.first, bf16[16,576,2048]{2,1,0:T(8,128)(2,1)} %bitcast.46, bf16[2,1536,576]{2,1,0:T(8,128)(2,1)} %get-tuple-element.29.refs_1_, bf16[2,576,1536]{2,1,0:T(8,128)(2,1)} %get-tuple-element.30.refs_2_, ...), custom_call_target="tpu_custom_call", output_to_operand_aliasing={{0}: (4, {})} | custom-call | flops 18119393280 | bytes 1474560 | tf_op jit(solution)/shard_map/fwd_24/pallas_call | solution.py:167
  264.1 0.3 collective-permute-start.2
  264.4 0.0 collective-permute-done.refs_3_
  264.4 21.0 %fwd_29.1 = (bf16[16,576,2048]{2,1,0:T(8,128)(2,1)}, bf16[3,576,512]{2,1,0:T(8,128)(2,1)}) custom-call(s32[1]{0:T(128)} %bitcast.first, bf16[16,576,2048]{2,1,0:T(8,128)(2,1)} %bitcast.47, bf16[2,1536,576]{2,1,0:T(8,128)(2,1)} %get-tuple-element.29.refs_1_, bf16[2,576,1536]{2,1,0:T(8,128)(2,1)} %get-tuple-element.30.refs_2_, ...), custom_call_target="tpu_custom_call", output_to_operand_aliasing={{0}: (5, {})} | custom-call | flops 10871635968 | bytes 884736 | tf_op jit(solution)/shard_map/fwd_29/pallas_call | solution.py:167
  285.4 0.3 collective-permute-start.1
  285.7 0.0 collective-permute-done.2.tiles_ref
  285.7 2.7 place_24.1.old_ref
  288.4 0.6 collective-permute-done.1.tiles_ref
  289.0 2.3 place_29.1
Async XLA Ops:
  234.9 29.5 %collective-permute-start = (bf16[12,576,512]{2,1,0:T(8,128)(2,1)}, bf16[12,576,512]{2,1,0:T(8,128)(2,1)}, u32[]{:S(2)}, u32[]{:S(2)}) collective-permute-start(bf16[12,576,512]{2,1,0:T(8,128)(2,1)} %get-tuple-element.45), channel_id=1, source_target_pairs={{0,1},{1,0},{2,3},{3,2},{4,5},{5,4},{6,7},{7,6}} | collective-permute-start | bytes 21233672 | tf_op jit(solution)/shard_map/ppermute | solution.py:221
  264.1 21.5 %collective-permute-start.2 = (bf16[5,576,512]{2,1,0:T(8,128)(2,1)}, bf16[5,576,512]{2,1,0:T(8,128)(2,1)}, u32[]{:S(2)}, u32[]{:S(2)}) collective-permute-start(bf16[5,576,512]{2,1,0:T(8,128)(2,1)} %get-tuple-element.49), channel_id=1, source_target_pairs={{0,1},{1,0},{2,3},{3,2},{4,5},{5,4},{6,7},{7,6}} | collective-permute-start | bytes 8847368 | tf_op jit(solution)/shard_map/ppermute | solution.py:221
  285.4 3.7 %collective-permute-start.1 = (bf16[3,576,512]{2,1,0:T(8,128)(2,1)}, bf16[3,576,512]{2,1,0:T(8,128)(2,1)}, u32[]{:S(2)}, u32[]{:S(2)}) collective-permute-start(bf16[3,576,512]{2,1,0:T(8,128)(2,1)} %get-tuple-element.48), channel_id=1, source_target_pairs={{0,1},{1,0},{2,3},{3,2},{4,5},{5,4},{6,7},{7,6}} | collective-permute-start | bytes 5308424 | tf_op jit(solution)/shard_map/ppermute | solution.py:221

commit v7 on v6

--- a/solution.py
+++ b/solution.py
@@ -32,7 +32,7 @@
 GELU_CUB = GELU_LIN * 0.044715
 ROW_TILE = 512
 FF_TILE = 256
-CHUNKS = ((12, 256), (5, 128), (3, 384))
+CHUNKS = ((12, 256), (5, 256), (3, 512))
 N_FIRST = 12
 VMEM_LIMIT = 67000000
 
@@ -86,15 +86,17 @@
     def y_copy(which):
         return pltpu.make_async_copy(y_buf.at[which], out_ref.at[tile_place(n_own, per_micro, mine, base + step)], y_sem.at[which])
 
-    def enter(index):
-        share = copies[index][3]
-        return pltpu.make_async_copy(copy_refs[index].at[pl.ds(step * share, share)], copy_bufs[index], in_sem.at[index])
-
-    def leave(index):
+    def enter(index, turn):
+        _, _, _, share = copies[index]
+        slot = lax.rem(turn, 2)
+        return pltpu.make_async_copy(copy_refs[index].at[pl.ds(turn * share, share)], copy_bufs[index].at[slot], in_sem.at[index, slot])
+
+    def leave(index, turn):
         from_peer, first, _, share = copies[index]
+        slot = lax.rem(turn, 2)
         owner = 1 - mine if from_peer else mine
-        return [pltpu.make_async_copy(copy_bufs[index].at[tile], out_ref.at[tile_place(n_own, per_micro, owner, first + step * share + tile)],
-                                      out_sem.at[index, tile]) for tile in range(share)]
+        return [pltpu.make_async_copy(copy_bufs[index].at[slot, tile], out_ref.at[tile_place(n_own, per_micro, owner, first + turn * share + tile)],
+                                      out_sem.at[index, slot, tile]) for tile in range(share)]
 
     def weight_copies(block):
         return [pltpu.make_async_copy(src.at[block], dst.at[block], wt_sem.at[block, kind])
@@ -104,43 +106,39 @@
         pairs = zip(state_buf, state_out) if leaving else zip(state_in, state_buf)
         return [pltpu.make_async_copy(src, dst, state_sem.at[index]) for index, (src, dst) in enumerate(pairs)]
 
-    def for_copies(action):
+    def for_copies(turn, action):
         for index in range(n_copy):
-            pl.when(step * copies[index][3] < copies[index][2])(functools.partial(action, index))
-
-    def leave_start(index):
-        enter(index).wait()
-        start_all(leave(index))
-
-    @pl.when(step == 0)
-    def _():
-        start_all(weight_copies(0) + weight_copies(1) + state_copies(False))
-
-    for_copies(lambda index: enter(index).start())
-    cols = x_ref[0]
-    for block in range(2):
-        pl.when(step == 0)(lambda: wait_all(weight_copies(block)))
-        cols = tile_forward(cols, w_up_t.at[block], w_dn_t.at[block], hidden_ref, ff_tile)
-        if block == 0:
-            for_copies(leave_start)
-
+            pl.when(jnp.logical_and(turn >= 0, turn * copies[index][3] < copies[index][2]))(functools.partial(action, index, turn))
+
+    def leave_start(index, turn):
+        enter(index, turn).wait()
+        start_all(leave(index, turn))
+
+    pl.when(step == 0)(lambda: start_all(weight_copies(0) + weight_copies(1) + state_copies(False)))
+    for_copies(step - 1, leave_start)
+    for_copies(step - 2, lambda index, turn: wait_all(leave(index, turn)))
+    for_copies(step, lambda index, turn: enter(index, turn).start())
     pl.when(step >= 2)(lambda: y_copy(slot).wait())
-    y_buf[slot] = cols
-    y_ref[0] = cols
-    y_copy(slot).start()
-    for_copies(lambda index: wait_all(leave(index)))
     if n_state:
         @pl.when(step == 1)
         def _():
             wait_all(state_copies(False))
             start_all(state_copies(True))
 
+    pl.when(step == 0)(lambda: wait_all(weight_copies(0) + weight_copies(1)))
+    cols = x_ref[0]
+    for block in range(2):
+        cols = tile_forward(cols, w_up_t.at[block], w_dn_t.at[block], hidden_ref.at[block], ff_tile)
+    y_buf[slot] = cols
+    y_ref[0] = cols
+    y_copy(slot).start()
+
     @pl.when(step == n_steps - 1)
     def _():
+        for_copies(step - 1, lambda index, turn: wait_all(leave(index, turn)))
         y_copy(slot).wait()
+        y_copy(1 - slot).wait()
         wait_all(state_copies(True))
-
-    pl.when(jnp.logical_and(step == n_steps - 1, step >= 1))(lambda: y_copy(1 - slot).wait())
 
 
 def forward_chunk(base, n_chunk, ff_tile, micro_t, w_up_t, w_down_t, prev_out, copied, states):
@@ -157,7 +155,11 @@
         in_specs.append(any_spec)
         operands.append(prev_out)
         aliases = {len(operands): 0}
-    copies = [(from_peer, first, array.shape[0], pl.cdiv(array.shape[0], n_chunk)) for array, from_peer, first in copied]
+    copies = []
+    for array, from_peer, first in copied:
+        count = array.shape[0]
+        share = min(size for size in range(1, count + 1) if count % size == 0 and count // size < n_chunk)
+        copies.append((from_peer, first, count, share))
     max_share = max([1] + [share for *_, share in copies])
     dma = pltpu.SemaphoreType.DMA
 
@@ -170,9 +172,9 @@
             num_scalar_prefetch=1, grid=(n_chunk,), in_specs=in_specs,
             out_specs=[any_spec, pl.BlockSpec((1, width, ROW_TILE), lambda i, first: (i, 0, 0))] + [any_spec] * len(states),
             scratch_shapes=[pltpu.VMEM(w_up_t.shape, jnp.bfloat16), pltpu.VMEM(w_down_t.shape, jnp.bfloat16),
-                            pltpu.VMEM((ff_width, ROW_TILE), jnp.bfloat16), pltpu.VMEM((2, width, ROW_TILE), jnp.bfloat16),
-                            dma((2,)), dma((2, 2)), dma((2,)), dma((2, max_share)), dma((6,))]
-            + [pltpu.VMEM((share, width, ROW_TILE), jnp.bfloat16) for *_, share in copies]
+                            pltpu.VMEM((2, ff_width, ROW_TILE), jnp.bfloat16), pltpu.VMEM((2, width, ROW_TILE), jnp.bfloat16),
+                            dma((2,)), dma((2, 2)), dma((2, 2)), dma((2, 2, max_share)), dma((6,))]
+            + [pltpu.VMEM((2, share, width, ROW_TILE), jnp.bfloat16) for *_, share in copies]
             + [pltpu.VMEM(array.shape, array.dtype) for array in states]),
         out_shape=[jax.ShapeDtypeStruct(micro_t.shape, jnp.bfloat16),
                    jax.ShapeDtypeStruct((n_chunk, width, ROW_TILE), jnp.bfloat16)]
@@ -267,13 +269,13 @@
 
     to_peer, to_x, to_y = (chip, peer), (chip_x, core), (chip_y, core)
 
+    up_state = [part.at[0, index * up_rows:(index + 1) * up_rows] for index in range(3)]
+    dn_state = [part.at[1, :, index * dn_cols:(index + 1) * dn_cols] for index in range(3)]
     loads = [pltpu.make_async_copy(src, dst, load_sem.at[index]) for index, (src, dst) in enumerate([
         (grad_in.at[:, cols_of(core, half_rows)], grad), (acts_in.at[:, cols_of(core, half_rows)], acts.at[core]),
         (cmp_up, wts.at[core, 0]), (cmp_dn, wts.at[core, 1]),
         (acc_up, sums.at[core, 0]), (acc_dn, sums.at[core, 1]),
-        (mst_up, part.at[0, 0:up_rows]), (mo1_up, part.at[0, up_rows:2 * up_rows]), (mo2_up, part.at[0, 2 * up_rows:3 * up_rows]),
-        (mst_dn, part.at[1, :, 0:dn_cols]), (mo1_dn, part.at[1, :, dn_cols:2 * dn_cols]),
-        (mo2_dn, part.at[1, :, 2 * dn_cols:3 * dn_cols])])]
+        *zip((mst_up, mo1_up, mo2_up), up_state), *zip((mst_dn, mo1_dn, mo2_dn), dn_state)])]
     for copy in loads[:6]:
         copy.start()
 
@@ -501,20 +503,18 @@
         for copy in up_peer + dn_peer:
             copy.wait_recv()
 
-    state = adamw_update(part[0, 0:up_rows], part[0, up_rows:2 * up_rows], part[0, 2 * up_rows:3 * up_rows], clip * last_up[...], rate)
+    state = adamw_update(*[ref[...] for ref in up_state], clip * last_up[...], rate)
     wts[core, 0, rows_of(chip)] = state[0].astype(jnp.bfloat16)
-    for index in range(3):
-        part[0, index * up_rows:(index + 1) * up_rows] = state[index]
+    for ref, value in zip(up_state, state):
+        ref[...] = value
     pl.when(core == 0)(gather_up)
-    state = adamw_update(part[1, :, 0:dn_cols], part[1, :, dn_cols:2 * dn_cols], part[1, :, 2 * dn_cols:3 * dn_cols], clip * last_dn[...], rate)
+    state = adamw_update(*[ref[...] for ref in dn_state], clip * last_dn[...], rate)
     wts[core, 1, :, cols_of(chip, dn_cols)] = state[0].astype(jnp.bfloat16)
-    for index in range(3):
-        part[1, :, index * dn_cols:(index + 1) * dn_cols] = state[index]
+    for ref, value in zip(dn_state, state):
+        ref[...] = value
     pl.when(core == 0)(gather_dn)
     stores = [pltpu.make_async_copy(src, dst, store_sem.at[index]) for index, (src, dst) in enumerate([
-        (part.at[0, 0:up_rows], new_up), (part.at[0, up_rows:2 * up_rows], out1_up), (part.at[0, 2 * up_rows:3 * up_rows], out2_up),
-        (part.at[1, :, 0:dn_cols], new_dn), (part.at[1, :, dn_cols:2 * dn_cols], out1_dn),
-        (part.at[1, :, 2 * dn_cols:3 * dn_cols], out2_dn)])]
+        *zip(up_state, (new_up, out1_up, out2_up)), *zip(dn_state, (new_dn, out1_dn, out2_dn))])]
     for copy in stores:
         copy.start()
 
@@ -554,26 +554,27 @@
     turned[...] = wts[0, 0].T
     start_all(weights_out(0))
 
-    def first_block(tile, carry):
-        for number, action in ((4, gather_relay), (5, gather_near), (7, gather_far)):
-            pl.when(jnp.logical_and(core == 1, tile == number))(action)
-        x_load(tile).wait()
-        mid = tile_forward(x_slot(tile)[...], turned, wts.at[0, 1], hidden_ref, FF_TILE)
-        sums[mid_slot(tile)] = mid.astype(jnp.float32)
-        pl.when(tile + n_slot < n_first)(lambda: x_load(tile + n_slot).start())
+    def first_block(pair, carry):
+        for number, action in ((2, gather_relay), (3, gather_near), (4, gather_far)):
+            pl.when(jnp.logical_and(core == 1, pair == number))(action)
+        tiles = (2 * pair, 2 * pair + 1)
+        wait_all([x_load(tile) for tile in tiles])
+        for half, tile in enumerate(tiles):
+            mid = tile_forward(x_slot(tile)[...], turned, wts.at[0, 1], hidden_ref.at[half], FF_TILE)
+            sums[mid_slot(tile)] = mid.astype(jnp.float32)
+        pl.when(tiles[1] + n_slot < n_first)(lambda: start_all([x_load(tile + n_slot) for tile in tiles]))
         return carry
 
-    lax.fori_loop(0, n_first, first_block, 0)
+    lax.fori_loop(0, n_first // 2, first_block, 0)
     pl.when(core == 0)(gather_peer)
     weights_out(0)[0].wait()
     turned[...] = wts[1, 0].T
     start_all(weights_out(1))
 
     def y_out(tile):
-        slot = lax.rem(tile, 2)
-        y_slot = grad.at[:, cols_of(slot, ROW_TILE)]
-        keep = pltpu.make_async_copy(y_slot, own_first.at[tile], tile_sem.at[1, slot])
-        give = pltpu.make_async_remote_copy(src_ref=y_slot, dst_ref=peer_first.at[tile], send_sem=tile_sem.at[2, slot],
+        slot = lax.rem(tile, n_slot)
+        keep = pltpu.make_async_copy(x_slot(tile), own_first.at[tile], tile_sem.at[1, slot])
+        give = pltpu.make_async_remote_copy(src_ref=x_slot(tile), dst_ref=peer_first.at[tile], send_sem=tile_sem.at[2, slot],
                                             recv_sem=recv_sem.at[51 + tile], device_id=to_peer, device_id_type=MESH_ID)
         return keep, give
 
@@ -582,16 +583,20 @@
         keep.wait()
         give.wait_send()
 
-    def second_block(tile, carry):
-        result = tile_forward(sums[mid_slot(tile)].astype(jnp.bfloat16), turned, wts.at[1, 1], hidden_ref, FF_TILE)
-        pl.when(tile >= 2)(lambda: y_wait(tile - 2))
-        grad[:, cols_of(lax.rem(tile, 2), ROW_TILE)] = result
-        start_all(y_out(tile))
+    def second_block(pair, carry):
+        tiles = (2 * pair, 2 * pair + 1)
+        for tile in tiles:
+            pl.when(pair >= 2)(functools.partial(y_wait, tile - n_slot))
+        for half, tile in enumerate(tiles):
+            place = x_slot(tile)
+            place[...] = tile_forward(sums[mid_slot(tile)].astype(jnp.bfloat16), turned, wts.at[1, 1], hidden_ref.at[half], FF_TILE)
+        for tile in tiles:
+            start_all(y_out(tile))
         return carry
 
-    lax.fori_loop(0, n_first, second_block, 0)
-    y_wait(n_first - 2)
-    y_wait(n_first - 1)
+    lax.fori_loop(0, n_first // 2, second_block, 0)
+    for tile in range(n_first - n_slot, n_first):
+        y_wait(tile)
     for tile in range(n_first):
         y_out(tile)[1].wait_recv()
 
@@ -629,7 +634,7 @@
             pltpu.VMEM((half_rows, ff_width), bf16), pltpu.VMEM((2, 2, width, ff_width), f32), pltpu.VMEM((2, width, ff_width), f32),
             pltpu.VMEM((2, up_rows, ff_width), f32), pltpu.VMEM((2, width, dn_cols), f32),
             pltpu.VMEM((up_rows, ff_width), f32), pltpu.VMEM((width, dn_cols), f32), pltpu.VMEM((2 * n_data, 8, 128), f32),
-            pltpu.VMEM((ff_width, width), bf16), pltpu.VMEM((ff_width, ROW_TILE), bf16),
+            pltpu.VMEM((ff_width, width), bf16), pltpu.VMEM((2, ff_width, ROW_TILE), bf16),
             pltpu.SemaphoreType.DMA((n_sem,)), pltpu.SemaphoreType.DMA((n_sem,)), pltpu.SemaphoreType.DMA((12,)),
             pltpu.SemaphoreType.DMA((10,)), pltpu.SemaphoreType.DMA((3, 4))],
         compiler_params=pltpu.CompilerParams(collective_id=0, has_side_effects=True, vmem_limit_bytes=VMEM_LIMIT),

time: 292 us -> 290 us (level)
  no operation moved by 1% of the time
where the time goes in v7:
time: 290 us; the launch traced here: 289 us
  Pallas kernels  286 us (99%)
    pallas_call x1, Pallas kernels, update_weights(): pl.pallas_call(body, in_specs=[any_spec] * 13 + [smem_spec] * 2, out_spec...  166 us
    pallas_call x3, Pallas kernels, forward_chunk(): pl.pallas_call(body, grid_spec=pltpu.PrefetchScalarGridSpec(num_scalar_pr...  115 us
  transfers between devices with their start and end apart: 3, of which 1 were waited for; matrix products, arithmetic and copies ran while one was open for 0% of the time, Pallas kernels for 18%

profile of v7, /device:TPU:0, one launch (start us, length us, event | category | flops | bytes accessed | tf_op | source)
XLA Modules:
  0.0 289.4 jit_solution(16792639151836395228)
XLA Ops:
  1.9 165.9 %update.1 = (f32[144,1536]{1,0:T(8,128)}, f32[576,384]{1,0:T(8,128)}, f32[144,1536]{1,0:T(8,128)}, f32[144,1536]{1,0:T(8,128)}, f32[576,384]{1,0:T(8,128)}, /*in...) custom-call(f32[144,1536]{1,0:T(8,128)} %bitcast.54, ...), custom_call_target="tpu_custom_call" | custom-call | flops 61605937152 | bytes 60000000 | tf_op jit(solution)/shard_map/update/pallas_call | solution.py:625
  167.8 65.0 %fwd_12.1 = (bf16[16,576,2048]{2,1,0:T(8,128)(2,1)}, bf16[12,576,512]{2,1,0:T(8,128)(2,1)}, f32[144,1536]{1,0:T(8,128)}, f32[576,384]{1,0:T(8,128)}, f32[144,153...) custom-call(s32[1]{0:T(128)} %bitcast.first, bf16[16,576,2048]{2,1,0:T(8,128)(2,1)} %bitcast.45, ...), custom_call_target="tpu_custom_call" | custom-call | flops 43486543872 | bytes 3538944 | tf_op jit(solution)/shard_map/fwd_12/pallas_call | solution.py:169
  232.8 0.2 collective-permute-start
  233.0 29.5 %fwd_24.1 = (bf16[16,576,2048]{2,1,0:T(8,128)(2,1)}, bf16[5,576,512]{2,1,0:T(8,128)(2,1)}) custom-call(s32[1]{0:T(128)} %bitcast.first, bf16[16,576,2048]{2,1,0:T(8,128)(2,1)} %bitcast.46, bf16[2,1536,576]{2,1,0:T(8,128)(2,1)} %get-tuple-element.29.refs_1_, bf16[2,576,1536]{2,1,0:T(8,128)(2,1)} %get-tuple-element.30.refs_2_, ...), custom_call_target="tpu_custom_call", output_to_operand_aliasing={{0}: (4, {})} | custom-call | flops 18119393280 | bytes 1474560 | tf_op jit(solution)/shard_map/fwd_24/pallas_call | solution.py:169
  262.6 0.3 collective-permute-start.2
  262.9 0.0 collective-permute-done.refs_3_
  262.9 20.3 %fwd_29.1 = (bf16[16,576,2048]{2,1,0:T(8,128)(2,1)}, bf16[3,576,512]{2,1,0:T(8,128)(2,1)}) custom-call(s32[1]{0:T(128)} %bitcast.first, bf16[16,576,2048]{2,1,0:T(8,128)(2,1)} %bitcast.47, bf16[2,1536,576]{2,1,0:T(8,128)(2,1)} %get-tuple-element.29.refs_1_, bf16[2,576,1536]{2,1,0:T(8,128)(2,1)} %get-tuple-element.30.refs_2_, ...), custom_call_target="tpu_custom_call", output_to_operand_aliasing={{0}: (5, {})} | custom-call | flops 10871635968 | bytes 884736 | tf_op jit(solution)/shard_map/fwd_29/pallas_call | solution.py:169
  283.2 0.2 collective-permute-start.1
  283.5 0.0 collective-permute-done.2.tiles_ref
  283.5 2.7 place_24.1.old_ref
  286.2 0.7 collective-permute-done.1.tiles_ref
  286.9 2.3 place_29.1
Async XLA Ops:
  232.8 30.1 %collective-permute-start = (bf16[12,576,512]{2,1,0:T(8,128)(2,1)}, bf16[12,576,512]{2,1,0:T(8,128)(2,1)}, u32[]{:S(2)}, u32[]{:S(2)}) collective-permute-start(bf16[12,576,512]{2,1,0:T(8,128)(2,1)} %get-tuple-element.45), channel_id=1, source_target_pairs={{0,1},{1,0},{2,3},{3,2},{4,5},{5,4},{6,7},{7,6}} | collective-permute-start | bytes 21233672 | tf_op jit(solution)/shard_map/ppermute | solution.py:223
  262.6 20.9 %collective-permute-start.2 = (bf16[5,576,512]{2,1,0:T(8,128)(2,1)}, bf16[5,576,512]{2,1,0:T(8,128)(2,1)}, u32[]{:S(2)}, u32[]{:S(2)}) collective-permute-start(bf16[5,576,512]{2,1,0:T(8,128)(2,1)} %get-tuple-element.49), channel_id=1, source_target_pairs={{0,1},{1,0},{2,3},{3,2},{4,5},{5,4},{6,7},{7,6}} | collective-permute-start | bytes 8847368 | tf_op jit(solution)/shard_map/ppermute | solution.py:223
  283.2 3.7 %collective-permute-start.1 = (bf16[3,576,512]{2,1,0:T(8,128)(2,1)}, bf16[3,576,512]{2,1,0:T(8,128)(2,1)}, u32[]{:S(2)}, u32[]{:S(2)}) collective-permute-start(bf16[3,576,512]{2,1,0:T(8,128)(2,1)} %get-tuple-element.48), channel_id=1, source_target_pairs={{0,1},{1,0},{2,3},{3,2},{4,5},{5,4},{6,7},{7,6}} | collective-permute-start | bytes 5308424 | tf_op jit(solution)/shard_map/ppermute | solution.py:223

commit v8 on v7

--- a/solution.py
+++ b/solution.py
@@ -32,8 +32,9 @@
 GELU_CUB = GELU_LIN * 0.044715
 ROW_TILE = 512
 FF_TILE = 256
-CHUNKS = ((12, 256), (5, 256), (3, 512))
-N_FIRST = 12
+CHUNKS = ((6, 256), (2, 256))
+N_MID = 12
+N_FIRST = 24
 VMEM_LIMIT = 67000000
 
 
@@ -541,7 +542,7 @@
         copy.wait_send()
 
     def weights_out(block):
-        return [pltpu.make_async_copy(turned, w_up_out.at[block], store_sem.at[6 + block]),
+        return [pltpu.make_async_copy(turned.at[block], w_up_out.at[block], store_sem.at[6 + block]),
                 pltpu.make_async_copy(wts.at[block, 1], w_dn_out.at[block], store_sem.at[8 + block])]
 
     n_first = own_first.shape[0]
@@ -551,7 +552,7 @@
         row = tile // per_row
         return row // 2, lax.rem(row, 2), slice(None), cols_of(lax.rem(tile, per_row), ROW_TILE)
 
-    turned[...] = wts[0, 0].T
+    turned[0] = wts[0, 0].T
     start_all(weights_out(0))
 
     def first_block(pair, carry):
@@ -560,15 +561,14 @@
         tiles = (2 * pair, 2 * pair + 1)
         wait_all([x_load(tile) for tile in tiles])
         for half, tile in enumerate(tiles):
-            mid = tile_forward(x_slot(tile)[...], turned, wts.at[0, 1], hidden_ref.at[half], FF_TILE)
+            mid = tile_forward(x_slot(tile)[...], turned.at[0], wts.at[0, 1], hidden_ref.at[half], FF_TILE)
             sums[mid_slot(tile)] = mid.astype(jnp.float32)
-        pl.when(tiles[1] + n_slot < n_first)(lambda: start_all([x_load(tile + n_slot) for tile in tiles]))
+        pl.when(tiles[1] + n_slot < N_MID)(lambda: start_all([x_load(tile + n_slot) for tile in tiles]))
         return carry
 
-    lax.fori_loop(0, n_first // 2, first_block, 0)
+    lax.fori_loop(0, N_MID // 2, first_block, 0)
     pl.when(core == 0)(gather_peer)
-    weights_out(0)[0].wait()
-    turned[...] = wts[1, 0].T
+    turned[1] = wts[1, 0].T
     start_all(weights_out(1))
 
     def y_out(tile):
@@ -589,12 +589,34 @@
             pl.when(pair >= 2)(functools.partial(y_wait, tile - n_slot))
         for half, tile in enumerate(tiles):
             place = x_slot(tile)
-            place[...] = tile_forward(sums[mid_slot(tile)].astype(jnp.bfloat16), turned, wts.at[1, 1], hidden_ref.at[half], FF_TILE)
+            place[...] = tile_forward(sums[mid_slot(tile)].astype(jnp.bfloat16), turned.at[1], wts.at[1, 1], hidden_ref.at[half], FF_TILE)
         for tile in tiles:
             start_all(y_out(tile))
         return carry
 
-    lax.fori_loop(0, n_first // 2, second_block, 0)
+    n_late = ff_width // ROW_TILE
+
+    def late_slot(tile):
+        return d_pre.at[0:width, cols_of(lax.rem(tile, n_late), ROW_TILE)]
+
+    def late_load(tile):
+        return pltpu.make_async_copy(micro_in.at[tile_place(n_own, per_micro, core, tile)], late_slot(tile), tile_sem.at[3, lax.rem(tile, n_late)])
+
+    def whole_tile(tile, carry):
+        y_wait(tile - n_slot)
+        late_load(tile).wait()
+        cols = late_slot(tile)[...]
+        for block in range(2):
+            cols = tile_forward(cols, turned.at[block], wts.at[block, 1], hidden_ref.at[block], FF_TILE)
+        place = x_slot(tile)
+        place[...] = cols
+        start_all(y_out(tile))
+        pl.when(tile + n_late < n_first)(lambda: late_load(tile + n_late).start())
+        return carry
+
+    start_all([late_load(N_MID + tile) for tile in range(n_late)])
+    lax.fori_loop(0, N_MID // 2, second_block, 0)
+    lax.fori_loop(N_MID, n_first, whole_tile, 0)
     for tile in range(n_first - n_slot, n_first):
         y_wait(tile)
     for tile in range(n_first):
@@ -602,7 +624,7 @@
 
     for copy in [up_x, up_y, up_relay, dn_x, dn_y, dn_relay] + up_peer + dn_peer:
         copy.wait_send()
-    for copy in stores + weights_out(0)[1:] + weights_out(1):
+    for copy in stores + weights_out(0) + weights_out(1):
         copy.wait()
 
 
@@ -634,9 +656,9 @@
             pltpu.VMEM((half_rows, ff_width), bf16), pltpu.VMEM((2, 2, width, ff_width), f32), pltpu.VMEM((2, width, ff_width), f32),
             pltpu.VMEM((2, up_rows, ff_width), f32), pltpu.VMEM((2, width, dn_cols), f32),
             pltpu.VMEM((up_rows, ff_width), f32), pltpu.VMEM((width, dn_cols), f32), pltpu.VMEM((2 * n_data, 8, 128), f32),
-            pltpu.VMEM((ff_width, width), bf16), pltpu.VMEM((2, ff_width, ROW_TILE), bf16),
+            pltpu.VMEM((2, ff_width, width), bf16), pltpu.VMEM((2, ff_width, ROW_TILE), bf16),
             pltpu.SemaphoreType.DMA((n_sem,)), pltpu.SemaphoreType.DMA((n_sem,)), pltpu.SemaphoreType.DMA((12,)),
-            pltpu.SemaphoreType.DMA((10,)), pltpu.SemaphoreType.DMA((3, 4))],
+            pltpu.SemaphoreType.DMA((10,)), pltpu.SemaphoreType.DMA((4, 4))],
         compiler_params=pltpu.CompilerParams(collective_id=0, has_side_effects=True, vmem_limit_bytes=VMEM_LIMIT),
         cost_estimate=pl.CostEstimate(flops=flops, bytes_accessed=60000000, transcendentals=0),
         name="update",

time: 290 us -> 287 us (0.990)
    pallas_call x3 -> x2, Pallas kernels: 115 us -> 57.3 us  [forward_chunk(): pl.pallas_call(body, grid_spec=pltpu.PrefetchScalarGridSpec(num_scalar_pr...]
    pallas_call x1, Pallas kernels: 166 us -> 222 us  [update_weights(): pl.pallas_call(body, in_specs=[any_spec] * 13 + [smem_spec] * 2, out_spec...]
  transfers between devices with their start and end apart: 3 -> 2, of which waited for: 1 -> 0; matrix products, arithmetic and copies ran while one was open for 0% -> 0% of each run, Pallas kernels for 18% -> 6%
where the time goes in v8:
time: 287 us
  Pallas kernels  284 us (99%)
    pallas_call x1, Pallas kernels, update_weights(): pl.pallas_call(body, in_specs=[any_spec] * 13 + [smem_spec] * 2, out_spec...  222 us
    pallas_call x2, Pallas kernels, forward_chunk(): pl.pallas_call(body, grid_spec=pltpu.PrefetchScalarGridSpec(num_scalar_pr...  57.3 us
  transfers between devices with their start and end apart: 2, of which 0 were waited for; matrix products, arithmetic and copies ran while one was open for 0% of the time, Pallas kernels for 6%

profile of v8, /device:TPU:0, one launch (start us, length us, event | category | flops | bytes accessed | tf_op | source)
XLA Modules:
  0.0 286.6 jit_solution(565388224267143460)
XLA Ops:
  1.9 221.5 %update.1 = (f32[144,1536]{1,0:T(8,128)}, f32[576,384]{1,0:T(8,128)}, f32[144,1536]{1,0:T(8,128)}, f32[144,1536]{1,0:T(8,128)}, f32[576,384]{1,0:T(8,128)}, /*in...) custom-call(f32[144,1536]{1,0:T(8,128)} %bitcast.53, ...), custom_call_target="tpu_custom_call" | custom-call | flops 105092481024 | bytes 60000000 | tf_op jit(solution)/shard_map/update/pallas_call | solution.py:647
  223.5 41.9 %fwd_24.1 = (bf16[16,576,2048]{2,1,0:T(8,128)(2,1)}, bf16[6,576,512]{2,1,0:T(8,128)(2,1)}, f32[144,1536]{1,0:T(8,128)}, f32[576,384]{1,0:T(8,128)}, f32[144,1536...) custom-call(s32[1]{0:T(128)} %bitcast.first, bf16[16,576,2048]{2,1,0:T(8,128)(2,1)} %bitcast.45, ...), custom_call_target="tpu_custom_call" | custom-call | flops 21743271936 | bytes 1769472 | tf_op jit(solution)/shard_map/fwd_24/pallas_call | solution.py:170
  265.3 0.2 collective-permute-start.1
  265.6 15.4 %fwd_30.1 = (bf16[16,576,2048]{2,1,0:T(8,128)(2,1)}, bf16[2,576,512]{2,1,0:T(8,128)(2,1)}) custom-call(s32[1]{0:T(128)} %bitcast.first, bf16[16,576,2048]{2,1,0:T(8,128)(2,1)} %bitcast.46, bf16[2,1536,576]{2,1,0:T(8,128)(2,1)} %get-tuple-element.27.refs_1_, bf16[2,576,1536]{2,1,0:T(8,128)(2,1)} %get-tuple-element.28.refs_2_, ...), custom_call_target="tpu_custom_call", output_to_operand_aliasing={{0}: (4, {})} | custom-call | flops 7247757312 | bytes 589824 | tf_op jit(solution)/shard_map/fwd_30/pallas_call | solution.py:170
  281.0 0.3 collective-permute-start
  281.3 0.0 collective-permute-done.1.tiles_ref
  281.3 3.0 %place_24.1.old_ref = bf16[16,576,2048]{2,1,0:T(8,128)(2,1)} custom-call(bf16[6,576,512]{2,1,0:T(8,128)(2,1)} %collective-permute-done.1.tiles_ref, bf16[16,576,2048]{2,1,0:T(8,128)(2,1)} %get-tuple-element.46.old_ref), custom_call_target="tpu_custom_call", output_to_operand_aliasing={{}: (1, {})} | custom-call | tf_op jit(solution)/shard_map/place_24/pallas_call | solution.py:206
  284.3 0.0 collective-permute-done.tiles_ref
  284.3 2.1 place_30.1
Async XLA Ops:
  265.3 16.0 %collective-permute-start.1 = (bf16[6,576,512]{2,1,0:T(8,128)(2,1)}, bf16[6,576,512]{2,1,0:T(8,128)(2,1)}, u32[]{:S(2)}, u32[]{:S(2)}) collective-permute-start(bf16[6,576,512]{2,1,0:T(8,128)(2,1)} %get-tuple-element.45), channel_id=1, source_target_pairs={{0,1},{1,0},{2,3},{3,2},{4,5},{5,4},{6,7},{7,6}} | collective-permute-start | bytes 10616840 | tf_op jit(solution)/shard_map/ppermute | solution.py:224
  281.0 3.3 %collective-permute-start = (bf16[2,576,512]{2,1,0:T(8,128)(2,1)}, bf16[2,576,512]{2,1,0:T(8,128)(2,1)}, u32[]{:S(2)}, u32[]{:S(2)}) collective-permute-start(bf16[2,576,512]{2,1,0:T(8,128)(2,1)} %get-tuple-element.44), channel_id=1, source_target_pairs={{0,1},{1,0},{2,3},{3,2},{4,5},{5,4},{6,7},{7,6}} | collective-permute-start | bytes 3538952 | tf_op jit(solution)/shard_map/ppermute | solution.py:224

commit v9 on v8

--- a/solution.py
+++ b/solution.py
@@ -32,9 +32,9 @@
 GELU_CUB = GELU_LIN * 0.044715
 ROW_TILE = 512
 FF_TILE = 256
-CHUNKS = ((6, 256), (2, 256))
+CHUNKS = ((10, 256), (2, 256))
 N_MID = 12
-N_FIRST = 24
+N_FIRST = 20
 VMEM_LIMIT = 67000000
 
 

time: 287 us -> 285 us (level)
    pallas_call x1, Pallas kernels: 222 us -> 203 us  [update_weights(): pl.pallas_call(body, in_specs=[any_spec] * 13 + [smem_spec] * 2, out_spec...]
    pallas_call x2, Pallas kernels: 57.3 us -> 72.3 us  [forward_chunk(): pl.pallas_call(body, grid_spec=pltpu.PrefetchScalarGridSpec(num_scalar_pr...]
  transfers between devices with their start and end apart: 2 -> 2, of which waited for: 0 -> 0; matrix products, arithmetic and copies ran while one was open for 0% -> 0% of each run, Pallas kernels for 6% -> 7%
where the time goes in v9:
time: 285 us
  Pallas kernels  282 us (99%)
    pallas_call x1, Pallas kernels, update_weights(): pl.pallas_call(body, in_specs=[any_spec] * 13 + [smem_spec] * 2, out_spec...  203 us
    pallas_call x2, Pallas kernels, forward_chunk(): pl.pallas_call(body, grid_spec=pltpu.PrefetchScalarGridSpec(num_scalar_pr...  72.3 us
    pallas_call x2, Pallas kernels, place_tiles(): pl.pallas_call(body, in_specs=[any_spec] * 2, out_specs=any_spec, out_sha...  7.44 us
  transfers between devices with their start and end apart: 2, of which 0 were waited for; matrix products, arithmetic and copies ran while one was open for 0% of the time, Pallas kernels for 7%

profile of v9, /device:TPU:0, one launch (start us, length us, event | category | flops | bytes accessed | tf_op | source)
XLA Modules:
  0.0 285.2 jit_solution(10706719802231228374)
XLA Ops:
  1.9 202.7 %update.1 = (f32[144,1536]{1,0:T(8,128)}, f32[576,384]{1,0:T(8,128)}, f32[144,1536]{1,0:T(8,128)}, f32[144,1536]{1,0:T(8,128)}, f32[576,384]{1,0:T(8,128)}, /*in...) custom-call(f32[144,1536]{1,0:T(8,128)} %bitcast.53, ...), custom_call_target="tpu_custom_call" | custom-call | flops 90596966400 | bytes 60000000 | tf_op jit(solution)/shard_map/update/pallas_call | solution.py:647
  204.6 56.9 %fwd_20.1 = (bf16[16,576,2048]{2,1,0:T(8,128)(2,1)}, bf16[10,576,512]{2,1,0:T(8,128)(2,1)}, f32[144,1536]{1,0:T(8,128)}, f32[576,384]{1,0:T(8,128)}, f32[144,153...) custom-call(s32[1]{0:T(128)} %bitcast.first, bf16[16,576,2048]{2,1,0:T(8,128)(2,1)} %bitcast.45, ...), custom_call_target="tpu_custom_call" | custom-call | flops 36238786560 | bytes 2949120 | tf_op jit(solution)/shard_map/fwd_20/pallas_call | solution.py:170
  261.5 0.2 collective-permute-start.1
  261.8 15.4 %fwd_30.1 = (bf16[16,576,2048]{2,1,0:T(8,128)(2,1)}, bf16[2,576,512]{2,1,0:T(8,128)(2,1)}) custom-call(s32[1]{0:T(128)} %bitcast.first, bf16[16,576,2048]{2,1,0:T(8,128)(2,1)} %bitcast.46, bf16[2,1536,576]{2,1,0:T(8,128)(2,1)} %get-tuple-element.27.refs_1_, bf16[2,576,1536]{2,1,0:T(8,128)(2,1)} %get-tuple-element.28.refs_2_, ...), custom_call_target="tpu_custom_call", output_to_operand_aliasing={{0}: (4, {})} | custom-call | flops 7247757312 | bytes 589824 | tf_op jit(solution)/shard_map/fwd_30/pallas_call | solution.py:170
  277.2 0.3 collective-permute-start
  277.5 0.0 collective-permute-done.1.tiles_ref
  277.5 5.3 %place_20.1.old_ref = bf16[16,576,2048]{2,1,0:T(8,128)(2,1)} custom-call(bf16[10,576,512]{2,1,0:T(8,128)(2,1)} %collective-permute-done.1.tiles_ref, bf16[16,576,2048]{2,1,0:T(8,128)(2,1)} %get-tuple-element.46.old_ref), custom_call_target="tpu_custom_call", output_to_operand_aliasing={{}: (1, {})} | custom-call | tf_op jit(solution)/shard_map/place_20/pallas_call | solution.py:206
  282.9 0.0 collective-permute-done.tiles_ref
  282.9 2.1 place_30.1
Async XLA Ops:
  261.5 16.0 %collective-permute-start.1 = (bf16[10,576,512]{2,1,0:T(8,128)(2,1)}, bf16[10,576,512]{2,1,0:T(8,128)(2,1)}, u32[]{:S(2)}, u32[]{:S(2)}) collective-permute-start(bf16[10,576,512]{2,1,0:T(8,128)(2,1)} %get-tuple-element.45), channel_id=1, source_target_pairs={{0,1},{1,0},{2,3},{3,2},{4,5},{5,4},{6,7},{7,6}} | collective-permute-start | bytes 17694728 | tf_op jit(solution)/shard_map/ppermute | solution.py:224
  277.2 5.7 %collective-permute-start = (bf16[2,576,512]{2,1,0:T(8,128)(2,1)}, bf16[2,576,512]{2,1,0:T(8,128)(2,1)}, u32[]{:S(2)}, u32[]{:S(2)}) collective-permute-start(bf16[2,576,512]{2,1,0:T(8,128)(2,1)} %get-tuple-element.44), channel_id=1, source_target_pairs={{0,1},{1,0},{2,3},{3,2},{4,5},{5,4},{6,7},{7,6}} | collective-permute-start | bytes 3538952 | tf_op jit(solution)/shard_map/ppermute | solution.py:224
